TPU v7x, 512 devices: a 8x2x16 block of a 8x8x16 slice. The times are simulated.
512 devices in a mesh: parts: 2 (over y), mem: 16 (over z), space: 16 (over x, core).
Axes of the slice: x: 8, y: 2, z: 16, core: 2. Of those that a mesh axis runs over, the one named last changes fastest.
The devices are a block of a 8x8x16 slice.
Arguments:
- ensemble: bfloat16 [64, 70, 32768], P('mem', None, ('parts', 'space')), parts along dimension 2, may hold values from -6 to 6
- transform: bfloat16 [128, 64], P('parts'), parts along dimension 0, may hold values from -0.75 to 0.75
- obs_operator: bfloat16 [16, 70], replicated, may hold values from -0.75 to 0.75
- obs_weight: float32 [16, 32768], P(None, ('parts', 'space')), parts along dimension 1, may hold values from 0.25 to 40, as said below
Outputs:
- analysis: bfloat16 [64, 70, 32768], P('mem', None, ('parts', 'space')), parts along dimension 2
- prior_gram: float32 [128, 64], P('parts'), parts along dimension 0
- posterior_gram: float32 [128, 64], P('parts'), parts along dimension 0
There are 2 independent parts, one for each index of `parts`. A program takes and returns all parts, laid end to end along the dimension named above; an argument that names none is the same for every part. Nothing has to cross between parts.
Inputs may be any that keep to these rules, and one draw needn't show every extreme that they name: `obs_weight`: positive.
All inputs are finite; a program needn't handle non-finite values.
Results may differ from a plain program's by a relative error of at most 0.001.
Values may be sent and summed in bfloat16 or wider, within the bound.
No kernel may reach another device: no remote copies, remote signals or barrier semaphores. Data moves between devices by JAX's collectives and lax.ppermute only.
A program may use at most 64 MiB of HBM per device.

v0:
```python
import jax
import jax.numpy as jnp
from jax import lax
from jax.sharding import Mesh
from jax.sharding import PartitionSpec as P

MEMBERS = 64
MEM_SPACE = ("mem", "space_0", "space_1")
PARTS_SPACE = ("parts", "space_0", "space_1")


HIGHEST = lax.Precision.HIGHEST


def over_axes(array, axes):
    for axis in axes:
        array = lax.psum(array, axis)
    return array


def gram_terms(observed, weights):
    departures = observed - jnp.sum(observed, axis=0) / MEMBERS
    weighted = departures * weights[None, :, :]
    partial_gram = jnp.einsum("ioc,joc->ij", weighted, departures, precision=HIGHEST)
    return (partial_gram, jnp.sum(weights))


def per_device(ensemble, transform, obs_operator, obs_weight):
    local_members = ensemble.shape[0]
    mixing = transform.astype(jnp.float32)
    own_start = lax.axis_index("mem") * local_members
    own_columns = lax.dynamic_slice_in_dim(transform, own_start, local_members, 1)
    keep_mean = 1.0 - jnp.sum(own_columns.astype(jnp.float32), axis=0)
    members_block = lax.all_gather(ensemble, "mem", axis=0, tiled=True)
    combined = jnp.einsum(
        "kj,kvc->jvc", own_columns, members_block, preferred_element_type=jnp.float32
    )
    totals = jnp.sum(members_block, axis=0, dtype=jnp.float32)
    results = (totals, combined)
    totals = results[0]
    combined = results[1]
    member_mean = totals / MEMBERS
    analysis = (combined + member_mean[None, :, :] * keep_mean[:, None, None]).astype(jnp.bfloat16)
    observed = jnp.einsum("ov,mvc->moc", obs_operator, ensemble, preferred_element_type=jnp.float32)
    by_columns = lax.all_to_all(
        observed.astype(jnp.bfloat16), "mem", split_axis=2, concat_axis=0, tiled=True
    ).astype(observed.dtype)
    cells_here = by_columns.shape[2]
    own_weights = lax.dynamic_slice_in_dim(
        obs_weight, lax.axis_index("mem") * cells_here, cells_here, 1
    )
    partial_gram, weight_sum = gram_terms(by_columns, own_weights)
    gram_sum, weight_total = (over_axes(partial_gram, MEM_SPACE), over_axes(weight_sum, MEM_SPACE))
    prior_gram = gram_sum / weight_total
    carried = jnp.dot(mixing.T, prior_gram, precision=HIGHEST)
    posterior_gram = jnp.dot(carried, mixing, precision=HIGHEST)
    return (analysis, prior_gram, posterior_gram)


def solution(mesh):
    finer = Mesh(
        mesh.devices.reshape(mesh.shape["parts"], mesh.shape["mem"], 8, 2),
        ("parts", "mem", "space_0", "space_1"),
    )
    in_specs = (P("mem", None, PARTS_SPACE), P("parts", None), P(), P(None, PARTS_SPACE))
    out_specs = (P("mem", None, PARTS_SPACE), P("parts", None), P("parts", None))
    return jax.shard_map(
        per_device, mesh=finer, in_specs=in_specs, out_specs=out_specs, check_vma=False
    )
```

profile of v0, /device:TPU:80, one launch (start us, length us, event | category | flops | bytes accessed | tf_op | source)
XLA Modules:
  0.0 199.5 jit_solution(854474547940677901)
XLA Ops:
  7.3 2.0 %copy.30 = bf16[4,70,1024]{2,1,0:T(8,128)(2,1)} copy(bf16[4,70,1024]{2,0,1:T(4,128)(2,1)} %param.4) | data formatting | bytes 1146880 | tf_op args[0]
  9.4 1.3 fusion.8
  10.7 0.7 copy.33
  11.4 1.8 reshape.27
  13.2 43.7 %all-to-all-start = ((bf16[16,2,2048]{2,1,0:T(2,128)(2,1)}), bf16[16,2,2048]{2,1,0:T(2,128)(2,1)S(1)}, u32[]{:S(2)}, u32[]{:S(2)}) async-start(bf16[16,2,2048]{2,1,0:T(2,128)(2,1)} %reshape.27), calls=%async_computation | async-start | bytes 262144 | tf_op jit(solution)/shard_map/all_to_all | solution.py:45
  56.9 0.1 constant_dynamic-slice_fusion.1
  56.9 0.1 copy.36
  57.0 0.1 convert_reduce_fusion.2
  57.2 14.3 %all-to-all-done = bf16[16,2,2048]{2,1,0:T(2,128)(2,1)S(1)} async-done(((bf16[16,2,2048]{2,1,0:T(2,128)(2,1)}), bf16[16,2,2048]{2,1,0:T(2,128)(2,1)S(1)}, u32[]{:S(2)}, u32[]{:S(2)}) %all-to-all-start) | async-done | bytes 131104 | tf_op jit(solution)/shard_map/all_to_all | solution.py:45
  71.5 0.7 reshape.28
  72.2 0.2 bitcast_convert_fusion
  72.4 1.6 copy.34
  74.0 1.5 convert_reduce_fusion.1
  75.6 1.4 fusion.16
  77.0 0.6 convolution_bitcast_fusion
  77.6 57.2 %all-reduce = (f32[64,64]{1,0:T(8,128)S(1)}, f32[]{:T(128)}) all-reduce(f32[64,64]{1,0:T(8,128)S(1)} %convolution_bitcast_fusion, f32[]{:T(128)} %get-tuple-element.9), channel_id=1, replica_groups=mesh['parts'=2,'mem'=16,'space_0'=8,'space_1'=2] {'mem'}, use_global_device_ids=true, to_apply=%region_4.0 | all-reduce | flops 4097 | bytes 32776 | tf_op jit(solution)/shard_map/psum | solution.py:17
  134.8 34.6 %all-reduce.1 = (f32[64,64]{1,0:T(8,128)S(1)}, f32[]{:T(128)}) all-reduce(f32[64,64]{1,0:T(8,128)S(1)} %get-tuple-element.3, f32[]{:T(128)} %get-tuple-element.4), channel_id=1, replica_groups=mesh['parts'=2,'mem'=16,'space_0'=8,'space_1'=2] {'space_0'}, use_global_device_ids=true, to_apply=%region_5.0 | all-reduce | flops 4097 | bytes 32776 | tf_op jit(solution)/shard_map/psum | solution.py:17
  169.4 4.6 %all-reduce.2 = (f32[64,64]{1,0:T(8,128)S(1)}, f32[]{:T(128)}) all-reduce(f32[64,64]{1,0:T(8,128)S(1)} %get-tuple-element.5, f32[]{:T(128)} %get-tuple-element.6), channel_id=1, replica_groups=mesh['parts'=2,'mem'=16,'space_0'=8,'space_1'=2] {'space_1'}, use_global_device_ids=true, to_apply=%region_6.0 | all-reduce | flops 4097 | bytes 32776 | tf_op jit(solution)/shard_map/psum | solution.py:17
  174.0 0.7 broadcast_divide_fusion
  174.6 0.2 fusion.17
  174.9 0.8 fusion.18
  175.7 6.2 %convert_reduce_fusion = f32[70,1024]{1,0:T(8,128)S(1)} fusion(bf16[64,70,1024]{2,1,0:T(8,128)(2,1)} %all-gather.2.cloned.1.call-done), kind=kLoop, calls=%fused_computation | loop fusion | flops 9103360 | bytes 9461760 | tf_op jit(solution)/shard_map/reduce_sum | solution.py:38
  182.0 0.1 copy-done.1
  182.1 10.6 %fusion.5 = bf16[4,70,1024]{2,0,1:T(4,128)(2,1)} fusion(bf16[64,70,1024]{2,1,0:T(8,128)(2,1)S(1)} %copy-done.1, f32[4]{0:T(128)S(1)} %broadcast_subtract_fusion, f32[70,1024]{1,0:T(8,128)S(1)} %broadcast_multiply_fusion, bf16[64,4]{1,0:T(8,128)(2,1)S(1)} %constant_dynamic-slice_fusion.1), kind=kOutput, calls=%fused_computation.4 | convolution fusion | flops 37560320 | bytes 10035728 | tf_op jit(solution)/shard_map/kj,kvc->jvc/dot_general | solution.py:35
  (14 shorter events, 0.3 us)
Async XLA Ops:
  7.2 49.7 %copy-start = (bf16[64,64]{1,0:T(8,128)(2,1)S(1)}, bf16[64,64]{1,0:T(8,128)(2,1)}, u32[]{:S(2)}) copy-start(bf16[64,64]{1,0:T(8,128)(2,1)} %param.5) | copy-start | bytes 24580
  7.2 168.5 %all-gather.2.cloned.1.call-start = ((), (), s32[]{:S(2)}) async-start(), calls=%async_computation.1 | async-start | bytes 10027008 | tf_op jit(solution)/shard_map/all_gather | solution.py:34
  13.2 58.3 %all-to-all-start = ((bf16[16,2,2048]{2,1,0:T(2,128)(2,1)}), bf16[16,2,2048]{2,1,0:T(2,128)(2,1)S(1)}, u32[]{:S(2)}, u32[]{:S(2)}) async-start(bf16[16,2,2048]{2,1,0:T(2,128)(2,1)} %reshape.27), calls=%async_computation | async-start | bytes 262144 | tf_op jit(solution)/shard_map/all_to_all | solution.py:45
  74.0 3.0 %copy-start.2 = (f32[16,4,16,64]{3,1,0,2:T(4,128)S(1)}, f32[16,4,16,64]{3,1,0,2:T(4,128)}, u32[]{:S(2)}) copy-start(f32[16,4,16,64]{3,1,0,2:T(4,128)} %copy.34) | copy-start | bytes 786436
  174.6 7.3 %copy-start.3 = (f32[64,64]{1,0:T(8,128)}, f32[64,64]{1,0:T(8,128)S(1)}, u32[]{:S(2)}) copy-start(f32[64,64]{1,0:T(8,128)S(1)} %broadcast_divide_fusion) | copy-start | bytes 49156
  175.7 6.4 %copy-start.1 = (bf16[64,70,1024]{2,1,0:T(8,128)(2,1)S(1)}, bf16[64,70,1024]{2,1,0:T(8,128)(2,1)}, u32[]{:S(2)}) copy-start(bf16[64,70,1024]{2,1,0:T(8,128)(2,1)} %all-gather.2.cloned.1.call-done) | copy-start | bytes 27525124
Sparse Core Ops, SparseCore 0:
  10.1 154.0 all-gather.1
where the time goes:
time: 200 us
  blocking collectives  96.4 us (48%)
  starting transfers between devices  43.7 us (22%)
  waiting for transfers between devices  14.4 us (7%)
  between operations  14.2 us (7%)
  matrix products  13.6 us (7%)
  other arithmetic  10.2 us (5%)
  local copies, waits for them, and re-layouts  7.1 us (4%)
    psum x3, blocking collectives, over_axes(): array = lax.psum(array, axis)  96.4 us
    all_to_all x1, starting transfers between devices, per_device(): lax.all_to_all(observed.astype(jnp.bfloat16), 'mem', split_axis=2, concat...  43.7 us
    all_to_all x1, waiting for transfers between devices, per_device(): lax.all_to_all(observed.astype(jnp.bfloat16), 'mem', split_axis=2, concat...  14.3 us
    dot_general x1, matrix products, per_device(): jnp.einsum('kj,kvc->jvc', own_columns, members_block, preferred_element_t...  10.6 us
    reduce_sum x1, other arithmetic, per_device(): totals = jnp.sum(members_block, axis=0, dtype=jnp.float32)  6.24 us
    unnamed x12, local copies, waits for them, and re-layouts  4.68 us
  transfers between devices with their start and end apart: 2, of which 1 were waited for; matrix products, arithmetic and copies ran while one was open for 6% of the time, Pallas kernels for 0%

commit v1 on v0

v1 whole, which is shorter than its diff:
```python
import jax
import jax.numpy as jnp
from jax import lax
from jax.sharding import PartitionSpec as P

MEMBERS = 64
LANES = 128
HIGHEST = lax.Precision.HIGHEST


def exchange(array, axis):
    return lax.all_to_all(array, axis, split_axis=0, concat_axis=0, tiled=True)


def to_all(array, axis, size):
    return exchange(jnp.broadcast_to(array[None], (size, *array.shape)), axis)


def per_device(mem, space, ensemble, transform, obs_operator, obs_weight):
    local, variables, cells = ensemble.shape
    quantities = obs_operator.shape[0]
    mixing = transform.astype(jnp.float32)
    tiles = cells // LANES
    halves = mem // tiles
    depth = variables // halves

    observed = jnp.einsum("ov,mvc->omc", obs_operator, ensemble, preferred_element_type=jnp.float32)
    by_quantity = exchange(observed.astype(jnp.bfloat16), "mem")

    blocks = ensemble.reshape(local, halves, depth, tiles, LANES)
    blocks = blocks.transpose(1, 3, 2, 0, 4).reshape(mem, depth, local, LANES)
    members = exchange(blocks, "mem")

    own = by_quantity.reshape(MEMBERS, cells).astype(jnp.float32)
    own_weights = lax.dynamic_slice_in_dim(obs_weight, lax.axis_index("mem"), 1, 0)
    departures = own - jnp.sum(own, axis=0, keepdims=True) / MEMBERS
    partial = lax.dot_general(
        departures * own_weights, departures, (((1,), (1,)), ((), ())), precision=HIGHEST
    )
    weight_sum = jnp.sum(own_weights)
    packed = jnp.concatenate([partial, jnp.broadcast_to(weight_sum, partial.shape)], axis=1)
    rows = MEMBERS // space
    packed = jnp.sum(exchange(packed.reshape(space, rows, LANES), "space"), axis=0)
    packed = jnp.sum(to_all(packed, "mem", mem), axis=0)
    packed = to_all(packed, "space", space).reshape(MEMBERS, LANES)
    prior_gram = packed[:, :MEMBERS] / packed[:, MEMBERS:]
    carried = jnp.dot(mixing.T, prior_gram, precision=HIGHEST)
    posterior_gram = jnp.dot(carried, mixing, precision=HIGHEST)

    members = members.transpose(1, 0, 2, 3).reshape(depth, MEMBERS, LANES)
    keep_mean = 1.0 - jnp.sum(mixing, axis=0)
    combined = jnp.einsum("ij,ric->rjc", transform, members, preferred_element_type=jnp.float32)
    member_mean = jnp.sum(members, axis=1, dtype=jnp.float32, keepdims=True) / MEMBERS
    mixed = (combined + member_mean * keep_mean[None, :, None]).astype(jnp.bfloat16)
    mixed = mixed.reshape(depth, mem, local, LANES).transpose(1, 0, 2, 3)
    mixed = exchange(mixed, "mem").reshape(halves, tiles, depth, local, LANES)
    analysis = mixed.transpose(3, 0, 2, 1, 4).reshape(ensemble.shape)
    return (analysis, prior_gram, posterior_gram)


def solution(mesh):
    def body(*args):
        return per_device(mesh.shape["mem"], mesh.shape["space"], *args)

    split = P(None, ("parts", "space"))
    whole = P("mem", None, ("parts", "space"))
    parts = P("parts", None)
    return jax.shard_map(
        body, mesh=mesh, in_specs=(whole, parts, P(), split), out_specs=(whole, parts, parts),
        check_vma=False,
    )
```

time: 200 us -> 180 us (0.900)
  blocking collectives: 96.4 us -> 14.9 us
  waiting for transfers between devices: 14.4 us -> 87.7 us
  starting transfers between devices: 43.7 us -> 63.4 us
  between operations: 14.2 us -> 0.84 us
  matrix products: 13.6 us -> 3.27 us
  other arithmetic: 10.2 us -> 2 us
    psum x3 -> x0, blocking collectives: 96.4 us -> none  [over_axes(): array = lax.psum(array, axis)]
    all_to_all x1 -> x5, waiting for transfers between devices: 14.3 us -> 87.7 us  [exchange(): return lax.all_to_all(array, axis, split_axis=0, concat_axis=0, tiled=True)]
    all_to_all x1 -> x5, starting transfers between devices: 43.7 us -> 63.4 us  [exchange(): return lax.all_to_all(array, axis, split_axis=0, concat_axis=0, tiled=True)]
    all_to_all x0 -> x1, blocking collectives: none -> 14.9 us  [exchange(): return lax.all_to_all(array, axis, split_axis=0, concat_axis=0, tiled=True)]
    dot_general x3, matrix products: 12.6 us -> 2.23 us  [the longest x1 1.51 us: per_device(): jnp.einsum('ov,mvc->omc', obs_operator, ensemble, preferred_element_type=...]
    reduce_sum x5 -> x6, other arithmetic: 9.28 us -> 1.78 us  [the longest x1 1.38 us: per_device(): weight_sum = jnp.sum(own_weights)]
    unnamed x12 -> x8, local copies, waits for them, and re-layouts: 4.68 us -> 0.7 us
    reshape x0 -> x4, local copies, waits for them, and re-layouts: none -> 3.2 us  [the longest x2 1.25 us: per_device(): blocks = ensemble.reshape(local, halves, depth, tiles, LANES)]
  transfers between devices with their start and end apart: 2 -> 5, of which waited for: 1 -> 5; matrix products, arithmetic and copies ran while one was open for 6% -> 3% of each run, Pallas kernels for 0% -> 0%
where the time goes in v1:
time: 180 us; the launch traced here: 179 us
  waiting for transfers between devices  87.7 us (49%)
  starting transfers between devices  63.4 us (35%)
  blocking collectives  14.9 us (8%)
  local copies, waits for them, and re-layouts  7.13 us (4%)
  matrix products  3.27 us (2%)
  other arithmetic  2 us (1%)
    all_to_all x5, waiting for transfers between devices, exchange(): return lax.all_to_all(array, axis, split_axis=0, concat_axis=0, tiled=True)  87.7 us
    all_to_all x5, starting transfers between devices, exchange(): return lax.all_to_all(array, axis, split_axis=0, concat_axis=0, tiled=True)  63.4 us
    all_to_all x1, blocking collectives, exchange(): return lax.all_to_all(array, axis, split_axis=0, concat_axis=0, tiled=True)  14.9 us
  transfers between devices with their start and end apart: 5, of which 5 were waited for; matrix products, arithmetic and copies ran while one was open for 3% of the time, Pallas kernels for 0%

profile of v1, /device:TPU:80, one launch (start us, length us, event | category | flops | bytes accessed | tf_op | source)
XLA Modules:
  0.0 179.2 jit_solution(13152252369627029700)
XLA Ops:
  0.6 0.7 copy-done
  1.3 1.5 convolution_convert_fusion
  2.8 0.8 copy.37
  3.6 43.7 %all-to-all-start.2 = ((bf16[16,4,1024]{2,1,0:T(4,128)(2,1)}), bf16[16,4,1024]{2,1,0:T(4,128)(2,1)S(1)}, u32[]{:S(2)}, u32[]{:S(2)}) async-start(bf16[16,4,1024]{2,1,0:T(4,128)(2,1)} %copy.37), calls=%async_computation.2 | async-start | bytes 262144 | tf_op jit(solution)/shard_map/all_to_all | solution.py:12
  47.3 1.4 fusion.5
  48.7 13.2 %all-to-all-done.2 = bf16[16,4,1024]{2,1,0:T(4,128)(2,1)S(1)} async-done(((bf16[16,4,1024]{2,1,0:T(4,128)(2,1)}), bf16[16,4,1024]{2,1,0:T(4,128)(2,1)S(1)}, u32[]{:S(2)}, u32[]{:S(2)}) %all-to-all-start.2) | async-done | bytes 131104 | tf_op jit(solution)/shard_map/all_to_all | solution.py:12
  62.3 0.4 fusion.6
  62.7 0.7 concatenate.3
  63.3 14.9 %all_to_all.30 = f32[16,4,128]{2,1,0:T(4,128)S(1)} all-to-all(f32[16,4,128]{2,1,0:T(4,128)S(1)} %bitcast.46), channel_id=1, replica_groups=mesh['parts'=2,'mem'=16,'space'=16] {'space'}, dimensions={0} | all-to-all | bytes 65536 | tf_op jit(solution)/shard_map/all_to_all | solution.py:12
  78.3 0.6 broadcast_in_dim.4
  78.9 4.0 %all-to-all-start.4 = ((f32[16,4,128]{2,1,0:T(4,128)}), f32[16,4,128]{2,1,0:T(4,128)S(1)}, u32[]{:S(2)}, u32[]{:S(2)}) async-start(f32[16,4,128]{2,1,0:T(4,128)} %broadcast_in_dim.4), calls=%async_computation.4 | async-start | bytes 65536 | tf_op jit(solution)/shard_map/all_to_all | solution.py:12
  83.2 1.0 copy.31
  84.2 11.1 %all-to-all-done.4 = f32[16,4,128]{2,1,0:T(4,128)S(1)} async-done(((f32[16,4,128]{2,1,0:T(4,128)}), f32[16,4,128]{2,1,0:T(4,128)S(1)}, u32[]{:S(2)}, u32[]{:S(2)}) %all-to-all-start.4) | async-done | bytes 32800 | tf_op jit(solution)/shard_map/all_to_all | solution.py:12
  95.3 4.2 %all-to-all-start = ((bf16[16,35,4,128]{3,2,1,0:T(4,128)(2,1)}), bf16[16,35,4,128]{3,2,1,0:T(4,128)(2,1)S(1)}, u32[]{:S(2)}, u32[]{:S(2)}) async-start(bf16[16,35,4,128]{3,2,1,0:T(4,128)(2,1)} %bitcast.1), calls=%async_computation | async-start | bytes 1146880 | tf_op jit(solution)/shard_map/all_to_all | solution.py:12
  99.5 28.9 %all-to-all-done = bf16[16,35,4,128]{3,2,1,0:T(4,128)(2,1)S(1)} async-done(((bf16[16,35,4,128]{3,2,1,0:T(4,128)(2,1)}), bf16[16,35,4,128]{3,2,1,0:T(4,128)(2,1)S(1)}, u32[]{:S(2)}, u32[]{:S(2)}) %all-to-all-start) | async-done | bytes 573472 | tf_op jit(solution)/shard_map/all_to_all | solution.py:12
  128.4 0.6 broadcast_in_dim.5
  129.0 3.9 %all-to-all-start.5 = ((f32[16,4,128]{2,1,0:T(4,128)}), f32[16,4,128]{2,1,0:T(4,128)S(1)}, u32[]{:S(2)}, u32[]{:S(2)}) async-start(f32[16,4,128]{2,1,0:T(4,128)} %broadcast_in_dim.5), calls=%async_computation.5 | async-start | bytes 65536 | tf_op jit(solution)/shard_map/all_to_all | solution.py:12
  133.5 0.4 fusion.1
  133.9 1.0 copy.45
  134.9 5.4 %all-to-all-done.5 = f32[16,4,128]{2,1,0:T(4,128)S(1)} async-done(((f32[16,4,128]{2,1,0:T(4,128)}), f32[16,4,128]{2,1,0:T(4,128)S(1)}, u32[]{:S(2)}, u32[]{:S(2)}) %all-to-all-start.5) | async-done | bytes 32800 | tf_op jit(solution)/shard_map/all_to_all | solution.py:12
  140.3 7.6 %all-to-all-start.1 = ((bf16[16,35,4,128]{3,2,1,0:T(4,128)(2,1)}), bf16[16,35,4,128]{3,2,1,0:T(4,128)(2,1)S(1)}, u32[]{:S(2)}, u32[]{:S(2)}) async-start(bf16[16,35,4,128]{3,2,1,0:T(4,128)(2,1)} %bitcast.40), calls=%async_computation.1 | async-start | bytes 1146880 | tf_op jit(solution)/shard_map/all_to_all | solution.py:12
  148.2 0.8 fusion.8
  149.1 29.1 %all-to-all-done.1 = bf16[16,35,4,128]{3,2,1,0:T(4,128)(2,1)S(1)} async-done(((bf16[16,35,4,128]{3,2,1,0:T(4,128)(2,1)}), bf16[16,35,4,128]{3,2,1,0:T(4,128)(2,1)S(1)}, u32[]{:S(2)}, u32[]{:S(2)}) %all-to-all-start.1) | async-done | bytes 573472 | tf_op jit(solution)/shard_map/all_to_all | solution.py:12
  178.3 0.9 reshape.66
  (23 shorter events, 1.6 us)
Async XLA Ops:
  0.6 0.7 copy-start
  3.6 58.3 %all-to-all-start.2 = ((bf16[16,4,1024]{2,1,0:T(4,128)(2,1)}), bf16[16,4,1024]{2,1,0:T(4,128)(2,1)S(1)}, u32[]{:S(2)}, u32[]{:S(2)}) async-start(bf16[16,4,1024]{2,1,0:T(4,128)(2,1)} %copy.37), calls=%async_computation.2 | async-start | bytes 262144 | tf_op jit(solution)/shard_map/all_to_all | solution.py:12
  62.2 20.7 %copy-start.1 = (bf16[4,70,1024]{2,0,1:T(4,128)(2,1)S(1)}, bf16[4,70,1024]{2,0,1:T(4,128)(2,1)}, u32[]{:S(2)}) copy-start(bf16[4,70,1024]{2,0,1:T(4,128)(2,1)} %param.4) | copy-start | bytes 1720324
  78.9 16.4 %all-to-all-start.4 = ((f32[16,4,128]{2,1,0:T(4,128)}), f32[16,4,128]{2,1,0:T(4,128)S(1)}, u32[]{:S(2)}, u32[]{:S(2)}) async-start(f32[16,4,128]{2,1,0:T(4,128)} %broadcast_in_dim.4), calls=%async_computation.4 | async-start | bytes 65536 | tf_op jit(solution)/shard_map/all_to_all | solution.py:12
  95.3 4.2 %copy-start.2 = (bf16[64,64]{1,0:T(8,128)(2,1)S(1)}, bf16[64,64]{1,0:T(8,128)(2,1)}, u32[]{:S(2)}) copy-start(bf16[64,64]{1,0:T(8,128)(2,1)} %param.5) | copy-start | bytes 24580
  95.3 33.1 %all-to-all-start = ((bf16[16,35,4,128]{3,2,1,0:T(4,128)(2,1)}), bf16[16,35,4,128]{3,2,1,0:T(4,128)(2,1)S(1)}, u32[]{:S(2)}, u32[]{:S(2)}) async-start(bf16[16,35,4,128]{3,2,1,0:T(4,128)(2,1)} %bitcast.1), calls=%async_computation | async-start | bytes 1146880 | tf_op jit(solution)/shard_map/all_to_all | solution.py:12
  129.0 11.3 %all-to-all-start.5 = ((f32[16,4,128]{2,1,0:T(4,128)}), f32[16,4,128]{2,1,0:T(4,128)S(1)}, u32[]{:S(2)}, u32[]{:S(2)}) async-start(f32[16,4,128]{2,1,0:T(4,128)} %broadcast_in_dim.5), calls=%async_computation.5 | async-start | bytes 65536 | tf_op jit(solution)/shard_map/all_to_all | solution.py:12
  140.3 37.9 %all-to-all-start.1 = ((bf16[16,35,4,128]{3,2,1,0:T(4,128)(2,1)}), bf16[16,35,4,128]{3,2,1,0:T(4,128)(2,1)S(1)}, u32[]{:S(2)}, u32[]{:S(2)}) async-start(bf16[16,35,4,128]{3,2,1,0:T(4,128)(2,1)} %bitcast.40), calls=%async_computation.1 | async-start | bytes 1146880 | tf_op jit(solution)/shard_map/all_to_all | solution.py:12
  148.0 30.3 %copy-start.3 = (f32[64,64]{1,0:T(8,128)}, f32[64,64]{1,0:T(8,128)S(1)}, u32[]{:S(2)}) copy-start(f32[64,64]{1,0:T(8,128)S(1)} %slice_divide_fusion) | copy-start | bytes 49156

commit v2 on v1

v2 whole, which is shorter than its diff:
```python
import jax
import jax.numpy as jnp
from jax import lax
from jax.sharding import Mesh
from jax.sharding import PartitionSpec as P


MEMBERS = 64
LANES = 128
HIGHEST = lax.Precision.HIGHEST


def exchange(array, axis):
    return lax.all_to_all(array, axis, split_axis=0, concat_axis=0, tiled=True)


def per_device(mem, ensemble, transform, obs_operator, obs_weight):
    local, variables, cells = ensemble.shape
    quantities = obs_operator.shape[0]
    mixing = transform.astype(jnp.float32)
    width = cells // mem
    halves = LANES // width
    depth = variables // halves

    blocks = ensemble.reshape(local, halves, depth, mem, width)
    blocks = blocks.transpose(3, 2, 0, 1, 4).reshape(mem, depth, local, LANES)
    members = exchange(blocks, "mem")

    members = members.transpose(1, 0, 2, 3).reshape(depth, MEMBERS, LANES)
    keep_mean = 1.0 - jnp.sum(mixing, axis=0)
    combined = jnp.einsum("ij,ric->rjc", transform, members, preferred_element_type=jnp.float32)
    member_mean = jnp.sum(members, axis=1, dtype=jnp.float32, keepdims=True) / MEMBERS
    mixed = (combined + member_mean * keep_mean[None, :, None]).astype(jnp.bfloat16)
    mixed = mixed.reshape(depth, mem, local, LANES).transpose(1, 0, 2, 3)
    mixed = exchange(mixed, "mem")

    own_weights = lax.dynamic_slice_in_dim(obs_weight, lax.axis_index("mem") * width, width, 1)
    coefficient = obs_operator.astype(jnp.float32).reshape(quantities, halves, depth)
    coefficient = jnp.repeat(coefficient.transpose(0, 2, 1), width, axis=2)
    observed = jnp.sum(coefficient[:, :, None, :] * members.astype(jnp.float32)[None], axis=1)
    observed = jnp.sum(observed.reshape(quantities, MEMBERS, halves, width), axis=2)
    departures = observed - jnp.sum(observed, axis=1, keepdims=True) / MEMBERS
    partial = jnp.einsum(
        "oic,ojc->ij", departures * own_weights[:, None, :], departures, precision=HIGHEST
    )
    weight_sum = jnp.sum(own_weights)
    packed = jnp.concatenate([partial[: MEMBERS // 2], partial[MEMBERS // 2 :]], axis=1)
    packed = jnp.concatenate([packed, jnp.broadcast_to(weight_sum, (8, LANES))], axis=0)
    packed = lax.psum(packed, "space_0")
    packed = lax.psum(packed, "space_1")
    packed = exchange(jnp.broadcast_to(packed[None], (mem, *packed.shape)), "mem")
    packed = jnp.sum(packed, axis=0)
    gram_sum = jnp.concatenate([packed[:32, :MEMBERS], packed[:32, MEMBERS:]], axis=0)
    prior_gram = gram_sum / packed[32:33, :1]
    carried = jnp.dot(mixing.T, prior_gram, precision=HIGHEST)
    posterior_gram = jnp.dot(carried, mixing, precision=HIGHEST)

    mixed = mixed.reshape(mem, depth, local, halves, width)
    analysis = mixed.transpose(2, 3, 1, 0, 4).reshape(ensemble.shape)
    return (analysis, prior_gram, posterior_gram)


def solution(mesh):
    parts, mem, space = mesh.shape["parts"], mesh.shape["mem"], mesh.shape["space"]
    finer = Mesh(
        mesh.devices.reshape(parts, mem, space // 2, 2), ("parts", "mem", "space_0", "space_1")
    )

    def body(*args):
        return per_device(mem, *args)

    columns = ("parts", "space_0", "space_1")
    whole, rows, split = P("mem", None, columns), P("parts", None), P(None, columns)
    return jax.shard_map(
        body, mesh=finer, in_specs=(whole, rows, P(), split), out_specs=(whole, rows, rows),
        check_vma=False,
    )
```

time: 180 us -> 189 us (1.050)
  blocking collectives: 14.9 us -> 34.2 us
  waiting for transfers between devices: 87.7 us -> 76.2 us
  starting transfers between devices: 63.4 us -> 57.1 us
  local copies, waits for them, and re-layouts: 7.13 us -> 11.5 us
  other arithmetic: 2 us -> 6.31 us
    psum x0 -> x2, blocking collectives: none -> 34.2 us  [the longest x1 30.7 us: per_device(): packed = lax.psum(packed, 'space_0')]
    all_to_all x1 -> x0, blocking collectives: 14.9 us -> none  [exchange(): return lax.all_to_all(array, axis, split_axis=0, concat_axis=0, tiled=True)]
    all_to_all x5 -> x3, waiting for transfers between devices: 87.7 us -> 76.2 us  [exchange(): return lax.all_to_all(array, axis, split_axis=0, concat_axis=0, tiled=True)]
    all_to_all x5 -> x3, starting transfers between devices: 63.4 us -> 57.1 us  [exchange(): return lax.all_to_all(array, axis, split_axis=0, concat_axis=0, tiled=True)]
    reshape x3 -> x6, local copies, waits for them, and re-layouts: 2.19 us -> 6.96 us  [the longest x2 3.1 us: per_device(): blocks = ensemble.reshape(local, halves, depth, mem, width)]
    reduce_sum x3 -> x4, other arithmetic: 0.12 us -> 3.15 us  [the longest x2 1.82 us: per_device(): departures = observed - jnp.sum(observed, axis=1, keepdims=True) / MEMBERS]
  transfers between devices with their start and end apart: 5 -> 3, of which waited for: 5 -> 3; matrix products, arithmetic and copies ran while one was open for 3% -> 3% of each run, Pallas kernels for 0% -> 0%
where the time goes in v2:
time: 189 us; the launch traced here: 188 us
  waiting for transfers between devices  76.2 us (40%)
  starting transfers between devices  57.1 us (30%)
  blocking collectives  34.2 us (18%)
  local copies, waits for them, and re-layouts  11.5 us (6%)
  other arithmetic  6.31 us (3%)
  matrix products  2.02 us (1%)
    all_to_all x3, waiting for transfers between devices, exchange(): return lax.all_to_all(array, axis, split_axis=0, concat_axis=0, tiled=True)  76.2 us
    all_to_all x3, starting transfers between devices, exchange(): return lax.all_to_all(array, axis, split_axis=0, concat_axis=0, tiled=True)  57.1 us
    psum x1, blocking collectives, per_device(): packed = lax.psum(packed, 'space_0')  30.7 us
  transfers between devices with their start and end apart: 3, of which 3 were waited for; matrix products, arithmetic and copies ran while one was open for 3% of the time, Pallas kernels for 0%

profile of v2, /device:TPU:80, one launch (start us, length us, event | category | flops | bytes accessed | tf_op | source)
XLA Modules:
  0.0 188.2 jit_solution(717135360476084942)
XLA Ops:
  0.6 1.9 %reshape.51 = bf16[4,2,35,16,64]{4,3,0,2,1:T(8,128)(2,1)S(1)} reshape(bf16[4,70,1024]{2,0,1:T(4,128)(2,1)} %param.4) | data formatting | bytes 1146880 | tf_op jit(solution)/shard_map/reshape | solution.py:25
  2.6 1.2 copy.38
  3.8 1.4 reshape.52
  5.1 43.7 %all-to-all-start = ((bf16[16,35,4,128]{3,2,1,0:T(4,128)(2,1)}), bf16[16,35,4,128]{3,2,1,0:T(4,128)(2,1)S(1)}, u32[]{:S(2)}, u32[]{:S(2)}) async-start(bf16[16,35,4,128]{3,2,1,0:T(4,128)(2,1)} %reshape.52), calls=%async_computation | async-start | bytes 1146880 | tf_op jit(solution)/shard_map/all_to_all | solution.py:14
  49.1 0.8 broadcast_in_dim.4
  50.3 28.6 %all-to-all-done = bf16[16,35,4,128]{3,2,1,0:T(4,128)(2,1)S(1)} async-done(((bf16[16,35,4,128]{3,2,1,0:T(4,128)(2,1)}), bf16[16,35,4,128]{3,2,1,0:T(4,128)(2,1)S(1)}, u32[]{:S(2)}, u32[]{:S(2)}) %all-to-all-start) | async-done | bytes 573472 | tf_op jit(solution)/shard_map/all_to_all | solution.py:14
  79.4 1.8 multiply_reduce_fusion
  81.2 0.6 reshape.58
  81.9 1.3 reduce_sum.73
  83.2 1.4 fusion.7
  84.6 0.6 convolution_bitcast_fusion.1
  85.3 0.7 select_maximum_fusion
  86.0 30.7 %psum.14 = f32[40,128]{1,0:T(8,128)S(1)} all-reduce(f32[40,128]{1,0:T(8,128)S(1)} %select_maximum_fusion), channel_id=1, replica_groups=mesh['parts'=2,'mem'=16,'space_0'=8,'space_1'=2] {'space_0'}, use_global_device_ids=true, to_apply=%region_7.0 | all-reduce | flops 5120 | bytes 40960 | tf_op jit(solution)/shard_map/psum | solution.py:49
  116.7 3.4 %psum.15 = f32[40,128]{1,0:T(8,128)S(1)} all-reduce(f32[40,128]{1,0:T(8,128)S(1)} %psum.14), channel_id=1, replica_groups=mesh['parts'=2,'mem'=16,'space_0'=8,'space_1'=2] {'space_1'}, use_global_device_ids=true, to_apply=%region_8.0 | all-reduce | flops 5120 | bytes 40960 | tf_op jit(solution)/shard_map/psum | solution.py:50
  120.2 0.7 broadcast_in_dim.5
  120.9 7.4 %all-to-all-start.2 = ((f32[16,40,128]{2,1,0:T(8,128)}), f32[16,40,128]{2,1,0:T(8,128)S(1)}, u32[]{:S(2)}, u32[]{:S(2)}) async-start(f32[16,40,128]{2,1,0:T(8,128)} %broadcast_in_dim.5), calls=%async_computation.2 | async-start | bytes 655360 | tf_op jit(solution)/shard_map/all_to_all | solution.py:14
  129.0 1.0 copy.39
  130.0 19.7 %all-to-all-done.2 = f32[16,40,128]{2,1,0:T(8,128)S(1)} async-done(((f32[16,40,128]{2,1,0:T(8,128)}), f32[16,40,128]{2,1,0:T(8,128)S(1)}, u32[]{:S(2)}, u32[]{:S(2)}) %all-to-all-start.2) | async-done | bytes 327712 | tf_op jit(solution)/shard_map/all_to_all | solution.py:14
  149.7 6.1 %all-to-all-start.1 = ((bf16[16,35,4,128]{3,2,1,0:T(4,128)(2,1)}), bf16[16,35,4,128]{3,2,1,0:T(4,128)(2,1)S(1)}, u32[]{:S(2)}, u32[]{:S(2)}) async-start(bf16[16,35,4,128]{3,2,1,0:T(4,128)(2,1)} %bitcast.36), calls=%async_computation.1 | async-start | bytes 1146880 | tf_op jit(solution)/shard_map/all_to_all | solution.py:14
  155.8 0.5 slice.24
  156.4 0.7 maximum_divide_fusion
  157.3 0.8 fusion.11
  158.1 27.9 %all-to-all-done.1 = bf16[16,35,4,128]{3,2,1,0:T(4,128)(2,1)S(1)} async-done(((bf16[16,35,4,128]{3,2,1,0:T(4,128)(2,1)}), bf16[16,35,4,128]{3,2,1,0:T(4,128)(2,1)S(1)}, u32[]{:S(2)}, u32[]{:S(2)}) %all-to-all-start.1) | async-done | bytes 573472 | tf_op jit(solution)/shard_map/all_to_all | solution.py:14
  186.8 1.5 reshape.56
  (25 shorter events, 3.0 us)
Async XLA Ops:
  3.7 45.1 %copy-start.2 = (bf16[16,70]{1,0:T(8,128)(2,1)S(1)}, bf16[16,70]{1,0:T(8,128)(2,1)}, u32[]{:S(2)}) copy-start(bf16[16,70]{1,0:T(8,128)(2,1)} %param.6) | copy-start | bytes 6724
  5.1 73.9 %all-to-all-start = ((bf16[16,35,4,128]{3,2,1,0:T(4,128)(2,1)}), bf16[16,35,4,128]{3,2,1,0:T(4,128)(2,1)S(1)}, u32[]{:S(2)}, u32[]{:S(2)}) async-start(bf16[16,35,4,128]{3,2,1,0:T(4,128)(2,1)} %reshape.52), calls=%async_computation | async-start | bytes 1146880 | tf_op jit(solution)/shard_map/all_to_all | solution.py:14
  84.6 43.7 %copy-start = (bf16[64,64]{1,0:T(8,128)(2,1)S(1)}, bf16[64,64]{1,0:T(8,128)(2,1)}, u32[]{:S(2)}) copy-start(bf16[64,64]{1,0:T(8,128)(2,1)} %param.5) | copy-start | bytes 24580
  120.9 28.8 %all-to-all-start.2 = ((f32[16,40,128]{2,1,0:T(8,128)}), f32[16,40,128]{2,1,0:T(8,128)S(1)}, u32[]{:S(2)}, u32[]{:S(2)}) async-start(f32[16,40,128]{2,1,0:T(8,128)} %broadcast_in_dim.5), calls=%async_computation.2 | async-start | bytes 655360 | tf_op jit(solution)/shard_map/all_to_all | solution.py:14
  149.7 36.3 %all-to-all-start.1 = ((bf16[16,35,4,128]{3,2,1,0:T(4,128)(2,1)}), bf16[16,35,4,128]{3,2,1,0:T(4,128)(2,1)S(1)}, u32[]{:S(2)}, u32[]{:S(2)}) async-start(bf16[16,35,4,128]{3,2,1,0:T(4,128)(2,1)} %bitcast.36), calls=%async_computation.1 | async-start | bytes 1146880 | tf_op jit(solution)/shard_map/all_to_all | solution.py:14
  157.1 29.7 %copy-start.1 = (f32[64,64]{1,0:T(8,128)}, f32[64,64]{1,0:T(8,128)S(1)}, u32[]{:S(2)}) copy-start(f32[64,64]{1,0:T(8,128)S(1)} %maximum_divide_fusion) | copy-start | bytes 49156

commit v3 on v2

v3 whole, which is shorter than its diff:
```python
import functools

import jax
import jax.numpy as jnp
from jax import lax
from jax.experimental import pallas as pl
from jax.experimental.pallas import tpu as pltpu
from jax.sharding import Mesh
from jax.sharding import PartitionSpec as P


MEMBERS = 64
LANES = 128
GROUP = 4
VMEM_LIMIT = 12 << 20
HIGHEST = lax.Precision.HIGHEST


SMEM = pl.BlockSpec(memory_space=pltpu.SMEM)
VMEM = pl.BlockSpec(memory_space=pltpu.VMEM)


def exchange(array, axis):
    return lax.all_to_all(array, axis, split_axis=0, concat_axis=0, tiled=True)


def to_partner(array):
    return lax.ppermute(array, "space_1", [(0, 1), (1, 0)])


def vmem(shape, dtype):
    return jax.ShapeDtypeStruct(shape, dtype)


def kernel(body, out_shape, in_specs, flops, moved, scratch=()):
    many = isinstance(out_shape, tuple)
    return pl.pallas_call(
        body, out_shape=out_shape, in_specs=in_specs,
        out_specs=(VMEM,) * len(out_shape) if many else VMEM, scratch_shapes=scratch,
        cost_estimate=pl.CostEstimate(flops=flops, bytes_accessed=moved, transcendentals=0),
        compiler_params=pltpu.CompilerParams(vmem_limit_bytes=VMEM_LIMIT),
    )


def pack_kernel(x_ref, o_ref):
    depth, half = o_ref.shape[1], LANES // 2
    for tile in range(x_ref.shape[2] // LANES):
        at = slice(tile * LANES, (tile + 1) * LANES)
        low, high = x_ref[:depth, :, at], x_ref[depth:, :, at]
        o_ref[2 * tile] = jnp.concatenate([low[..., :half], high[..., :half]], axis=-1)
        o_ref[2 * tile + 1] = jnp.concatenate([low[..., half:], high[..., half:]], axis=-1)


def unpack_kernel(x_ref, o_ref):
    depth, half = x_ref.shape[1], LANES // 2
    for tile in range(o_ref.shape[2] // LANES):
        at = slice(tile * LANES, (tile + 1) * LANES)
        left, right = x_ref[2 * tile], x_ref[2 * tile + 1]
        o_ref[:depth, :, at] = jnp.concatenate([left[..., :half], right[..., :half]], axis=-1)
        o_ref[depth:, :, at] = jnp.concatenate([left[..., half:], right[..., half:]], axis=-1)


def fold(array, rows):
    return jnp.concatenate(
        [array[i * rows : (i + 1) * rows] for i in range(array.shape[0] // rows)], axis=1
    )


def unfold(array, width):
    return jnp.concatenate(
        [array[:, i * width : (i + 1) * width] for i in range(LANES // width)], axis=0
    )


def prepare_kernel(
    mem_ref, operator_ref, weight_ref, transform_ref,
    factor_ref, pairs_ref, total_ref, mixing_ref, turned_ref,
):
    depth, quantities, _ = factor_ref.shape
    low = lax.broadcasted_iota(jnp.int32, (quantities, LANES), 1) < LANES // 2
    operator = operator_ref[...].astype(jnp.float32)
    for r in range(depth):
        factor_ref[r] = jnp.where(low, operator[:, r : r + 1], operator[:, depth + r : depth + r + 1])
    place = mem_ref[0, 0]
    tile = weight_ref[:, pl.ds(pl.multiple_of(place // 2 * LANES, LANES), LANES)]
    turned = pltpu.roll(tile, LANES // 2, 1)
    even = place % 2 == 0
    near, far = jnp.where(even, tile, turned), jnp.where(even, turned, tile)
    for pair in range(quantities // 2):
        one, two = near[2 * pair : 2 * pair + 1], far[2 * pair + 1 : 2 * pair + 2]
        pairs_ref[pair : pair + 1, :] = jnp.where(low[:1], one, two)
    total_ref[...] = jnp.full(total_ref.shape, jnp.sum(weight_ref[...]), jnp.float32)
    mixing = transform_ref[...].astype(jnp.float32)
    mixing_ref[...] = mixing
    turned_ref[...] = mixing.T


def gram_kernel(core_ref, x_ref, factor_ref, weight_ref, total_ref, mine_ref, other_ref, lhs, rhs):
    depth, quantities = factor_ref.shape[:2]
    low = lax.broadcasted_iota(jnp.int32, (MEMBERS, LANES), 1) < LANES // 2
    zero = jnp.zeros((MEMBERS, LANES), jnp.float32)
    for first in range(0, quantities, GROUP):

        def step(r, sums, first=first):
            x = x_ref[r].astype(jnp.float32)
            return tuple(
                s + x * factor_ref[r, pl.ds(first + i, 1), :] for i, s in enumerate(sums)
            )

        sums = lax.fori_loop(0, depth, step, (zero,) * GROUP, unroll=5)
        for i in range(0, GROUP, 2):
            one, two = sums[i], sums[i + 1]
            both = jnp.where(low, one, two) + pltpu.roll(jnp.where(low, two, one), LANES // 2, 1)
            departures = both - jnp.sum(both, axis=0, keepdims=True) / MEMBERS
            pair = (first + i) // 2
            at = slice(pair * LANES, (pair + 1) * LANES)
            rhs[:, at] = departures
            lhs[:, at] = departures * weight_ref[pair : pair + 1, :]
    gram = lax.dot_general(
        lhs[...], rhs[...], (((1,), (1,)), ((), ())), precision=HIGHEST,
        preferred_element_type=jnp.float32,
    )
    half, quarter = MEMBERS // 2, MEMBERS // 4
    cross = gram[:half, half:]
    weights = total_ref[:4]
    upper = jnp.concatenate(
        [fold(gram[:half, :half], 8), fold(cross[:quarter], 4), weights], axis=0
    )
    lower = jnp.concatenate(
        [fold(gram[half:, half:], 8), fold(cross[quarter:], 4), weights], axis=0
    )
    first_core = core_ref[0, 0] == 0
    mine_ref[...] = jnp.where(first_core, upper, lower)
    other_ref[...] = jnp.where(first_core, lower, upper)


def final_kernel(core_ref, mine_ref, other_ref, mixing_ref, turned_ref, prior_ref, posterior_ref):
    half = MEMBERS // 2
    first_core = core_ref[0, 0] == 0
    mine, other = mine_ref[...], other_ref[...]
    upper, lower = jnp.where(first_core, mine, other), jnp.where(first_core, other, mine)
    cross = jnp.concatenate([unfold(upper[8:], half), unfold(lower[8:], half)], axis=0)
    gram = jnp.concatenate(
        [
            jnp.concatenate([unfold(upper[:8], half), cross], axis=1),
            jnp.concatenate([cross.T, unfold(lower[:8], half)], axis=1),
        ],
        axis=0,
    )
    prior_ref[...] = gram
    dot = functools.partial(jnp.dot, precision=HIGHEST, preferred_element_type=jnp.float32)
    posterior_ref[...] = dot(dot(turned_ref[...], gram), mixing_ref[...])


def per_device(mem, ensemble, transform, obs_operator, obs_weight):
    local, variables, cells = ensemble.shape
    quantities = obs_operator.shape[0]
    halves = LANES * mem // cells
    depth = variables // halves
    core = lax.axis_index("space_1").astype(jnp.int32).reshape(1, 1)
    place = lax.axis_index("mem").astype(jnp.int32).reshape(1, 1)
    state_bytes = 2 * ensemble.size
    square = vmem((MEMBERS, MEMBERS), jnp.float32)

    blocks = kernel(
        pack_kernel, vmem((mem, depth, local, LANES), jnp.bfloat16), [VMEM],
        state_bytes, 2 * state_bytes,
    )(ensemble.transpose(1, 0, 2))
    members = exchange(blocks, "mem")

    shapes = ((depth, quantities, LANES), (quantities // halves, LANES), (8, LANES))
    factor, pairs, total, mixing, turned = kernel(
        prepare_kernel, (*(vmem(s, jnp.float32) for s in shapes), square, square),
        [SMEM, VMEM, VMEM, VMEM], 4 * obs_weight.size, 8 * obs_weight.size,
    )(place, obs_operator, obs_weight, transform)

    members = members.transpose(1, 0, 2, 3).reshape(depth, MEMBERS, LANES)
    keep_mean = 1.0 - jnp.sum(mixing, axis=0)
    combined = jnp.einsum("ij,ric->rjc", transform, members, preferred_element_type=jnp.float32)
    member_mean = jnp.sum(members, axis=1, dtype=jnp.float32, keepdims=True) / MEMBERS
    mixed = (combined + member_mean * keep_mean[None, :, None]).astype(jnp.bfloat16)
    mixed = mixed.reshape(depth, mem, local, LANES).transpose(1, 0, 2, 3)
    mixed = exchange(mixed, "mem")

    mine, other = kernel(
        gram_kernel, (vmem((16, LANES), jnp.float32),) * 2,
        [SMEM, VMEM, VMEM, VMEM, VMEM], 4 * depth * quantities * MEMBERS * LANES, state_bytes,
        [pltpu.VMEM((MEMBERS, quantities // halves * LANES), jnp.float32)] * 2,
    )(core, members, factor, pairs, total)
    mine = mine + to_partner(other)
    mine = lax.psum(mine, "space_0")
    mine = (mine[:12] / mine[12:13]).reshape(3, 4, LANES)
    mine = exchange(jnp.broadcast_to(mine[None], (mem, *mine.shape)), "mem")
    mine = jnp.sum(mine, axis=0).reshape(12, LANES)
    other = to_partner(mine)
    prior_gram, posterior_gram = kernel(
        final_kernel, (square, square), [SMEM, VMEM, VMEM, VMEM, VMEM],
        4 * MEMBERS**3, 16 * MEMBERS**2,
    )(core, mine, other, mixing, turned)

    analysis = kernel(
        unpack_kernel, vmem((variables, local, cells), jnp.bfloat16), [VMEM],
        state_bytes, 2 * state_bytes,
    )(mixed)
    return (analysis.transpose(1, 0, 2), prior_gram, posterior_gram)


def solution(mesh):
    parts, mem, space = mesh.shape["parts"], mesh.shape["mem"], mesh.shape["space"]
    finer = Mesh(
        mesh.devices.reshape(parts, mem, space // 2, 2), ("parts", "mem", "space_0", "space_1")
    )

    def body(*args):
        return per_device(mem, *args)

    columns = ("parts", "space_0", "space_1")
    whole, rows, split = P("mem", None, columns), P("parts", None), P(None, columns)
    return jax.shard_map(
        body, mesh=finer, in_specs=(whole, rows, P(), split), out_specs=(whole, rows, rows),
        check_vma=False,
    )
```

time: 189 us -> 154 us (0.81)
  blocking collectives: 34.2 us -> 18.2 us
  waiting for transfers between devices: 76.2 us -> 64.8 us
  local copies, waits for them, and re-layouts: 11.5 us -> 3.03 us
  Pallas kernels: 0 us -> 6.66 us
  other arithmetic: 6.31 us -> 0.34 us
  starting transfers between devices: 57.1 us -> 59.1 us
    psum x2 -> x1, blocking collectives: 34.2 us -> 18.2 us  [per_device(): mine = lax.psum(mine, 'space_0')]
    all_to_all x3, waiting for transfers between devices: 76.2 us -> 62.8 us  [exchange(): return lax.all_to_all(array, axis, split_axis=0, concat_axis=0, tiled=True)]
    reshape x6 -> x1, local copies, waits for them, and re-layouts: 6.96 us -> 0.01 us  [per_device(): mine = jnp.sum(mine, axis=0).reshape(12, LANES)]
    pallas_call x0 -> x5, Pallas kernels: none -> 6.66 us  [the longest x1 2.34 us: per_device(): kernel(gram_kernel, (vmem((16, LANES), jnp.float32),) * 2, [SMEM, VMEM, V...]
    reduce_sum x5 -> x1, other arithmetic: 4.53 us -> 0.03 us  [per_device(): mine = jnp.sum(mine, axis=0).reshape(12, LANES)]
    ppermute x0 -> x2, starting transfers between devices: none -> 3.9 us  [to_partner(): return lax.ppermute(array, 'space_1', [(0, 1), (1, 0)])]
    ppermute x0 -> x2, waiting for transfers between devices: none -> 2.01 us  [to_partner(): return lax.ppermute(array, 'space_1', [(0, 1), (1, 0)])]
    all_to_all x3, starting transfers between devices: 57.1 us -> 55.2 us  [exchange(): return lax.all_to_all(array, axis, split_axis=0, concat_axis=0, tiled=True)]
  transfers between devices with their start and end apart: 3 -> 5, of which waited for: 3 -> 5; matrix products, arithmetic and copies ran while one was open for 3% -> 1% of each run, Pallas kernels for 0% -> 1%
where the time goes in v3:
time: 154 us; the launch traced here: 153 us
  waiting for transfers between devices  64.8 us (42%)
  starting transfers between devices  59.1 us (38%)
  blocking collectives  18.2 us (12%)
  Pallas kernels  6.66 us (4%)
  local copies, waits for them, and re-layouts  3.03 us (2%)
    all_to_all x3, waiting for transfers between devices, exchange(): return lax.all_to_all(array, axis, split_axis=0, concat_axis=0, tiled=True)  62.8 us
    all_to_all x3, starting transfers between devices, exchange(): return lax.all_to_all(array, axis, split_axis=0, concat_axis=0, tiled=True)  55.2 us
    psum x1, blocking collectives, per_device(): mine = lax.psum(mine, 'space_0')  18.2 us
    ppermute x2, starting transfers between devices, to_partner(): return lax.ppermute(array, 'space_1', [(0, 1), (1, 0)])  3.9 us
  transfers between devices with their start and end apart: 5, of which 5 were waited for; matrix products, arithmetic and copies ran while one was open for 1% of the time, Pallas kernels for 1%

profile of v3, /device:TPU:80, one launch (start us, length us, event | category | flops | bytes accessed | tf_op | source)
XLA Modules:
  0.0 153.4 jit_solution(14334231308172681334)
XLA Ops:
  0.6 0.0 copy-start
  0.6 1.1 copy-done
  1.7 1.5 shard_map.67
  3.2 43.8 %all-to-all-start = ((bf16[16,35,4,128]{3,2,1,0:T(4,128)(2,1)}), bf16[16,35,4,128]{3,2,1,0:T(4,128)(2,1)S(1)}, u32[]{:S(2)}, u32[]{:S(2)}) async-start(bf16[16,35,4,128]{3,2,1,0:T(4,128)(2,1)} %shard_map.67), calls=%async_computation | async-start | bytes 1146880 | tf_op jit(solution)/shard_map/all_to_all | solution.py:24
  47.0 0.0 copy-done.1
  47.0 0.3 shard_map.68
  47.3 29.8 %all-to-all-done = bf16[16,35,4,128]{3,2,1,0:T(4,128)(2,1)S(1)} async-done(((bf16[16,35,4,128]{3,2,1,0:T(4,128)(2,1)}), bf16[16,35,4,128]{3,2,1,0:T(4,128)(2,1)S(1)}, u32[]{:S(2)}, u32[]{:S(2)}) %all-to-all-start) | async-done | bytes 573472 | tf_op jit(solution)/shard_map/all_to_all | solution.py:24
  77.2 0.3 copy.12
  77.5 2.3 %shard_map.70 = (f32[16,128]{1,0:T(8,128)S(1)}, f32[16,128]{1,0:T(8,128)S(1)}) custom-call(s32[1,1]{1,0:T(1,128)} %bitcast.9.core_ref, bf16[35,64,128]{2,1,0:T(8,128)(2,1)S(1)} %bitcast.23, f32[35,16,128]{2,1,0:T(8,128)S(1)} %get-tuple-element.13.factor_ref, f32[8,128]{1,0:T(8,128)S(1)} %get-tuple-element.14.weight_ref, f32[8,128]{1,0:T(8,128)S(1)} %get-tuple-element.15.total_ref), custom_call_target="tpu_custom_call" | custom-call | flops 18350080 | bytes 573440 | tf_op jit(solution)/shard_map/pallas_call | solution.py:185
  79.8 2.0 %collective-permute-start = (f32[16,128]{1,0:T(8,128)S(1)}, f32[16,128]{1,0:T(8,128)S(1)}, u32[]{:S(2)}, u32[]{:S(2)}) collective-permute-start(f32[16,128]{1,0:T(8,128)S(1)} %get-tuple-element.17), channel_id=1, source_target_pairs={{0,1},{1,0},{2,3},{3,2},{4,5},{5,4},{6,7},{7,6},{8,9},{9,8},{10,11... | collective-permute-start | bytes 24584 | tf_op jit(solution)/shard_map/ppermute | solution.py:28
  81.8 0.3 convert_reduce_fusion
  82.0 0.9 collective-permute-done
  82.9 18.2 %psum.7 = f32[16,128]{1,0:T(8,128)S(1)} all-reduce(f32[16,128]{1,0:T(8,128)S(1)} %add.9), channel_id=1, replica_groups=mesh['parts'=2,'mem'=16,'space_0'=8,'space_1'=2] {'space_0'}, use_global_device_ids=true, to_apply=%region_2.0 | all-reduce | flops 2048 | bytes 16384 | tf_op jit(solution)/shard_map/psum | solution.py:191
  101.2 0.6 broadcast_in_dim.10
  101.8 7.4 %all-to-all-start.2 = ((f32[16,3,4,128]{3,2,1,0:T(4,128)}), f32[16,3,4,128]{3,2,1,0:T(4,128)S(1)}, u32[]{:S(2)}, u32[]{:S(2)}) async-start(f32[16,3,4,128]{3,2,1,0:T(4,128)} %broadcast_in_dim.10), calls=%async_computation.2 | async-start | bytes 196608 | tf_op jit(solution)/shard_map/all_to_all | solution.py:24
  109.3 0.4 fusion.1
  109.6 1.0 copy.17
  110.6 11.5 %all-to-all-done.2 = f32[16,3,4,128]{3,2,1,0:T(4,128)S(1)} async-done(((f32[16,3,4,128]{3,2,1,0:T(4,128)}), f32[16,3,4,128]{3,2,1,0:T(4,128)S(1)}, u32[]{:S(2)}, u32[]{:S(2)}) %all-to-all-start.2) | async-done | bytes 98336 | tf_op jit(solution)/shard_map/all_to_all | solution.py:24
  122.1 4.0 %all-to-all-start.1 = ((bf16[16,35,4,128]{3,2,1,0:T(4,128)(2,1)}), bf16[16,35,4,128]{3,2,1,0:T(4,128)(2,1)S(1)}, u32[]{:S(2)}, u32[]{:S(2)}) async-start(bf16[16,35,4,128]{3,2,1,0:T(4,128)(2,1)} %bitcast.22), calls=%async_computation.1 | async-start | bytes 1146880 | tf_op jit(solution)/shard_map/all_to_all | solution.py:24
  126.2 1.9 %collective-permute-start.1 = (f32[12,128]{1,0:T(8,128)S(1)}, f32[12,128]{1,0:T(8,128)S(1)}, u32[]{:S(2)}, u32[]{:S(2)}) collective-permute-start(f32[12,128]{1,0:T(8,128)S(1)} %reshape.33.mine_ref), channel_id=1, source_target_pairs={{0,1},{1,0},{2,3},{3,2},{4,5},{5,4},{6,7},{7,6},{8,9},{9,8},{10,11... | collective-permute-start | bytes 18440 | tf_op jit(solution)/shard_map/ppermute | solution.py:28
  128.2 1.1 collective-permute-done.1.other_ref
  129.3 1.1 shard_map.71
  130.4 21.5 %all-to-all-done.1.x_ref = bf16[16,35,4,128]{3,2,1,0:T(4,128)(2,1)S(1)} async-done(((bf16[16,35,4,128]{3,2,1,0:T(4,128)(2,1)}), bf16[16,35,4,128]{3,2,1,0:T(4,128)(2,1)S(1)}, u32[]{:S(2)}, u32[]{:S(2)}) %all-to-all-start.1) | async-done | bytes 573472 | tf_op jit(solution)/shard_map/all_to_all | solution.py:24
  151.9 1.5 shard_map.69
  (14 shorter events, 0.1 us)
Async XLA Ops:
  0.6 1.1 copy-start
  3.2 43.8 %copy-start.1 = (bf16[64,64]{1,0:T(8,128)(2,1)S(1)}, bf16[64,64]{1,0:T(8,128)(2,1)}, u32[]{:S(2)}) copy-start(bf16[64,64]{1,0:T(8,128)(2,1)} %transform_ref.1) | copy-start | bytes 24580
  3.2 43.8 %copy-start.2 = (f32[16,1024]{1,0:T(8,128)S(1)}, f32[16,1024]{1,0:T(8,128)}, u32[]{:S(2)}) copy-start(f32[16,1024]{1,0:T(8,128)} %weight_ref.1) | copy-start | bytes 196612
  3.2 43.9 %copy-start.3 = (bf16[16,70]{1,0:T(8,128)(2,1)S(1)}, bf16[16,70]{1,0:T(8,128)(2,1)}, u32[]{:S(2)}) copy-start(bf16[16,70]{1,0:T(8,128)(2,1)} %operator_ref.1) | copy-start | bytes 6724
  3.2 74.0 %all-to-all-start = ((bf16[16,35,4,128]{3,2,1,0:T(4,128)(2,1)}), bf16[16,35,4,128]{3,2,1,0:T(4,128)(2,1)S(1)}, u32[]{:S(2)}, u32[]{:S(2)}) async-start(bf16[16,35,4,128]{3,2,1,0:T(4,128)(2,1)} %shard_map.67), calls=%async_computation | async-start | bytes 1146880 | tf_op jit(solution)/shard_map/all_to_all | solution.py:24
  79.8 3.1 %collective-permute-start = (f32[16,128]{1,0:T(8,128)S(1)}, f32[16,128]{1,0:T(8,128)S(1)}, u32[]{:S(2)}, u32[]{:S(2)}) collective-permute-start(f32[16,128]{1,0:T(8,128)S(1)} %get-tuple-element.17), channel_id=1, source_target_pairs={{0,1},{1,0},{2,3},{3,2},{4,5},{5,4},{6,7},{7,6},{8,9},{9,8},{10,11... | collective-permute-start | bytes 24584 | tf_op jit(solution)/shard_map/ppermute | solution.py:28
  101.8 20.3 %all-to-all-start.2 = ((f32[16,3,4,128]{3,2,1,0:T(4,128)}), f32[16,3,4,128]{3,2,1,0:T(4,128)S(1)}, u32[]{:S(2)}, u32[]{:S(2)}) async-start(f32[16,3,4,128]{3,2,1,0:T(4,128)} %broadcast_in_dim.10), calls=%async_computation.2 | async-start | bytes 196608 | tf_op jit(solution)/shard_map/all_to_all | solution.py:24
  122.1 29.8 %all-to-all-start.1 = ((bf16[16,35,4,128]{3,2,1,0:T(4,128)(2,1)}), bf16[16,35,4,128]{3,2,1,0:T(4,128)(2,1)S(1)}, u32[]{:S(2)}, u32[]{:S(2)}) async-start(bf16[16,35,4,128]{3,2,1,0:T(4,128)(2,1)} %bitcast.22), calls=%async_computation.1 | async-start | bytes 1146880 | tf_op jit(solution)/shard_map/all_to_all | solution.py:24
  126.2 3.1 %collective-permute-start.1 = (f32[12,128]{1,0:T(8,128)S(1)}, f32[12,128]{1,0:T(8,128)S(1)}, u32[]{:S(2)}, u32[]{:S(2)}) collective-permute-start(f32[12,128]{1,0:T(8,128)S(1)} %reshape.33.mine_ref), channel_id=1, source_target_pairs={{0,1},{1,0},{2,3},{3,2},{4,5},{5,4},{6,7},{7,6},{8,9},{9,8},{10,11... | collective-permute-start | bytes 18440 | tf_op jit(solution)/shard_map/ppermute | solution.py:28

commit v4 on v3

--- a/solution.py
+++ b/solution.py
@@ -12,6 +12,9 @@
 MEMBERS = 64
 LANES = 128
 GROUP = 4
+BLOCK = 16
+PACK_TILES = 2
+GRAM_ROWS = 20
 VMEM_LIMIT = 12 << 20
 HIGHEST = lax.Precision.HIGHEST
 
@@ -24,21 +27,17 @@
     return lax.all_to_all(array, axis, split_axis=0, concat_axis=0, tiled=True)
 
 
-def to_partner(array):
-    return lax.ppermute(array, "space_1", [(0, 1), (1, 0)])
-
-
 def vmem(shape, dtype):
     return jax.ShapeDtypeStruct(shape, dtype)
 
 
-def kernel(body, out_shape, in_specs, flops, moved, scratch=()):
+def kernel(body, out_shape, in_specs, flops, moved, scratch=(), out_specs=None, **more):
     many = isinstance(out_shape, tuple)
     return pl.pallas_call(
-        body, out_shape=out_shape, in_specs=in_specs,
-        out_specs=(VMEM,) * len(out_shape) if many else VMEM, scratch_shapes=scratch,
+        body, out_shape=out_shape, in_specs=in_specs, scratch_shapes=scratch,
+        out_specs=out_specs or ((VMEM,) * len(out_shape) if many else VMEM),
         cost_estimate=pl.CostEstimate(flops=flops, bytes_accessed=moved, transcendentals=0),
-        compiler_params=pltpu.CompilerParams(vmem_limit_bytes=VMEM_LIMIT),
+        **{"compiler_params": pltpu.CompilerParams(vmem_limit_bytes=VMEM_LIMIT), **more},
     )
 
 
@@ -60,16 +59,28 @@
         o_ref[depth:, :, at] = jnp.concatenate([left[..., half:], right[..., half:]], axis=-1)
 
 
-def fold(array, rows):
-    return jnp.concatenate(
-        [array[i * rows : (i + 1) * rows] for i in range(array.shape[0] // rows)], axis=1
-    )
-
-
-def unfold(array, width):
-    return jnp.concatenate(
-        [array[:, i * width : (i + 1) * width] for i in range(LANES // width)], axis=0
-    )
+def fold(gram):
+    rows = [gram[at : at + BLOCK, at:] for at in range(0, MEMBERS, BLOCK)]
+    first = jnp.concatenate([rows[0], rows[1], rows[3]], axis=1)
+    rest = jnp.concatenate([rows[2][i : i + 4] for i in range(0, BLOCK, 4)], axis=1)
+    return jnp.concatenate([first, rest], axis=0)
+
+
+def unfold(first, rest):
+    width = 2 * BLOCK
+    third = jnp.concatenate([rest[:, i : i + width] for i in range(0, LANES, width)], axis=0)
+    rows = [first[:, :64], first[:, 64:112], third, first[:, 112:]]
+    upper = jnp.concatenate(
+        [
+            jnp.concatenate([jnp.zeros((BLOCK, MEMBERS - r.shape[1]), jnp.float32), r], axis=1)
+            if r.shape[1] < MEMBERS else r
+            for r in rows
+        ],
+        axis=0,
+    )
+    row = lax.broadcasted_iota(jnp.int32, upper.shape, 0) // BLOCK
+    column = lax.broadcasted_iota(jnp.int32, upper.shape, 1) // BLOCK
+    return jnp.where(row <= column, upper, upper.T)
 
 
 def prepare_kernel(
@@ -95,7 +106,7 @@
     turned_ref[...] = mixing.T
 
 
-def gram_kernel(core_ref, x_ref, factor_ref, weight_ref, total_ref, mine_ref, other_ref, lhs, rhs):
+def gram_kernel(x_ref, factor_ref, weight_ref, total_ref, gram_ref, lhs, rhs):
     depth, quantities = factor_ref.shape[:2]
     low = lax.broadcasted_iota(jnp.int32, (MEMBERS, LANES), 1) < LANES // 2
     zero = jnp.zeros((MEMBERS, LANES), jnp.float32)
@@ -120,33 +131,19 @@
         lhs[...], rhs[...], (((1,), (1,)), ((), ())), precision=HIGHEST,
         preferred_element_type=jnp.float32,
     )
-    half, quarter = MEMBERS // 2, MEMBERS // 4
-    cross = gram[:half, half:]
-    weights = total_ref[:4]
-    upper = jnp.concatenate(
-        [fold(gram[:half, :half], 8), fold(cross[:quarter], 4), weights], axis=0
-    )
-    lower = jnp.concatenate(
-        [fold(gram[half:, half:], 8), fold(cross[quarter:], 4), weights], axis=0
-    )
-    first_core = core_ref[0, 0] == 0
-    mine_ref[...] = jnp.where(first_core, upper, lower)
-    other_ref[...] = jnp.where(first_core, lower, upper)
-
-
-def final_kernel(core_ref, mine_ref, other_ref, mixing_ref, turned_ref, prior_ref, posterior_ref):
-    half = MEMBERS // 2
-    first_core = core_ref[0, 0] == 0
-    mine, other = mine_ref[...], other_ref[...]
-    upper, lower = jnp.where(first_core, mine, other), jnp.where(first_core, other, mine)
-    cross = jnp.concatenate([unfold(upper[8:], half), unfold(lower[8:], half)], axis=0)
-    gram = jnp.concatenate(
-        [
-            jnp.concatenate([unfold(upper[:8], half), cross], axis=1),
-            jnp.concatenate([cross.T, unfold(lower[:8], half)], axis=1),
-        ],
-        axis=0,
-    )
+    gram_ref[...] = jnp.concatenate([fold(gram), total_ref[:4]], axis=0)
+
+
+def spread_kernel(gram_ref, o_ref):
+    scaled = gram_ref[:GRAM_ROWS] / gram_ref[GRAM_ROWS : GRAM_ROWS + 1]
+    for i in range(o_ref.shape[1]):
+        piece = scaled[4 * i : 4 * i + 4]
+        o_ref[:, i] = jnp.broadcast_to(piece[None], (o_ref.shape[0], *piece.shape))
+
+
+def final_kernel(gram_ref, mixing_ref, turned_ref, prior_ref, posterior_ref):
+    pieces = [jnp.sum(gram_ref[:, i], axis=0) for i in range(gram_ref.shape[1])]
+    gram = unfold(jnp.concatenate(pieces[:4], axis=0), pieces[4])
     prior_ref[...] = gram
     dot = functools.partial(jnp.dot, precision=HIGHEST, preferred_element_type=jnp.float32)
     posterior_ref[...] = dot(dot(turned_ref[...], gram), mixing_ref[...])
@@ -157,14 +154,17 @@
     quantities = obs_operator.shape[0]
     halves = LANES * mem // cells
     depth = variables // halves
-    core = lax.axis_index("space_1").astype(jnp.int32).reshape(1, 1)
     place = lax.axis_index("mem").astype(jnp.int32).reshape(1, 1)
     state_bytes = 2 * ensemble.size
     square = vmem((MEMBERS, MEMBERS), jnp.float32)
 
+    step = PACK_TILES * LANES
     blocks = kernel(
-        pack_kernel, vmem((mem, depth, local, LANES), jnp.bfloat16), [VMEM],
-        state_bytes, 2 * state_bytes,
+        pack_kernel, vmem((mem, depth, local, LANES), jnp.bfloat16),
+        [pl.BlockSpec((variables, local, step), lambda i: (0, 0, i))],
+        state_bytes, 2 * state_bytes, grid=(cells // step,),
+        out_specs=pl.BlockSpec((2 * PACK_TILES, depth, local, LANES), lambda i: (i, 0, 0, 0)),
+        compiler_params=pltpu.CompilerParams(),
     )(ensemble.transpose(1, 0, 2))
     members = exchange(blocks, "mem")
 
@@ -182,21 +182,20 @@
     mixed = mixed.reshape(depth, mem, local, LANES).transpose(1, 0, 2, 3)
     mixed = exchange(mixed, "mem")
 
-    mine, other = kernel(
-        gram_kernel, (vmem((16, LANES), jnp.float32),) * 2,
-        [SMEM, VMEM, VMEM, VMEM, VMEM], 4 * depth * quantities * MEMBERS * LANES, state_bytes,
+    gram = kernel(
+        gram_kernel, vmem((GRAM_ROWS + 4, LANES), jnp.float32), [VMEM] * 4,
+        4 * depth * quantities * MEMBERS * LANES, state_bytes,
         [pltpu.VMEM((MEMBERS, quantities // halves * LANES), jnp.float32)] * 2,
-    )(core, members, factor, pairs, total)
-    mine = mine + to_partner(other)
-    mine = lax.psum(mine, "space_0")
-    mine = (mine[:12] / mine[12:13]).reshape(3, 4, LANES)
-    mine = exchange(jnp.broadcast_to(mine[None], (mem, *mine.shape)), "mem")
-    mine = jnp.sum(mine, axis=0).reshape(12, LANES)
-    other = to_partner(mine)
+    )(members, factor, pairs, total)
+    gram = lax.psum(lax.psum(gram, "space_1"), "space_0")
+    gram = kernel(
+        spread_kernel, vmem((mem, GRAM_ROWS // 4, 4, LANES), jnp.float32),
+        [VMEM], GRAM_ROWS * LANES, 4 * mem * GRAM_ROWS * LANES,
+    )(gram)
+    gram = exchange(gram, "mem")
     prior_gram, posterior_gram = kernel(
-        final_kernel, (square, square), [SMEM, VMEM, VMEM, VMEM, VMEM],
-        4 * MEMBERS**3, 16 * MEMBERS**2,
-    )(core, mine, other, mixing, turned)
+        final_kernel, (square, square), [VMEM] * 3, 4 * MEMBERS**3, 16 * MEMBERS**2
+    )(gram, mixing, turned)
 
     analysis = kernel(
         unpack_kernel, vmem((variables, local, cells), jnp.bfloat16), [VMEM],

time: 154 us -> 165 us (1.071)
  blocking collectives: 18.2 us -> 34 us
  starting transfers between devices: 59.1 us -> 56 us
  Pallas kernels: 6.66 us -> 9.5 us
  waiting for transfers between devices: 64.8 us -> 62.2 us
  local copies, waits for them, and re-layouts: 3.03 us -> 1.32 us
    psum x1 -> x2, blocking collectives: 18.2 us -> 34 us  [per_device(): gram = lax.psum(lax.psum(gram, 'space_1'), 'space_0')]
    ppermute x2 -> x0, starting transfers between devices: 3.9 us -> none  [to_partner(): return lax.ppermute(array, 'space_1', [(0, 1), (1, 0)])]
    pallas_call x3 -> x4, Pallas kernels: 4.93 us -> 7.78 us  [the longest x1 3.6 us: per_device(): kernel(pack_kernel, vmem((mem, depth, local, LANES), jnp.bfloat16), [pl.B...]
    ppermute x2 -> x0, waiting for transfers between devices: 2.01 us -> none  [to_partner(): return lax.ppermute(array, 'space_1', [(0, 1), (1, 0)])]
  transfers between devices with their start and end apart: 5 -> 3, of which waited for: 5 -> 3; matrix products, arithmetic and copies ran while one was open for 1% -> 1% of each run, Pallas kernels for 1% -> 1%
where the time goes in v4:
time: 165 us; the launch traced here: 164 us
  waiting for transfers between devices  62.2 us (38%)
  starting transfers between devices  56 us (34%)
  blocking collectives  34 us (21%)
  Pallas kernels  9.5 us (6%)
    all_to_all x3, waiting for transfers between devices, exchange(): return lax.all_to_all(array, axis, split_axis=0, concat_axis=0, tiled=True)  62.2 us
    all_to_all x3, starting transfers between devices, exchange(): return lax.all_to_all(array, axis, split_axis=0, concat_axis=0, tiled=True)  56 us
    psum x2, blocking collectives, per_device(): gram = lax.psum(lax.psum(gram, 'space_1'), 'space_0')  34 us
    pallas_call x1, Pallas kernels, per_device(): kernel(pack_kernel, vmem((mem, depth, local, LANES), jnp.bfloat16), [pl.B...  3.6 us
  transfers between devices with their start and end apart: 3, of which 3 were waited for; matrix products, arithmetic and copies ran while one was open for 1% of the time, Pallas kernels for 1%

profile of v4, /device:TPU:80, one launch (start us, length us, event | category | flops | bytes accessed | tf_op | source)
XLA Modules:
  0.0 164.5 jit_solution(15091826186723237275)
XLA Ops:
  0.6 3.6 %shard_map.67 = bf16[16,35,4,128]{3,2,1,0:T(4,128)(2,1)} custom-call(bf16[70,4,1024]{2,1,0:T(4,128)(2,1)} %bitcast.24), custom_call_target="tpu_custom_call" | custom-call | flops 573440 | bytes 1146880 | tf_op jit(solution)/shard_map/pallas_call | solution.py:162
  4.2 0.0 copy-start
  4.2 0.0 copy-start.1
  4.2 0.0 copy-start.2
  4.2 43.8 %all-to-all-start = ((bf16[16,35,4,128]{3,2,1,0:T(4,128)(2,1)}), bf16[16,35,4,128]{3,2,1,0:T(4,128)(2,1)S(1)}, u32[]{:S(2)}, u32[]{:S(2)}) async-start(bf16[16,35,4,128]{3,2,1,0:T(4,128)(2,1)} %shard_map.67), calls=%async_computation | async-start | bytes 1146880 | tf_op jit(solution)/shard_map/all_to_all | solution.py:27
  48.1 0.0 copy-done
  48.1 0.0 copy-done.1
  48.1 0.0 copy-done.2
  48.1 0.3 shard_map.68
  48.4 29.9 %all-to-all-done = bf16[16,35,4,128]{3,2,1,0:T(4,128)(2,1)S(1)} async-done(((bf16[16,35,4,128]{3,2,1,0:T(4,128)(2,1)}), bf16[16,35,4,128]{3,2,1,0:T(4,128)(2,1)S(1)}, u32[]{:S(2)}, u32[]{:S(2)}) %all-to-all-start) | async-done | bytes 573472 | tf_op jit(solution)/shard_map/all_to_all | solution.py:27
  78.2 0.3 copy.8
  78.5 2.3 %shard_map.70 = f32[24,128]{1,0:T(8,128)S(1)} custom-call(bf16[35,64,128]{2,1,0:T(8,128)(2,1)S(1)} %bitcast.20, f32[35,16,128]{2,1,0:T(8,128)S(1)} %get-tuple-element.11.factor_ref, f32[8,128]{1,0:T(8,128)S(1)} %get-tuple-element.12.weight_ref, f32[8,128]{1,0:T(8,128)S(1)} %get-tuple-element.13.total_ref), custom_call_target="tpu_custom_call" | custom-call | flops 18350080 | bytes 573440 | tf_op jit(solution)/shard_map/pallas_call | solution.py:185
  80.9 3.3 %psum.14 = f32[24,128]{1,0:T(8,128)S(1)} all-reduce(f32[24,128]{1,0:T(8,128)S(1)} %shard_map.70), channel_id=1, replica_groups=mesh['parts'=2,'mem'=16,'space_0'=8,'space_1'=2] {'space_1'}, use_global_device_ids=true, to_apply=%region_2.0 | all-reduce | flops 3072 | bytes 24576 | tf_op jit(solution)/shard_map/psum | solution.py:190
  84.2 30.7 %psum.15.gram_ref = f32[24,128]{1,0:T(8,128)S(1)} all-reduce(f32[24,128]{1,0:T(8,128)S(1)} %psum.14), channel_id=1, replica_groups=mesh['parts'=2,'mem'=16,'space_0'=8,'space_1'=2] {'space_0'}, use_global_device_ids=true, to_apply=%region_3.0 | all-reduce | flops 3072 | bytes 24576 | tf_op jit(solution)/shard_map/psum | solution.py:190
  114.9 0.7 shard_map.71
  115.6 7.4 %all-to-all-start.2 = ((f32[16,5,4,128]{3,2,1,0:T(4,128)}), f32[16,5,4,128]{3,2,1,0:T(4,128)S(1)}, u32[]{:S(2)}, u32[]{:S(2)}) async-start(f32[16,5,4,128]{3,2,1,0:T(4,128)} %shard_map.71), calls=%async_computation.2 | async-start | bytes 327680 | tf_op jit(solution)/shard_map/all_to_all | solution.py:27
  123.0 0.3 convert_reduce_fusion
  123.3 0.4 fusion.1
  123.6 1.0 copy.11
  124.7 11.5 %all-to-all-done.2.gram_ref = f32[16,5,4,128]{3,2,1,0:T(4,128)S(1)} async-done(((f32[16,5,4,128]{3,2,1,0:T(4,128)}), f32[16,5,4,128]{3,2,1,0:T(4,128)S(1)}, u32[]{:S(2)}, u32[]{:S(2)}) %all-to-all-start.2) | async-done | bytes 163872 | tf_op jit(solution)/shard_map/all_to_all | solution.py:27
  136.1 4.8 %all-to-all-start.1 = ((bf16[16,35,4,128]{3,2,1,0:T(4,128)(2,1)}), bf16[16,35,4,128]{3,2,1,0:T(4,128)(2,1)S(1)}, u32[]{:S(2)}, u32[]{:S(2)}) async-start(bf16[16,35,4,128]{3,2,1,0:T(4,128)(2,1)} %bitcast.19), calls=%async_computation.1 | async-start | bytes 1146880 | tf_op jit(solution)/shard_map/all_to_all | solution.py:27
  141.0 1.2 shard_map.72
  142.2 20.9 %all-to-all-done.1.x_ref = bf16[16,35,4,128]{3,2,1,0:T(4,128)(2,1)S(1)} async-done(((bf16[16,35,4,128]{3,2,1,0:T(4,128)(2,1)}), bf16[16,35,4,128]{3,2,1,0:T(4,128)(2,1)S(1)}, u32[]{:S(2)}, u32[]{:S(2)}) %all-to-all-start.1) | async-done | bytes 573472 | tf_op jit(solution)/shard_map/all_to_all | solution.py:27
  163.0 1.5 shard_map.69
  (3 shorter events, 0.0 us)
Async XLA Ops:
  4.2 43.8 %copy-start = (bf16[64,64]{1,0:T(8,128)(2,1)S(1)}, bf16[64,64]{1,0:T(8,128)(2,1)}, u32[]{:S(2)}) copy-start(bf16[64,64]{1,0:T(8,128)(2,1)} %transform_ref.1) | copy-start | bytes 24580
  4.2 43.8 %copy-start.1 = (f32[16,1024]{1,0:T(8,128)S(1)}, f32[16,1024]{1,0:T(8,128)}, u32[]{:S(2)}) copy-start(f32[16,1024]{1,0:T(8,128)} %weight_ref.1) | copy-start | bytes 196612
  4.2 43.9 %copy-start.2 = (bf16[16,70]{1,0:T(8,128)(2,1)S(1)}, bf16[16,70]{1,0:T(8,128)(2,1)}, u32[]{:S(2)}) copy-start(bf16[16,70]{1,0:T(8,128)(2,1)} %operator_ref.1) | copy-start | bytes 6724
  4.2 74.0 %all-to-all-start = ((bf16[16,35,4,128]{3,2,1,0:T(4,128)(2,1)}), bf16[16,35,4,128]{3,2,1,0:T(4,128)(2,1)S(1)}, u32[]{:S(2)}, u32[]{:S(2)}) async-start(bf16[16,35,4,128]{3,2,1,0:T(4,128)(2,1)} %shard_map.67), calls=%async_computation | async-start | bytes 1146880 | tf_op jit(solution)/shard_map/all_to_all | solution.py:27
  115.6 20.6 %all-to-all-start.2 = ((f32[16,5,4,128]{3,2,1,0:T(4,128)}), f32[16,5,4,128]{3,2,1,0:T(4,128)S(1)}, u32[]{:S(2)}, u32[]{:S(2)}) async-start(f32[16,5,4,128]{3,2,1,0:T(4,128)} %shard_map.71), calls=%async_computation.2 | async-start | bytes 327680 | tf_op jit(solution)/shard_map/all_to_all | solution.py:27
  136.1 26.9 %all-to-all-start.1 = ((bf16[16,35,4,128]{3,2,1,0:T(4,128)(2,1)}), bf16[16,35,4,128]{3,2,1,0:T(4,128)(2,1)S(1)}, u32[]{:S(2)}, u32[]{:S(2)}) async-start(bf16[16,35,4,128]{3,2,1,0:T(4,128)(2,1)} %bitcast.19), calls=%async_computation.1 | async-start | bytes 1146880 | tf_op jit(solution)/shard_map/all_to_all | solution.py:27

commit v5 on v4

--- a/solution.py
+++ b/solution.py
@@ -13,18 +13,22 @@
 LANES = 128
 GROUP = 4
 BLOCK = 16
-PACK_TILES = 2
-GRAM_ROWS = 20
+PACK_STEPS = 2
 VMEM_LIMIT = 12 << 20
 HIGHEST = lax.Precision.HIGHEST
 
 
 SMEM = pl.BlockSpec(memory_space=pltpu.SMEM)
 VMEM = pl.BlockSpec(memory_space=pltpu.VMEM)
+ANY = pl.BlockSpec(memory_space=pl.ANY)
 
 
 def exchange(array, axis):
     return lax.all_to_all(array, axis, split_axis=0, concat_axis=0, tiled=True)
+
+
+def to_partner(array):
+    return lax.ppermute(array, "space_1", [(0, 1), (1, 0)])
 
 
 def vmem(shape, dtype):
@@ -41,13 +45,33 @@
     )
 
 
-def pack_kernel(x_ref, o_ref):
+def pack_kernel(x_ref, o_ref, x, o, in_sems, out_sems):
     depth, half = o_ref.shape[1], LANES // 2
-    for tile in range(x_ref.shape[2] // LANES):
-        at = slice(tile * LANES, (tile + 1) * LANES)
-        low, high = x_ref[:depth, :, at], x_ref[depth:, :, at]
-        o_ref[2 * tile] = jnp.concatenate([low[..., :half], high[..., :half]], axis=-1)
-        o_ref[2 * tile + 1] = jnp.concatenate([low[..., half:], high[..., half:]], axis=-1)
+    cuts = [depth * i // PACK_STEPS for i in range(PACK_STEPS + 1)]
+    steps = [slice(a, b) for a, b in zip(cuts[:-1], cuts[1:], strict=True)]
+    shifted = [slice(depth + s.start, depth + s.stop) for s in steps]
+    reads = [
+        [pltpu.make_async_copy(x_ref.at[s], x.at[s], in_sems.at[i, j]) for j, s in enumerate(both)]
+        for i, both in enumerate(zip(steps, shifted, strict=True))
+    ]
+    writes = [
+        pltpu.make_async_copy(o.at[:, s], o_ref.at[:, s], out_sems.at[i])
+        for i, s in enumerate(steps)
+    ]
+    for read in reads:
+        read[0].start()
+        read[1].start()
+    for read, write, near, far in zip(reads, writes, steps, shifted, strict=True):
+        read[0].wait()
+        read[1].wait()
+        for tile in range(x.shape[2] // LANES):
+            at = slice(tile * LANES, (tile + 1) * LANES)
+            low, high = x[near, :, at], x[far, :, at]
+            o[2 * tile, near] = jnp.concatenate([low[..., :half], high[..., :half]], axis=-1)
+            o[2 * tile + 1, near] = jnp.concatenate([low[..., half:], high[..., half:]], axis=-1)
+        write.start()
+    for write in writes:
+        write.wait()
 
 
 def unpack_kernel(x_ref, o_ref):
@@ -63,7 +87,7 @@
     rows = [gram[at : at + BLOCK, at:] for at in range(0, MEMBERS, BLOCK)]
     first = jnp.concatenate([rows[0], rows[1], rows[3]], axis=1)
     rest = jnp.concatenate([rows[2][i : i + 4] for i in range(0, BLOCK, 4)], axis=1)
-    return jnp.concatenate([first, rest], axis=0)
+    return first, rest
 
 
 def unfold(first, rest):
@@ -106,7 +130,7 @@
     turned_ref[...] = mixing.T
 
 
-def gram_kernel(x_ref, factor_ref, weight_ref, total_ref, gram_ref, lhs, rhs):
+def gram_kernel(core_ref, x_ref, factor_ref, weight_ref, total_ref, mine_ref, other_ref, lhs, rhs):
     depth, quantities = factor_ref.shape[:2]
     low = lax.broadcasted_iota(jnp.int32, (MEMBERS, LANES), 1) < LANES // 2
     zero = jnp.zeros((MEMBERS, LANES), jnp.float32)
@@ -131,14 +155,26 @@
         lhs[...], rhs[...], (((1,), (1,)), ((), ())), precision=HIGHEST,
         preferred_element_type=jnp.float32,
     )
-    gram_ref[...] = jnp.concatenate([fold(gram), total_ref[:4]], axis=0)
-
-
-def spread_kernel(gram_ref, o_ref):
-    scaled = gram_ref[:GRAM_ROWS] / gram_ref[GRAM_ROWS : GRAM_ROWS + 1]
-    for i in range(o_ref.shape[1]):
-        piece = scaled[4 * i : 4 * i + 4]
-        o_ref[:, i] = jnp.broadcast_to(piece[None], (o_ref.shape[0], *piece.shape))
+    first, rest = fold(gram)
+    halves = [
+        (first[8 * i : 8 * i + 4], first[8 * i + 4 : 8 * i + 8],
+         jnp.concatenate([rest[2 * i : 2 * i + 2], total_ref[:2]], axis=0))
+        for i in range(2)
+    ]
+    first_core = core_ref[0, 0] == 0
+    for i, (upper, lower) in enumerate(zip(*halves, strict=True)):
+        mine_ref[i] = jnp.where(first_core, upper, lower)
+        other_ref[i] = jnp.where(first_core, lower, upper)
+
+
+def spread_kernel(core_ref, mine_ref, other_ref, o_ref):
+    first_core = core_ref[0, 0] == 0
+    mine, other = mine_ref[...], other_ref[...]
+    total = mine[2, 2:3]
+    upper, lower = jnp.where(first_core, mine, other), jnp.where(first_core, other, mine)
+    rest = jnp.concatenate([upper[2, :2], lower[2, :2]], axis=0)
+    for i, piece in enumerate((upper[0], upper[1], lower[0], lower[1], rest)):
+        o_ref[:, i] = jnp.broadcast_to((piece / total)[None], (o_ref.shape[0], *piece.shape))
 
 
 def final_kernel(gram_ref, mixing_ref, turned_ref, prior_ref, posterior_ref):
@@ -154,17 +190,20 @@
     quantities = obs_operator.shape[0]
     halves = LANES * mem // cells
     depth = variables // halves
+    core = lax.axis_index("space_1").astype(jnp.int32).reshape(1, 1)
     place = lax.axis_index("mem").astype(jnp.int32).reshape(1, 1)
     state_bytes = 2 * ensemble.size
     square = vmem((MEMBERS, MEMBERS), jnp.float32)
 
-    step = PACK_TILES * LANES
+    block_shape, state_shape = (mem, depth, local, LANES), (variables, local, cells)
     blocks = kernel(
-        pack_kernel, vmem((mem, depth, local, LANES), jnp.bfloat16),
-        [pl.BlockSpec((variables, local, step), lambda i: (0, 0, i))],
-        state_bytes, 2 * state_bytes, grid=(cells // step,),
-        out_specs=pl.BlockSpec((2 * PACK_TILES, depth, local, LANES), lambda i: (i, 0, 0, 0)),
-        compiler_params=pltpu.CompilerParams(),
+        pack_kernel, vmem(block_shape, jnp.bfloat16), [ANY],
+        state_bytes, 2 * state_bytes,
+        [
+            pltpu.VMEM(state_shape, jnp.bfloat16), pltpu.VMEM(block_shape, jnp.bfloat16),
+            pltpu.SemaphoreType.DMA((PACK_STEPS, 2)), pltpu.SemaphoreType.DMA((PACK_STEPS,)),
+        ],
+        out_specs=ANY, compiler_params=pltpu.CompilerParams(),
     )(ensemble.transpose(1, 0, 2))
     members = exchange(blocks, "mem")
 
@@ -182,16 +221,18 @@
     mixed = mixed.reshape(depth, mem, local, LANES).transpose(1, 0, 2, 3)
     mixed = exchange(mixed, "mem")
 
-    gram = kernel(
-        gram_kernel, vmem((GRAM_ROWS + 4, LANES), jnp.float32), [VMEM] * 4,
+    half = (3, 4, LANES)
+    mine, other = kernel(
+        gram_kernel, (vmem(half, jnp.float32),) * 2, [SMEM, *[VMEM] * 4],
         4 * depth * quantities * MEMBERS * LANES, state_bytes,
         [pltpu.VMEM((MEMBERS, quantities // halves * LANES), jnp.float32)] * 2,
-    )(members, factor, pairs, total)
-    gram = lax.psum(lax.psum(gram, "space_1"), "space_0")
+    )(core, members, factor, pairs, total)
+    mine = lax.psum(mine + to_partner(other), "space_0")
+    other = to_partner(mine)
     gram = kernel(
-        spread_kernel, vmem((mem, GRAM_ROWS // 4, 4, LANES), jnp.float32),
-        [VMEM], GRAM_ROWS * LANES, 4 * mem * GRAM_ROWS * LANES,
-    )(gram)
+        spread_kernel, vmem((mem, 5, 4, LANES), jnp.float32),
+        [SMEM, VMEM, VMEM], MEMBERS**2, 4 * mem * MEMBERS**2,
+    )(core, mine, other)
     gram = exchange(gram, "mem")
     prior_gram, posterior_gram = kernel(
         final_kernel, (square, square), [VMEM] * 3, 4 * MEMBERS**3, 16 * MEMBERS**2

time: 165 us -> 165 us (level)
  blocking collectives: 34 us -> 18.2 us
  waiting for transfers between devices: 62.2 us -> 74.4 us
  starting transfers between devices: 56 us -> 60.4 us
    psum x2 -> x1, blocking collectives: 34 us -> 18.2 us  [per_device(): mine = lax.psum(mine + to_partner(other), 'space_0')]
    all_to_all x3, waiting for transfers between devices: 62.2 us -> 72.2 us  [exchange(): return lax.all_to_all(array, axis, split_axis=0, concat_axis=0, tiled=True)]
    ppermute x0 -> x2, starting transfers between devices: none -> 3.9 us  [to_partner(): return lax.ppermute(array, 'space_1', [(0, 1), (1, 0)])]
    ppermute x0 -> x2, waiting for transfers between devices: none -> 2.23 us  [to_partner(): return lax.ppermute(array, 'space_1', [(0, 1), (1, 0)])]
  transfers between devices with their start and end apart: 3 -> 5, of which waited for: 3 -> 5; matrix products, arithmetic and copies ran while one was open for 1% -> 1% of each run, Pallas kernels for 1% -> 1%
where the time goes in v5:
time: 165 us; the launch traced here: 164 us
  waiting for transfers between devices  74.4 us (45%)
  starting transfers between devices  60.4 us (37%)
  blocking collectives  18.2 us (11%)
  Pallas kernels  8.4 us (5%)
    all_to_all x3, waiting for transfers between devices, exchange(): return lax.all_to_all(array, axis, split_axis=0, concat_axis=0, tiled=True)  72.2 us
    all_to_all x3, starting transfers between devices, exchange(): return lax.all_to_all(array, axis, split_axis=0, concat_axis=0, tiled=True)  56.5 us
    psum x1, blocking collectives, per_device(): mine = lax.psum(mine + to_partner(other), 'space_0')  18.2 us
    ppermute x2, starting transfers between devices, to_partner(): return lax.ppermute(array, 'space_1', [(0, 1), (1, 0)])  3.9 us
  transfers between devices with their start and end apart: 5, of which 5 were waited for; matrix products, arithmetic and copies ran while one was open for 1% of the time, Pallas kernels for 1%

profile of v5, /device:TPU:80, one launch (start us, length us, event | category | flops | bytes accessed | tf_op | source)
XLA Modules:
  0.0 164.3 jit_solution(900988957775106532)
XLA Ops:
  0.6 2.5 %shard_map.67 = bf16[16,35,4,128]{3,2,1,0:T(4,128)(2,1)} custom-call(bf16[70,4,1024]{2,1,0:T(4,128)(2,1)} %bitcast.25), custom_call_target="tpu_custom_call" | custom-call | flops 573440 | bytes 1146880 | tf_op jit(solution)/shard_map/pallas_call | solution.py:199
  3.1 0.0 copy-start
  3.1 0.0 copy-start.1
  3.1 0.0 copy-start.2
  3.1 43.8 %all-to-all-start = ((bf16[16,35,4,128]{3,2,1,0:T(4,128)(2,1)}), bf16[16,35,4,128]{3,2,1,0:T(4,128)(2,1)S(1)}, u32[]{:S(2)}, u32[]{:S(2)}) async-start(bf16[16,35,4,128]{3,2,1,0:T(4,128)(2,1)} %shard_map.67), calls=%async_computation | async-start | bytes 1146880 | tf_op jit(solution)/shard_map/all_to_all | solution.py:27
  47.0 0.3 shard_map.68
  47.3 29.9 %all-to-all-done = bf16[16,35,4,128]{3,2,1,0:T(4,128)(2,1)S(1)} async-done(((bf16[16,35,4,128]{3,2,1,0:T(4,128)(2,1)}), bf16[16,35,4,128]{3,2,1,0:T(4,128)(2,1)S(1)}, u32[]{:S(2)}, u32[]{:S(2)}) %all-to-all-start) | async-done | bytes 573472 | tf_op jit(solution)/shard_map/all_to_all | solution.py:27
  77.2 0.3 copy.8
  77.5 2.3 %shard_map.70 = (f32[3,4,128]{2,1,0:T(4,128)S(1)}, f32[3,4,128]{2,1,0:T(4,128)S(1)}) custom-call(s32[1,1]{1,0:T(1,128)} %bitcast.9.core_ref, bf16[35,64,128]{2,1,0:T(8,128)(2,1)S(1)} %bitcast.21, f32[35,16,128]{2,1,0:T(8,128)S(1)} %get-tuple-element.13.factor_ref, f32[8,128]{1,0:T(8,128)S(1)} %get-tuple-element.14.weight_ref, ...), custom_call_target="tpu_custom_call" | custom-call | flops 18350080 | bytes 573440 | tf_op jit(solution)/shard_map/pallas_call | solution.py:225
  79.8 2.0 %collective-permute-start = (f32[3,4,128]{2,1,0:T(4,128)S(1)}, f32[3,4,128]{2,1,0:T(4,128)S(1)}, u32[]{:S(2)}, u32[]{:S(2)}) collective-permute-start(f32[3,4,128]{2,1,0:T(4,128)S(1)} %get-tuple-element.17), channel_id=1, source_target_pairs={{0,1},{1,0},{2,3},{3,2},{4,5},{5,4},{6,7},{7,6},{8,9},{9,8},{10,11... | collective-permute-start | bytes 18440 | tf_op jit(solution)/shard_map/ppermute | solution.py:31
  81.8 1.1 collective-permute-done
  82.9 18.2 %psum.7.mine_ref = f32[3,4,128]{2,1,0:T(4,128)S(1)} all-reduce(f32[3,4,128]{2,1,0:T(4,128)S(1)} %add.9), channel_id=1, replica_groups=mesh['parts'=2,'mem'=16,'space_0'=8,'space_1'=2] {'space_0'}, use_global_device_ids=true, to_apply=%region_2.0 | all-reduce | flops 1536 | bytes 12288 | tf_op jit(solution)/shard_map/psum | solution.py:230
  101.1 2.0 %collective-permute-start.1 = (f32[3,4,128]{2,1,0:T(4,128)S(1)}, f32[3,4,128]{2,1,0:T(4,128)S(1)}, u32[]{:S(2)}, u32[]{:S(2)}) collective-permute-start(f32[3,4,128]{2,1,0:T(4,128)S(1)} %psum.7.mine_ref), channel_id=1, source_target_pairs={{0,1},{1,0},{2,3},{3,2},{4,5},{5,4},{6,7},{7,6},{8,9},{9,8},{10,11... | collective-permute-start | bytes 18440 | tf_op jit(solution)/shard_map/ppermute | solution.py:31
  103.1 1.1 collective-permute-done.1.other_ref
  104.2 0.7 shard_map.71
  104.9 7.4 %all-to-all-start.2 = ((f32[16,5,4,128]{3,2,1,0:T(4,128)}), f32[16,5,4,128]{3,2,1,0:T(4,128)S(1)}, u32[]{:S(2)}, u32[]{:S(2)}) async-start(f32[16,5,4,128]{3,2,1,0:T(4,128)} %shard_map.71), calls=%async_computation.2 | async-start | bytes 327680 | tf_op jit(solution)/shard_map/all_to_all | solution.py:27
  112.3 0.3 convert_reduce_fusion
  112.6 0.4 fusion.1
  113.0 1.0 copy.11
  114.0 13.3 %all-to-all-done.2.gram_ref = f32[16,5,4,128]{3,2,1,0:T(4,128)S(1)} async-done(((f32[16,5,4,128]{3,2,1,0:T(4,128)}), f32[16,5,4,128]{3,2,1,0:T(4,128)S(1)}, u32[]{:S(2)}, u32[]{:S(2)}) %all-to-all-start.2) | async-done | bytes 163872 | tf_op jit(solution)/shard_map/all_to_all | solution.py:27
  127.3 5.3 %all-to-all-start.1 = ((bf16[16,35,4,128]{3,2,1,0:T(4,128)(2,1)}), bf16[16,35,4,128]{3,2,1,0:T(4,128)(2,1)S(1)}, u32[]{:S(2)}, u32[]{:S(2)}) async-start(bf16[16,35,4,128]{3,2,1,0:T(4,128)(2,1)} %bitcast.20), calls=%async_computation.1 | async-start | bytes 1146880 | tf_op jit(solution)/shard_map/all_to_all | solution.py:27
  132.6 1.2 shard_map.72
  133.8 29.0 %all-to-all-done.1.x_ref = bf16[16,35,4,128]{3,2,1,0:T(4,128)(2,1)S(1)} async-done(((bf16[16,35,4,128]{3,2,1,0:T(4,128)(2,1)}), bf16[16,35,4,128]{3,2,1,0:T(4,128)(2,1)S(1)}, u32[]{:S(2)}, u32[]{:S(2)}) %all-to-all-start.1) | async-done | bytes 573472 | tf_op jit(solution)/shard_map/all_to_all | solution.py:27
  162.8 1.5 shard_map.69
  (7 shorter events, 0.0 us)
Async XLA Ops:
  3.1 43.9 %copy-start = (bf16[64,64]{1,0:T(8,128)(2,1)S(1)}, bf16[64,64]{1,0:T(8,128)(2,1)}, u32[]{:S(2)}) copy-start(bf16[64,64]{1,0:T(8,128)(2,1)} %transform_ref.1) | copy-start | bytes 24580
  3.1 43.9 %copy-start.1 = (f32[16,1024]{1,0:T(8,128)S(1)}, f32[16,1024]{1,0:T(8,128)}, u32[]{:S(2)}) copy-start(f32[16,1024]{1,0:T(8,128)} %weight_ref.1) | copy-start | bytes 196612
  3.1 43.9 %copy-start.2 = (bf16[16,70]{1,0:T(8,128)(2,1)S(1)}, bf16[16,70]{1,0:T(8,128)(2,1)}, u32[]{:S(2)}) copy-start(bf16[16,70]{1,0:T(8,128)(2,1)} %operator_ref.1) | copy-start | bytes 6724
  3.1 74.0 %all-to-all-start = ((bf16[16,35,4,128]{3,2,1,0:T(4,128)(2,1)}), bf16[16,35,4,128]{3,2,1,0:T(4,128)(2,1)S(1)}, u32[]{:S(2)}, u32[]{:S(2)}) async-start(bf16[16,35,4,128]{3,2,1,0:T(4,128)(2,1)} %shard_map.67), calls=%async_computation | async-start | bytes 1146880 | tf_op jit(solution)/shard_map/all_to_all | solution.py:27
  79.8 3.1 %collective-permute-start = (f32[3,4,128]{2,1,0:T(4,128)S(1)}, f32[3,4,128]{2,1,0:T(4,128)S(1)}, u32[]{:S(2)}, u32[]{:S(2)}) collective-permute-start(f32[3,4,128]{2,1,0:T(4,128)S(1)} %get-tuple-element.17), channel_id=1, source_target_pairs={{0,1},{1,0},{2,3},{3,2},{4,5},{5,4},{6,7},{7,6},{8,9},{9,8},{10,11... | collective-permute-start | bytes 18440 | tf_op jit(solution)/shard_map/ppermute | solution.py:31
  101.1 3.1 %collective-permute-start.1 = (f32[3,4,128]{2,1,0:T(4,128)S(1)}, f32[3,4,128]{2,1,0:T(4,128)S(1)}, u32[]{:S(2)}, u32[]{:S(2)}) collective-permute-start(f32[3,4,128]{2,1,0:T(4,128)S(1)} %psum.7.mine_ref), channel_id=1, source_target_pairs={{0,1},{1,0},{2,3},{3,2},{4,5},{5,4},{6,7},{7,6},{8,9},{9,8},{10,11... | collective-permute-start | bytes 18440 | tf_op jit(solution)/shard_map/ppermute | solution.py:31
  104.9 22.4 %all-to-all-start.2 = ((f32[16,5,4,128]{3,2,1,0:T(4,128)}), f32[16,5,4,128]{3,2,1,0:T(4,128)S(1)}, u32[]{:S(2)}, u32[]{:S(2)}) async-start(f32[16,5,4,128]{3,2,1,0:T(4,128)} %shard_map.71), calls=%async_computation.2 | async-start | bytes 327680 | tf_op jit(solution)/shard_map/all_to_all | solution.py:27
  127.3 35.5 %all-to-all-start.1 = ((bf16[16,35,4,128]{3,2,1,0:T(4,128)(2,1)}), bf16[16,35,4,128]{3,2,1,0:T(4,128)(2,1)S(1)}, u32[]{:S(2)}, u32[]{:S(2)}) async-start(bf16[16,35,4,128]{3,2,1,0:T(4,128)(2,1)} %bitcast.20), calls=%async_computation.1 | async-start | bytes 1146880 | tf_op jit(solution)/shard_map/all_to_all | solution.py:27

commit v6 on v5

--- a/solution.py
+++ b/solution.py
@@ -12,8 +12,8 @@
 MEMBERS = 64
 LANES = 128
 GROUP = 4
-BLOCK = 16
-PACK_STEPS = 2
+BLOCK = 4
+PACK_STEPS = 5
 VMEM_LIMIT = 12 << 20
 HIGHEST = lax.Precision.HIGHEST
 
@@ -23,8 +23,10 @@
 ANY = pl.BlockSpec(memory_space=pl.ANY)
 
 
-def exchange(array, axis):
-    return lax.all_to_all(array, axis, split_axis=0, concat_axis=0, tiled=True)
+def exchange(array, axis, groups=None):
+    return lax.all_to_all(
+        array, axis, split_axis=0, concat_axis=0, tiled=True, axis_index_groups=groups
+    )
 
 
 def to_partner(array):
@@ -83,25 +85,35 @@
         o_ref[depth:, :, at] = jnp.concatenate([left[..., half:], right[..., half:]], axis=-1)
 
 
+TILES = ((0, 1, 15), (2, 3, 11), (4, 5, 7), (6, 8, 9, 12, 13))
+REST = (10, 14)
+
+
 def fold(gram):
-    rows = [gram[at : at + BLOCK, at:] for at in range(0, MEMBERS, BLOCK)]
-    first = jnp.concatenate([rows[0], rows[1], rows[3]], axis=1)
-    rest = jnp.concatenate([rows[2][i : i + 4] for i in range(0, BLOCK, 4)], axis=1)
-    return first, rest
-
-
-def unfold(first, rest):
-    width = 2 * BLOCK
-    third = jnp.concatenate([rest[:, i : i + width] for i in range(0, LANES, width)], axis=0)
-    rows = [first[:, :64], first[:, 64:112], third, first[:, 112:]]
-    upper = jnp.concatenate(
-        [
-            jnp.concatenate([jnp.zeros((BLOCK, MEMBERS - r.shape[1]), jnp.float32), r], axis=1)
-            if r.shape[1] < MEMBERS else r
-            for r in rows
-        ],
-        axis=0,
-    )
+    def tile(rows):
+        at = [BLOCK * r for r in rows]
+        return jnp.concatenate([gram[a : a + BLOCK, a:] for a in at], axis=1)
+
+    rest = tile(REST)
+    row = jnp.concatenate([rest[i : i + 1] for i in range(BLOCK)], axis=1)
+    return [tile(rows) for rows in TILES], row
+
+
+def unfold(tiles, row):
+    width = LANES // BLOCK
+    rest = jnp.concatenate([row[:, i * width : (i + 1) * width] for i in range(BLOCK)], axis=0)
+    rows = {}
+    for members, tile in zip((*TILES, REST), (*tiles, rest), strict=True):
+        start = 0
+        for b in members:
+            wide = MEMBERS - BLOCK * b
+            piece = tile[:, start : start + wide]
+            if wide < MEMBERS:
+                blank = jnp.zeros((BLOCK, MEMBERS - wide), jnp.float32)
+                piece = jnp.concatenate([blank, piece], axis=1)
+            rows[b] = piece
+            start += wide
+    upper = jnp.concatenate([rows[b] for b in sorted(rows)], axis=0)
     row = lax.broadcasted_iota(jnp.int32, upper.shape, 0) // BLOCK
     column = lax.broadcasted_iota(jnp.int32, upper.shape, 1) // BLOCK
     return jnp.where(row <= column, upper, upper.T)
@@ -155,11 +167,10 @@
         lhs[...], rhs[...], (((1,), (1,)), ((), ())), precision=HIGHEST,
         preferred_element_type=jnp.float32,
     )
-    first, rest = fold(gram)
+    tiles, row = fold(gram)
     halves = [
-        (first[8 * i : 8 * i + 4], first[8 * i + 4 : 8 * i + 8],
-         jnp.concatenate([rest[2 * i : 2 * i + 2], total_ref[:2]], axis=0))
-        for i in range(2)
+        (*tiles[:2], total_ref[:4]),
+        (*tiles[2:], jnp.concatenate([total_ref[:2], row, row], axis=0)),
     ]
     first_core = core_ref[0, 0] == 0
     for i, (upper, lower) in enumerate(zip(*halves, strict=True)):
@@ -170,16 +181,21 @@
 def spread_kernel(core_ref, mine_ref, other_ref, o_ref):
     first_core = core_ref[0, 0] == 0
     mine, other = mine_ref[...], other_ref[...]
-    total = mine[2, 2:3]
+    total = mine[2, :1]
     upper, lower = jnp.where(first_core, mine, other), jnp.where(first_core, other, mine)
-    rest = jnp.concatenate([upper[2, :2], lower[2, :2]], axis=0)
-    for i, piece in enumerate((upper[0], upper[1], lower[0], lower[1], rest)):
-        o_ref[:, i] = jnp.broadcast_to((piece / total)[None], (o_ref.shape[0], *piece.shape))
+    tiles = (upper[0], upper[1], lower[0], lower[1], lower[2, 2:3])
+    rows = [(t / total)[i : i + 1] for t in tiles for i in range(t.shape[0])]
+    for i, row in enumerate(rows):
+        o_ref[:, i] = jnp.broadcast_to(row[None], (o_ref.shape[0], 1, LANES))
 
 
 def final_kernel(gram_ref, mixing_ref, turned_ref, prior_ref, posterior_ref):
-    pieces = [jnp.sum(gram_ref[:, i], axis=0) for i in range(gram_ref.shape[1])]
-    gram = unfold(jnp.concatenate(pieces[:4], axis=0), pieces[4])
+    rows = jnp.sum(gram_ref[...], axis=0)
+    tiles = [
+        jnp.concatenate([rows[BLOCK * i + k] for k in range(BLOCK)], axis=0)
+        for i in range(len(TILES))
+    ]
+    gram = unfold(tiles, rows[BLOCK * len(TILES)])
     prior_ref[...] = gram
     dot = functools.partial(jnp.dot, precision=HIGHEST, preferred_element_type=jnp.float32)
     posterior_ref[...] = dot(dot(turned_ref[...], gram), mixing_ref[...])
@@ -230,10 +246,11 @@
     mine = lax.psum(mine + to_partner(other), "space_0")
     other = to_partner(mine)
     gram = kernel(
-        spread_kernel, vmem((mem, 5, 4, LANES), jnp.float32),
+        spread_kernel, vmem((mem, 17, 1, LANES), jnp.float32),
         [SMEM, VMEM, VMEM], MEMBERS**2, 4 * mem * MEMBERS**2,
     )(core, mine, other)
-    gram = exchange(gram, "mem")
+    far_first = [i // 2 + i % 2 * (mem // 2) for i in range(mem)]
+    gram = exchange(gram, "mem", [far_first])
     prior_gram, posterior_gram = kernel(
         final_kernel, (square, square), [VMEM] * 3, 4 * MEMBERS**3, 16 * MEMBERS**2
     )(gram, mixing, turned)

time: 165 us -> 163 us (0.988)
  no operation moved by 1% of the time
where the time goes in v6:
time: 163 us
  waiting for transfers between devices  74.1 us (45%)
  starting transfers between devices  59.2 us (36%)
  blocking collectives  18.2 us (11%)
  Pallas kernels  8.57 us (5%)
    all_to_all x3, waiting for transfers between devices, exchange(): lax.all_to_all(array, axis, split_axis=0, concat_axis=0, tiled=True, axis...  71.8 us
    all_to_all x3, starting transfers between devices, exchange(): lax.all_to_all(array, axis, split_axis=0, concat_axis=0, tiled=True, axis...  55.2 us
    psum x1, blocking collectives, per_device(): mine = lax.psum(mine + to_partner(other), 'space_0')  18.2 us
    ppermute x2, starting transfers between devices, to_partner(): return lax.ppermute(array, 'space_1', [(0, 1), (1, 0)])  3.91 us
  transfers between devices with their start and end apart: 5, of which 5 were waited for; matrix products, arithmetic and copies ran while one was open for 1% of the time, Pallas kernels for 1%

profile of v6, /device:TPU:80, one launch (start us, length us, event | category | flops | bytes accessed | tf_op | source)
XLA Modules:
  0.0 162.8 jit_solution(5095999030106228017)
XLA Ops:
  0.6 2.6 %shard_map.67 = bf16[16,35,4,128]{3,2,1,0:T(4,128)(2,1)} custom-call(bf16[70,4,1024]{2,1,0:T(4,128)(2,1)} %bitcast.25), custom_call_target="tpu_custom_call" | custom-call | flops 573440 | bytes 1146880 | tf_op jit(solution)/shard_map/pallas_call | solution.py:215
  3.2 0.0 copy-start
  3.2 0.0 copy-start.1
  3.2 0.0 copy-start.2
  3.2 43.8 %all-to-all-start = ((bf16[16,35,4,128]{3,2,1,0:T(4,128)(2,1)}), bf16[16,35,4,128]{3,2,1,0:T(4,128)(2,1)S(1)}, u32[]{:S(2)}, u32[]{:S(2)}) async-start(bf16[16,35,4,128]{3,2,1,0:T(4,128)(2,1)} %shard_map.67), calls=%async_computation | async-start | bytes 1146880 | tf_op jit(solution)/shard_map/all_to_all | solution.py:27
  47.1 0.3 shard_map.68
  47.4 29.9 %all-to-all-done = bf16[16,35,4,128]{3,2,1,0:T(4,128)(2,1)S(1)} async-done(((bf16[16,35,4,128]{3,2,1,0:T(4,128)(2,1)}), bf16[16,35,4,128]{3,2,1,0:T(4,128)(2,1)S(1)}, u32[]{:S(2)}, u32[]{:S(2)}) %all-to-all-start) | async-done | bytes 573472 | tf_op jit(solution)/shard_map/all_to_all | solution.py:27
  77.3 0.3 copy.8
  77.6 2.4 %shard_map.70 = (f32[3,4,128]{2,1,0:T(4,128)S(1)}, f32[3,4,128]{2,1,0:T(4,128)S(1)}) custom-call(s32[1,1]{1,0:T(1,128)} %bitcast.9.core_ref, bf16[35,64,128]{2,1,0:T(8,128)(2,1)S(1)} %bitcast.21, f32[35,16,128]{2,1,0:T(8,128)S(1)} %get-tuple-element.13.factor_ref, f32[8,128]{1,0:T(8,128)S(1)} %get-tuple-element.14.weight_ref, ...), custom_call_target="tpu_custom_call" | custom-call | flops 18350080 | bytes 573440 | tf_op jit(solution)/shard_map/pallas_call | solution.py:241
  80.0 2.0 %collective-permute-start = (f32[3,4,128]{2,1,0:T(4,128)S(1)}, f32[3,4,128]{2,1,0:T(4,128)S(1)}, u32[]{:S(2)}, u32[]{:S(2)}) collective-permute-start(f32[3,4,128]{2,1,0:T(4,128)S(1)} %get-tuple-element.17), channel_id=1, source_target_pairs={{0,1},{1,0},{2,3},{3,2},{4,5},{5,4},{6,7},{7,6},{8,9},{9,8},{10,11... | collective-permute-start | bytes 18440 | tf_op jit(solution)/shard_map/ppermute | solution.py:33
  82.0 1.1 collective-permute-done
  83.1 18.2 %psum.7.mine_ref = f32[3,4,128]{2,1,0:T(4,128)S(1)} all-reduce(f32[3,4,128]{2,1,0:T(4,128)S(1)} %add.9), channel_id=1, replica_groups=mesh['parts'=2,'mem'=16,'space_0'=8,'space_1'=2] {'space_0'}, use_global_device_ids=true, to_apply=%region_2.0 | all-reduce | flops 1536 | bytes 12288 | tf_op jit(solution)/shard_map/psum | solution.py:246
  101.3 2.0 %collective-permute-start.1 = (f32[3,4,128]{2,1,0:T(4,128)S(1)}, f32[3,4,128]{2,1,0:T(4,128)S(1)}, u32[]{:S(2)}, u32[]{:S(2)}) collective-permute-start(f32[3,4,128]{2,1,0:T(4,128)S(1)} %psum.7.mine_ref), channel_id=1, source_target_pairs={{0,1},{1,0},{2,3},{3,2},{4,5},{5,4},{6,7},{7,6},{8,9},{9,8},{10,11... | collective-permute-start | bytes 18440 | tf_op jit(solution)/shard_map/ppermute | solution.py:33
  103.3 1.1 collective-permute-done.1.other_ref
  104.4 0.7 shard_map.71
  105.1 7.4 %all-to-all-start.2 = ((f32[16,17,1,128]{3,2,1,0:T(1,128)}), f32[16,17,1,128]{3,2,1,0:T(1,128)S(1)}, u32[]{:S(2)}, u32[]{:S(2)}) async-start(f32[16,17,1,128]{3,2,1,0:T(1,128)} %shard_map.71), calls=%async_computation.2 | async-start | bytes 278528 | tf_op jit(solution)/shard_map/all_to_all | solution.py:27
  112.5 0.3 convert_reduce_fusion
  112.8 0.4 fusion.1
  113.2 1.0 copy.11
  114.2 14.1 %all-to-all-done.2.gram_ref = f32[16,17,1,128]{3,2,1,0:T(1,128)S(1)} async-done(((f32[16,17,1,128]{3,2,1,0:T(1,128)}), f32[16,17,1,128]{3,2,1,0:T(1,128)S(1)}, u32[]{:S(2)}, u32[]{:S(2)}) %all-to-all-start.2) | async-done | bytes 139296 | tf_op jit(solution)/shard_map/all_to_all | solution.py:27
  128.2 4.0 %all-to-all-start.1 = ((bf16[16,35,4,128]{3,2,1,0:T(4,128)(2,1)}), bf16[16,35,4,128]{3,2,1,0:T(4,128)(2,1)S(1)}, u32[]{:S(2)}, u32[]{:S(2)}) async-start(bf16[16,35,4,128]{3,2,1,0:T(4,128)(2,1)} %bitcast.20), calls=%async_computation.1 | async-start | bytes 1146880 | tf_op jit(solution)/shard_map/all_to_all | solution.py:27
  132.3 1.2 shard_map.72
  133.5 27.9 %all-to-all-done.1.x_ref = bf16[16,35,4,128]{3,2,1,0:T(4,128)(2,1)S(1)} async-done(((bf16[16,35,4,128]{3,2,1,0:T(4,128)(2,1)}), bf16[16,35,4,128]{3,2,1,0:T(4,128)(2,1)S(1)}, u32[]{:S(2)}, u32[]{:S(2)}) %all-to-all-start.1) | async-done | bytes 573472 | tf_op jit(solution)/shard_map/all_to_all | solution.py:27
  161.3 1.5 shard_map.69
  (7 shorter events, 0.0 us)
Async XLA Ops:
  3.2 43.9 %copy-start = (bf16[64,64]{1,0:T(8,128)(2,1)S(1)}, bf16[64,64]{1,0:T(8,128)(2,1)}, u32[]{:S(2)}) copy-start(bf16[64,64]{1,0:T(8,128)(2,1)} %transform_ref.1) | copy-start | bytes 24580
  3.2 43.9 %copy-start.1 = (f32[16,1024]{1,0:T(8,128)S(1)}, f32[16,1024]{1,0:T(8,128)}, u32[]{:S(2)}) copy-start(f32[16,1024]{1,0:T(8,128)} %weight_ref.1) | copy-start | bytes 196612
  3.2 43.9 %copy-start.2 = (bf16[16,70]{1,0:T(8,128)(2,1)S(1)}, bf16[16,70]{1,0:T(8,128)(2,1)}, u32[]{:S(2)}) copy-start(bf16[16,70]{1,0:T(8,128)(2,1)} %operator_ref.1) | copy-start | bytes 6724
  3.2 74.0 %all-to-all-start = ((bf16[16,35,4,128]{3,2,1,0:T(4,128)(2,1)}), bf16[16,35,4,128]{3,2,1,0:T(4,128)(2,1)S(1)}, u32[]{:S(2)}, u32[]{:S(2)}) async-start(bf16[16,35,4,128]{3,2,1,0:T(4,128)(2,1)} %shard_map.67), calls=%async_computation | async-start | bytes 1146880 | tf_op jit(solution)/shard_map/all_to_all | solution.py:27
  80.0 3.1 %collective-permute-start = (f32[3,4,128]{2,1,0:T(4,128)S(1)}, f32[3,4,128]{2,1,0:T(4,128)S(1)}, u32[]{:S(2)}, u32[]{:S(2)}) collective-permute-start(f32[3,4,128]{2,1,0:T(4,128)S(1)} %get-tuple-element.17), channel_id=1, source_target_pairs={{0,1},{1,0},{2,3},{3,2},{4,5},{5,4},{6,7},{7,6},{8,9},{9,8},{10,11... | collective-permute-start | bytes 18440 | tf_op jit(solution)/shard_map/ppermute | solution.py:33
  101.3 3.1 %collective-permute-start.1 = (f32[3,4,128]{2,1,0:T(4,128)S(1)}, f32[3,4,128]{2,1,0:T(4,128)S(1)}, u32[]{:S(2)}, u32[]{:S(2)}) collective-permute-start(f32[3,4,128]{2,1,0:T(4,128)S(1)} %psum.7.mine_ref), channel_id=1, source_target_pairs={{0,1},{1,0},{2,3},{3,2},{4,5},{5,4},{6,7},{7,6},{8,9},{9,8},{10,11... | collective-permute-start | bytes 18440 | tf_op jit(solution)/shard_map/ppermute | solution.py:33
  105.1 23.1 %all-to-all-start.2 = ((f32[16,17,1,128]{3,2,1,0:T(1,128)}), f32[16,17,1,128]{3,2,1,0:T(1,128)S(1)}, u32[]{:S(2)}, u32[]{:S(2)}) async-start(f32[16,17,1,128]{3,2,1,0:T(1,128)} %shard_map.71), calls=%async_computation.2 | async-start | bytes 278528 | tf_op jit(solution)/shard_map/all_to_all | solution.py:27
  128.2 33.1 %all-to-all-start.1 = ((bf16[16,35,4,128]{3,2,1,0:T(4,128)(2,1)}), bf16[16,35,4,128]{3,2,1,0:T(4,128)(2,1)S(1)}, u32[]{:S(2)}, u32[]{:S(2)}) async-start(bf16[16,35,4,128]{3,2,1,0:T(4,128)(2,1)} %bitcast.20), calls=%async_computation.1 | async-start | bytes 1146880 | tf_op jit(solution)/shard_map/all_to_all | solution.py:27

commit v7 on v5

--- a/solution.py
+++ b/solution.py
@@ -23,12 +23,10 @@
 ANY = pl.BlockSpec(memory_space=pl.ANY)
 
 
-def exchange(array, axis):
-    return lax.all_to_all(array, axis, split_axis=0, concat_axis=0, tiled=True)
-
-
-def to_partner(array):
-    return lax.ppermute(array, "space_1", [(0, 1), (1, 0)])
+def exchange(array, axis, groups=None):
+    return lax.all_to_all(
+        array, axis, split_axis=0, concat_axis=0, tiled=True, axis_index_groups=groups
+    )
 
 
 def vmem(shape, dtype):
@@ -83,28 +81,41 @@
         o_ref[depth:, :, at] = jnp.concatenate([left[..., half:], right[..., half:]], axis=-1)
 
 
-def fold(gram):
-    rows = [gram[at : at + BLOCK, at:] for at in range(0, MEMBERS, BLOCK)]
-    first = jnp.concatenate([rows[0], rows[1], rows[3]], axis=1)
-    rest = jnp.concatenate([rows[2][i : i + 4] for i in range(0, BLOCK, 4)], axis=1)
-    return first, rest
-
-
-def unfold(first, rest):
-    width = 2 * BLOCK
-    third = jnp.concatenate([rest[:, i : i + width] for i in range(0, LANES, width)], axis=0)
-    rows = [first[:, :64], first[:, 64:112], third, first[:, 112:]]
-    upper = jnp.concatenate(
-        [
-            jnp.concatenate([jnp.zeros((BLOCK, MEMBERS - r.shape[1]), jnp.float32), r], axis=1)
-            if r.shape[1] < MEMBERS else r
-            for r in rows
-        ],
-        axis=0,
-    )
-    row = lax.broadcasted_iota(jnp.int32, upper.shape, 0) // BLOCK
-    column = lax.broadcasted_iota(jnp.int32, upper.shape, 1) // BLOCK
-    return jnp.where(row <= column, upper, upper.T)
+def fold(gram, total):
+    row = lax.broadcasted_iota(jnp.int32, (BLOCK, BLOCK), 0)
+    column = lax.broadcasted_iota(jnp.int32, (BLOCK, BLOCK), 1)
+    starts = range(0, MEMBERS, BLOCK)
+    across = [gram[a : a + BLOCK, a + BLOCK :] for a in starts[:-1]]
+    inner = [gram[a : a + BLOCK, a : a + BLOCK] for a in starts]
+    pairs = [
+        jnp.where(row < column, one, jnp.where(row > column, two, total))
+        for one, two in zip(inner[::2], inner[1::2], strict=True)
+    ]
+    return jnp.concatenate([*across, *pairs], axis=1)
+
+
+def unfold(packed):
+    row = lax.broadcasted_iota(jnp.int32, (BLOCK, BLOCK), 0)
+    column = lax.broadcasted_iota(jnp.int32, (BLOCK, BLOCK), 1)
+    blocks = MEMBERS // BLOCK
+    start, rows = 0, []
+    pair_start = BLOCK * blocks * (blocks - 1) // 2
+    for b in range(blocks):
+        wide = MEMBERS - BLOCK * (b + 1)
+        at = pair_start + BLOCK * (b // 2)
+        pair = packed[:, at : at + BLOCK]
+        pieces = [jnp.where(row < column if b % 2 == 0 else row > column, pair, 0.0)]
+        if b:
+            pieces.insert(0, jnp.zeros((BLOCK, BLOCK * b), jnp.float32))
+        if wide:
+            pieces.append(packed[:, start : start + wide])
+        rows.append(jnp.concatenate(pieces, axis=1))
+        start += wide
+    half = jnp.concatenate(rows, axis=0)
+    gram = half + half.T
+    row = lax.broadcasted_iota(jnp.int32, gram.shape, 0)
+    column = lax.broadcasted_iota(jnp.int32, gram.shape, 1)
+    return jnp.where(row == column, -jnp.sum(gram, axis=1, keepdims=True), gram)
 
 
 def prepare_kernel(
@@ -130,7 +141,7 @@
     turned_ref[...] = mixing.T
 
 
-def gram_kernel(core_ref, x_ref, factor_ref, weight_ref, total_ref, mine_ref, other_ref, lhs, rhs):
+def gram_kernel(x_ref, factor_ref, weight_ref, total_ref, gram_ref, lhs, rhs):
     depth, quantities = factor_ref.shape[:2]
     low = lax.broadcasted_iota(jnp.int32, (MEMBERS, LANES), 1) < LANES // 2
     zero = jnp.zeros((MEMBERS, LANES), jnp.float32)
@@ -155,31 +166,20 @@
         lhs[...], rhs[...], (((1,), (1,)), ((), ())), precision=HIGHEST,
         preferred_element_type=jnp.float32,
     )
-    first, rest = fold(gram)
-    halves = [
-        (first[8 * i : 8 * i + 4], first[8 * i + 4 : 8 * i + 8],
-         jnp.concatenate([rest[2 * i : 2 * i + 2], total_ref[:2]], axis=0))
-        for i in range(2)
-    ]
-    first_core = core_ref[0, 0] == 0
-    for i, (upper, lower) in enumerate(zip(*halves, strict=True)):
-        mine_ref[i] = jnp.where(first_core, upper, lower)
-        other_ref[i] = jnp.where(first_core, lower, upper)
-
-
-def spread_kernel(core_ref, mine_ref, other_ref, o_ref):
-    first_core = core_ref[0, 0] == 0
-    mine, other = mine_ref[...], other_ref[...]
-    total = mine[2, 2:3]
-    upper, lower = jnp.where(first_core, mine, other), jnp.where(first_core, other, mine)
-    rest = jnp.concatenate([upper[2, :2], lower[2, :2]], axis=0)
-    for i, piece in enumerate((upper[0], upper[1], lower[0], lower[1], rest)):
-        o_ref[:, i] = jnp.broadcast_to((piece / total)[None], (o_ref.shape[0], *piece.shape))
+    gram_ref[...] = fold(gram, total_ref[:1, :1])
+
+
+def spread_kernel(gram_ref, o_ref):
+    first = LANES - MEMBERS // 2
+    scaled = gram_ref[...] / gram_ref[:1, first : first + 1]
+    for i in range(BLOCK // 4):
+        piece = scaled[4 * i : 4 * i + 4]
+        o_ref[:, i] = jnp.broadcast_to(piece[None], (o_ref.shape[0], *piece.shape))
 
 
 def final_kernel(gram_ref, mixing_ref, turned_ref, prior_ref, posterior_ref):
     pieces = [jnp.sum(gram_ref[:, i], axis=0) for i in range(gram_ref.shape[1])]
-    gram = unfold(jnp.concatenate(pieces[:4], axis=0), pieces[4])
+    gram = unfold(jnp.concatenate(pieces, axis=0))
     prior_ref[...] = gram
     dot = functools.partial(jnp.dot, precision=HIGHEST, preferred_element_type=jnp.float32)
     posterior_ref[...] = dot(dot(turned_ref[...], gram), mixing_ref[...])
@@ -190,7 +190,6 @@
     quantities = obs_operator.shape[0]
     halves = LANES * mem // cells
     depth = variables // halves
-    core = lax.axis_index("space_1").astype(jnp.int32).reshape(1, 1)
     place = lax.axis_index("mem").astype(jnp.int32).reshape(1, 1)
     state_bytes = 2 * ensemble.size
     square = vmem((MEMBERS, MEMBERS), jnp.float32)
@@ -221,19 +220,18 @@
     mixed = mixed.reshape(depth, mem, local, LANES).transpose(1, 0, 2, 3)
     mixed = exchange(mixed, "mem")
 
-    half = (3, 4, LANES)
-    mine, other = kernel(
-        gram_kernel, (vmem(half, jnp.float32),) * 2, [SMEM, *[VMEM] * 4],
+    gram = kernel(
+        gram_kernel, vmem((BLOCK, LANES), jnp.float32), [VMEM] * 4,
         4 * depth * quantities * MEMBERS * LANES, state_bytes,
         [pltpu.VMEM((MEMBERS, quantities // halves * LANES), jnp.float32)] * 2,
-    )(core, members, factor, pairs, total)
-    mine = lax.psum(mine + to_partner(other), "space_0")
-    other = to_partner(mine)
+    )(members, factor, pairs, total)
+    gram = lax.psum(lax.psum(gram, "space_1"), "space_0")
     gram = kernel(
-        spread_kernel, vmem((mem, 5, 4, LANES), jnp.float32),
-        [SMEM, VMEM, VMEM], MEMBERS**2, 4 * mem * MEMBERS**2,
-    )(core, mine, other)
-    gram = exchange(gram, "mem")
+        spread_kernel, vmem((mem, BLOCK // 4, 4, LANES), jnp.float32), [VMEM],
+        MEMBERS**2, 2 * mem * MEMBERS**2,
+    )(gram)
+    far_first = [i // 2 + i % 2 * (mem // 2) for i in range(mem)]
+    gram = exchange(gram, "mem", [far_first])
     prior_gram, posterior_gram = kernel(
         final_kernel, (square, square), [VMEM] * 3, 4 * MEMBERS**3, 16 * MEMBERS**2
     )(gram, mixing, turned)

time: 165 us -> 155 us (0.939)
  waiting for transfers between devices: 74.4 us -> 66.7 us
  starting transfers between devices: 60.4 us -> 55.2 us
  blocking collectives: 18.2 us -> 20.8 us
    all_to_all x3, waiting for transfers between devices: 72.2 us -> 66.7 us  [exchange(): lax.all_to_all(array, axis, split_axis=0, concat_axis=0, tiled=True, axis...]
    ppermute x2 -> x0, starting transfers between devices: 3.9 us -> none  [to_partner(): return lax.ppermute(array, 'space_1', [(0, 1), (1, 0)])]
    psum x1 -> x2, blocking collectives: 18.2 us -> 20.8 us  [per_device(): gram = lax.psum(lax.psum(gram, 'space_1'), 'space_0')]
    ppermute x2 -> x0, waiting for transfers between devices: 2.23 us -> none  [to_partner(): return lax.ppermute(array, 'space_1', [(0, 1), (1, 0)])]
  transfers between devices with their start and end apart: 5 -> 3, of which waited for: 5 -> 3; matrix products, arithmetic and copies ran while one was open for 1% -> 1% of each run, Pallas kernels for 1% -> 1%
where the time goes in v7:
time: 155 us; the launch traced here: 154 us
  waiting for transfers between devices  66.7 us (43%)
  starting transfers between devices  55.2 us (36%)
  blocking collectives  20.8 us (13%)
  Pallas kernels  8.63 us (6%)
    all_to_all x3, waiting for transfers between devices, exchange(): lax.all_to_all(array, axis, split_axis=0, concat_axis=0, tiled=True, axis...  66.7 us
    all_to_all x3, starting transfers between devices, exchange(): lax.all_to_all(array, axis, split_axis=0, concat_axis=0, tiled=True, axis...  55.2 us
    psum x2, blocking collectives, per_device(): gram = lax.psum(lax.psum(gram, 'space_1'), 'space_0')  20.8 us
  transfers between devices with their start and end apart: 3, of which 3 were waited for; matrix products, arithmetic and copies ran while one was open for 1% of the time, Pallas kernels for 1%

profile of v7, /device:TPU:80, one launch (start us, length us, event | category | flops | bytes accessed | tf_op | source)
XLA Modules:
  0.0 154.1 jit_solution(3026869826954817837)
XLA Ops:
  0.6 2.5 %shard_map.67 = bf16[16,35,4,128]{3,2,1,0:T(4,128)(2,1)} custom-call(bf16[70,4,1024]{2,1,0:T(4,128)(2,1)} %bitcast.24), custom_call_target="tpu_custom_call" | custom-call | flops 573440 | bytes 1146880 | tf_op jit(solution)/shard_map/pallas_call | solution.py:198
  3.1 0.0 copy-start
  3.1 0.0 copy-start.1
  3.1 0.0 copy-start.2
  3.1 43.8 %all-to-all-start = ((bf16[16,35,4,128]{3,2,1,0:T(4,128)(2,1)}), bf16[16,35,4,128]{3,2,1,0:T(4,128)(2,1)S(1)}, u32[]{:S(2)}, u32[]{:S(2)}) async-start(bf16[16,35,4,128]{3,2,1,0:T(4,128)(2,1)} %shard_map.67), calls=%async_computation | async-start | bytes 1146880 | tf_op jit(solution)/shard_map/all_to_all | solution.py:27
  47.0 0.0 copy-done
  47.0 0.0 copy-done.1
  47.0 0.0 copy-done.2
  47.0 0.3 shard_map.68
  47.3 29.9 %all-to-all-done = bf16[16,35,4,128]{3,2,1,0:T(4,128)(2,1)S(1)} async-done(((bf16[16,35,4,128]{3,2,1,0:T(4,128)(2,1)}), bf16[16,35,4,128]{3,2,1,0:T(4,128)(2,1)S(1)}, u32[]{:S(2)}, u32[]{:S(2)}) %all-to-all-start) | async-done | bytes 573472 | tf_op jit(solution)/shard_map/all_to_all | solution.py:27
  77.2 0.3 copy.8
  77.5 2.4 %shard_map.70 = f32[16,128]{1,0:T(8,128)S(1)} custom-call(bf16[35,64,128]{2,1,0:T(8,128)(2,1)S(1)} %bitcast.20, f32[35,16,128]{2,1,0:T(8,128)S(1)} %get-tuple-element.11.factor_ref, f32[8,128]{1,0:T(8,128)S(1)} %get-tuple-element.12.weight_ref, f32[8,128]{1,0:T(8,128)S(1)} %get-tuple-element.13.total_ref), custom_call_target="tpu_custom_call" | custom-call | flops 18350080 | bytes 573440 | tf_op jit(solution)/shard_map/pallas_call | solution.py:223
  79.9 2.5 %psum.14 = f32[16,128]{1,0:T(8,128)S(1)} all-reduce(f32[16,128]{1,0:T(8,128)S(1)} %shard_map.70), channel_id=1, replica_groups=mesh['parts'=2,'mem'=16,'space_0'=8,'space_1'=2] {'space_1'}, use_global_device_ids=true, to_apply=%region_2.0 | all-reduce | flops 2048 | bytes 16384 | tf_op jit(solution)/shard_map/psum | solution.py:228
  82.4 18.2 %psum.15.gram_ref = f32[16,128]{1,0:T(8,128)S(1)} all-reduce(f32[16,128]{1,0:T(8,128)S(1)} %psum.14), channel_id=1, replica_groups=mesh['parts'=2,'mem'=16,'space_0'=8,'space_1'=2] {'space_0'}, use_global_device_ids=true, to_apply=%region_3.0 | all-reduce | flops 2048 | bytes 16384 | tf_op jit(solution)/shard_map/psum | solution.py:228
  100.7 0.8 shard_map.71
  101.4 7.4 %all-to-all-start.2 = ((f32[16,4,4,128]{3,2,1,0:T(4,128)}), f32[16,4,4,128]{3,2,1,0:T(4,128)S(1)}, u32[]{:S(2)}, u32[]{:S(2)}) async-start(f32[16,4,4,128]{3,2,1,0:T(4,128)} %shard_map.71), calls=%async_computation.2 | async-start | bytes 262144 | tf_op jit(solution)/shard_map/all_to_all | solution.py:27
  108.8 0.3 convert_reduce_fusion
  109.1 0.4 fusion.1
  109.5 1.0 copy.11
  110.5 12.4 %all-to-all-done.2.gram_ref = f32[16,4,4,128]{3,2,1,0:T(4,128)S(1)} async-done(((f32[16,4,4,128]{3,2,1,0:T(4,128)}), f32[16,4,4,128]{3,2,1,0:T(4,128)S(1)}, u32[]{:S(2)}, u32[]{:S(2)}) %all-to-all-start.2) | async-done | bytes 131104 | tf_op jit(solution)/shard_map/all_to_all | solution.py:27
  122.8 4.0 %all-to-all-start.1 = ((bf16[16,35,4,128]{3,2,1,0:T(4,128)(2,1)}), bf16[16,35,4,128]{3,2,1,0:T(4,128)(2,1)S(1)}, u32[]{:S(2)}, u32[]{:S(2)}) async-start(bf16[16,35,4,128]{3,2,1,0:T(4,128)(2,1)} %bitcast.19), calls=%async_computation.1 | async-start | bytes 1146880 | tf_op jit(solution)/shard_map/all_to_all | solution.py:27
  126.9 1.3 shard_map.72
  128.1 24.5 %all-to-all-done.1.x_ref = bf16[16,35,4,128]{3,2,1,0:T(4,128)(2,1)S(1)} async-done(((bf16[16,35,4,128]{3,2,1,0:T(4,128)(2,1)}), bf16[16,35,4,128]{3,2,1,0:T(4,128)(2,1)S(1)}, u32[]{:S(2)}, u32[]{:S(2)}) %all-to-all-start.1) | async-done | bytes 573472 | tf_op jit(solution)/shard_map/all_to_all | solution.py:27
  152.6 1.5 shard_map.69
  (3 shorter events, 0.0 us)
Async XLA Ops:
  3.1 43.9 %copy-start = (bf16[64,64]{1,0:T(8,128)(2,1)S(1)}, bf16[64,64]{1,0:T(8,128)(2,1)}, u32[]{:S(2)}) copy-start(bf16[64,64]{1,0:T(8,128)(2,1)} %transform_ref.1) | copy-start | bytes 24580
  3.1 43.9 %copy-start.1 = (f32[16,1024]{1,0:T(8,128)S(1)}, f32[16,1024]{1,0:T(8,128)}, u32[]{:S(2)}) copy-start(f32[16,1024]{1,0:T(8,128)} %weight_ref.1) | copy-start | bytes 196612
  3.1 43.9 %copy-start.2 = (bf16[16,70]{1,0:T(8,128)(2,1)S(1)}, bf16[16,70]{1,0:T(8,128)(2,1)}, u32[]{:S(2)}) copy-start(bf16[16,70]{1,0:T(8,128)(2,1)} %operator_ref.1) | copy-start | bytes 6724
  3.1 74.0 %all-to-all-start = ((bf16[16,35,4,128]{3,2,1,0:T(4,128)(2,1)}), bf16[16,35,4,128]{3,2,1,0:T(4,128)(2,1)S(1)}, u32[]{:S(2)}, u32[]{:S(2)}) async-start(bf16[16,35,4,128]{3,2,1,0:T(4,128)(2,1)} %shard_map.67), calls=%async_computation | async-start | bytes 1146880 | tf_op jit(solution)/shard_map/all_to_all | solution.py:27
  101.4 21.4 %all-to-all-start.2 = ((f32[16,4,4,128]{3,2,1,0:T(4,128)}), f32[16,4,4,128]{3,2,1,0:T(4,128)S(1)}, u32[]{:S(2)}, u32[]{:S(2)}) async-start(f32[16,4,4,128]{3,2,1,0:T(4,128)} %shard_map.71), calls=%async_computation.2 | async-start | bytes 262144 | tf_op jit(solution)/shard_map/all_to_all | solution.py:27
  122.8 29.8 %all-to-all-start.1 = ((bf16[16,35,4,128]{3,2,1,0:T(4,128)(2,1)}), bf16[16,35,4,128]{3,2,1,0:T(4,128)(2,1)S(1)}, u32[]{:S(2)}, u32[]{:S(2)}) async-start(bf16[16,35,4,128]{3,2,1,0:T(4,128)(2,1)} %bitcast.19), calls=%async_computation.1 | async-start | bytes 1146880 | tf_op jit(solution)/shard_map/all_to_all | solution.py:27

commit v8 on v7

--- a/solution.py
+++ b/solution.py
@@ -21,12 +21,17 @@
 SMEM = pl.BlockSpec(memory_space=pltpu.SMEM)
 VMEM = pl.BlockSpec(memory_space=pltpu.VMEM)
 ANY = pl.BlockSpec(memory_space=pl.ANY)
+HBM = pl.BlockSpec(memory_space=pltpu.HBM)
 
 
 def exchange(array, axis, groups=None):
     return lax.all_to_all(
         array, axis, split_axis=0, concat_axis=0, tiled=True, axis_index_groups=groups
     )
+
+
+def in_hbm(array):
+    return pltpu.with_memory_space_constraint(array, pltpu.HBM)
 
 
 def vmem(shape, dtype):
@@ -43,42 +48,32 @@
     )
 
 
-def pack_kernel(x_ref, o_ref, x, o, in_sems, out_sems):
+def pack_kernel(x_ref, transform_ref, o_ref, keep_ref, mixing_ref, x, sems, sem):
     depth, half = o_ref.shape[1], LANES // 2
     cuts = [depth * i // PACK_STEPS for i in range(PACK_STEPS + 1)]
     steps = [slice(a, b) for a, b in zip(cuts[:-1], cuts[1:], strict=True)]
     shifted = [slice(depth + s.start, depth + s.stop) for s in steps]
     reads = [
-        [pltpu.make_async_copy(x_ref.at[s], x.at[s], in_sems.at[i, j]) for j, s in enumerate(both)]
+        [pltpu.make_async_copy(x_ref.at[s], x.at[s], sems.at[i, j]) for j, s in enumerate(both)]
         for i, both in enumerate(zip(steps, shifted, strict=True))
     ]
-    writes = [
-        pltpu.make_async_copy(o.at[:, s], o_ref.at[:, s], out_sems.at[i])
-        for i, s in enumerate(steps)
-    ]
-    for read in reads:
-        read[0].start()
-        read[1].start()
-    for read, write, near, far in zip(reads, writes, steps, shifted, strict=True):
-        read[0].wait()
-        read[1].wait()
+    mixing_read = pltpu.make_async_copy(transform_ref, mixing_ref, sem)
+    for near_read, far_read in reads:
+        near_read.start()
+        far_read.start()
+    mixing_read.start()
+    for (near_read, far_read), near, far in zip(reads, steps, shifted, strict=True):
+        near_read.wait()
+        far_read.wait()
         for tile in range(x.shape[2] // LANES):
             at = slice(tile * LANES, (tile + 1) * LANES)
             low, high = x[near, :, at], x[far, :, at]
-            o[2 * tile, near] = jnp.concatenate([low[..., :half], high[..., :half]], axis=-1)
-            o[2 * tile + 1, near] = jnp.concatenate([low[..., half:], high[..., half:]], axis=-1)
-        write.start()
-    for write in writes:
-        write.wait()
-
-
-def unpack_kernel(x_ref, o_ref):
-    depth, half = x_ref.shape[1], LANES // 2
-    for tile in range(o_ref.shape[2] // LANES):
-        at = slice(tile * LANES, (tile + 1) * LANES)
-        left, right = x_ref[2 * tile], x_ref[2 * tile + 1]
-        o_ref[:depth, :, at] = jnp.concatenate([left[..., :half], right[..., :half]], axis=-1)
-        o_ref[depth:, :, at] = jnp.concatenate([left[..., half:], right[..., half:]], axis=-1)
+            o_ref[2 * tile, near] = jnp.concatenate([low[..., :half], high[..., :half]], axis=-1)
+            o_ref[2 * tile + 1, near] = jnp.concatenate([low[..., half:], high[..., half:]], axis=-1)
+    mixing_read.wait()
+    turned = mixing_ref[...].astype(jnp.float32).T
+    keep = (1.0 - jnp.sum(turned, axis=1, keepdims=True)) / MEMBERS
+    keep_ref[...] = jnp.broadcast_to(keep, keep_ref.shape)
 
 
 def fold(gram, total):
@@ -177,12 +172,23 @@
         o_ref[:, i] = jnp.broadcast_to(piece[None], (o_ref.shape[0], *piece.shape))
 
 
-def final_kernel(gram_ref, mixing_ref, turned_ref, prior_ref, posterior_ref):
+def final_kernel(
+    x_ref, gram_ref, mixing_ref, turned_ref, o_ref, prior_ref, posterior_ref, o, sem
+):
+    depth, half = x_ref.shape[1], LANES // 2
+    for tile in range(o.shape[2] // LANES):
+        at = slice(tile * LANES, (tile + 1) * LANES)
+        left, right = x_ref[2 * tile], x_ref[2 * tile + 1]
+        o[:depth, :, at] = jnp.concatenate([left[..., :half], right[..., :half]], axis=-1)
+        o[depth:, :, at] = jnp.concatenate([left[..., half:], right[..., half:]], axis=-1)
+    copy = pltpu.make_async_copy(o, o_ref, sem)
+    copy.start()
     pieces = [jnp.sum(gram_ref[:, i], axis=0) for i in range(gram_ref.shape[1])]
     gram = unfold(jnp.concatenate(pieces, axis=0))
     prior_ref[...] = gram
     dot = functools.partial(jnp.dot, precision=HIGHEST, preferred_element_type=jnp.float32)
     posterior_ref[...] = dot(dot(turned_ref[...], gram), mixing_ref[...])
+    copy.wait()
 
 
 def per_device(mem, ensemble, transform, obs_operator, obs_weight):
@@ -194,29 +200,29 @@
     state_bytes = 2 * ensemble.size
     square = vmem((MEMBERS, MEMBERS), jnp.float32)
 
-    block_shape, state_shape = (mem, depth, local, LANES), (variables, local, cells)
-    blocks = kernel(
-        pack_kernel, vmem(block_shape, jnp.bfloat16), [ANY],
-        state_bytes, 2 * state_bytes,
+    shapes = (
+        vmem((mem, depth, local, LANES), jnp.bfloat16), vmem((MEMBERS, LANES), jnp.float32),
+        vmem(transform.shape, transform.dtype),
+    )
+    blocks, keep_share, mixing_here = kernel(
+        pack_kernel, shapes, [HBM, HBM], state_bytes, 2 * state_bytes,
         [
-            pltpu.VMEM(state_shape, jnp.bfloat16), pltpu.VMEM(block_shape, jnp.bfloat16),
-            pltpu.SemaphoreType.DMA((PACK_STEPS, 2)), pltpu.SemaphoreType.DMA((PACK_STEPS,)),
+            pltpu.VMEM((variables, local, cells), jnp.bfloat16),
+            pltpu.SemaphoreType.DMA((PACK_STEPS, 2)), pltpu.SemaphoreType.DMA,
         ],
-        out_specs=ANY, compiler_params=pltpu.CompilerParams(),
-    )(ensemble.transpose(1, 0, 2))
+    )(in_hbm(ensemble.transpose(1, 0, 2)), in_hbm(transform))
     members = exchange(blocks, "mem")
 
     shapes = ((depth, quantities, LANES), (quantities // halves, LANES), (8, LANES))
     factor, pairs, total, mixing, turned = kernel(
         prepare_kernel, (*(vmem(s, jnp.float32) for s in shapes), square, square),
         [SMEM, VMEM, VMEM, VMEM], 4 * obs_weight.size, 8 * obs_weight.size,
-    )(place, obs_operator, obs_weight, transform)
+    )(place, obs_operator, obs_weight, mixing_here)
 
     members = members.transpose(1, 0, 2, 3).reshape(depth, MEMBERS, LANES)
-    keep_mean = 1.0 - jnp.sum(mixing, axis=0)
-    combined = jnp.einsum("ij,ric->rjc", transform, members, preferred_element_type=jnp.float32)
-    member_mean = jnp.sum(members, axis=1, dtype=jnp.float32, keepdims=True) / MEMBERS
-    mixed = (combined + member_mean * keep_mean[None, :, None]).astype(jnp.bfloat16)
+    combined = jnp.einsum("ij,ric->rjc", mixing_here, members, preferred_element_type=jnp.float32)
+    totals = jnp.sum(members, axis=1, dtype=jnp.float32, keepdims=True)
+    mixed = (combined + totals * keep_share[None]).astype(jnp.bfloat16)
     mixed = mixed.reshape(depth, mem, local, LANES).transpose(1, 0, 2, 3)
     mixed = exchange(mixed, "mem")
 
@@ -232,14 +238,12 @@
     )(gram)
     far_first = [i // 2 + i % 2 * (mem // 2) for i in range(mem)]
     gram = exchange(gram, "mem", [far_first])
-    prior_gram, posterior_gram = kernel(
-        final_kernel, (square, square), [VMEM] * 3, 4 * MEMBERS**3, 16 * MEMBERS**2
-    )(gram, mixing, turned)
-
-    analysis = kernel(
-        unpack_kernel, vmem((variables, local, cells), jnp.bfloat16), [VMEM],
-        state_bytes, 2 * state_bytes,
-    )(mixed)
+    state = vmem((variables, local, cells), jnp.bfloat16)
+    analysis, prior_gram, posterior_gram = kernel(
+        final_kernel, (state, square, square), [VMEM] * 4, state_bytes,
+        2 * state_bytes, [pltpu.VMEM(state.shape, state.dtype), pltpu.SemaphoreType.DMA],
+        out_specs=(ANY, VMEM, VMEM),
+    )(mixed, gram, mixing, turned)
     return (analysis.transpose(1, 0, 2), prior_gram, posterior_gram)
 
 

time: 155 us -> 159 us (1.026)
  blocking collectives: 20.8 us -> 53.8 us
  waiting for transfers between devices: 66.7 us -> 43.1 us
  starting transfers between devices: 55.2 us -> 51.2 us
    all_to_all x0 -> x1, blocking collectives: none -> 33.1 us  [exchange(): lax.all_to_all(array, axis, split_axis=0, concat_axis=0, tiled=True, axis...]
    all_to_all x3 -> x2, waiting for transfers between devices: 66.7 us -> 43.1 us  [exchange(): lax.all_to_all(array, axis, split_axis=0, concat_axis=0, tiled=True, axis...]
    all_to_all x3 -> x2, starting transfers between devices: 55.2 us -> 51.2 us  [exchange(): lax.all_to_all(array, axis, split_axis=0, concat_axis=0, tiled=True, axis...]
    pallas_call x3 -> x2, Pallas kernels: 5.21 us -> 4.83 us  [the longest x1 2.56 us: per_device(): kernel(pack_kernel, shapes, [HBM, HBM], state_bytes, 2 * state_bytes, [pl...]
  transfers between devices with their start and end apart: 3 -> 2, of which waited for: 3 -> 2; matrix products, arithmetic and copies ran while one was open for 1% -> 1% of each run, Pallas kernels for 1% -> 0%
where the time goes in v8:
time: 159 us; the launch traced here: 158 us
  blocking collectives  53.8 us (34%)
  starting transfers between devices  51.2 us (32%)
  waiting for transfers between devices  43.1 us (27%)
  Pallas kernels  8.27 us (5%)
    all_to_all x2, starting transfers between devices, exchange(): lax.all_to_all(array, axis, split_axis=0, concat_axis=0, tiled=True, axis...  51.2 us
    all_to_all x2, waiting for transfers between devices, exchange(): lax.all_to_all(array, axis, split_axis=0, concat_axis=0, tiled=True, axis...  43.1 us
    all_to_all x1, blocking collectives, exchange(): lax.all_to_all(array, axis, split_axis=0, concat_axis=0, tiled=True, axis...  33.1 us
    psum x2, blocking collectives, per_device(): gram = lax.psum(lax.psum(gram, 'space_1'), 'space_0')  20.8 us
  transfers between devices with their start and end apart: 2, of which 2 were waited for; matrix products, arithmetic and copies ran while one was open for 1% of the time, Pallas kernels for 0%

profile of v8, /device:TPU:80, one launch (start us, length us, event | category | flops | bytes accessed | tf_op | source)
XLA Modules:
  0.0 158.3 jit_solution(13831463255006063429)
XLA Ops:
  0.6 2.6 %shard_map.67 = (bf16[16,35,4,128]{3,2,1,0:T(4,128)(2,1)}, f32[64,128]{1,0:T(8,128)S(1)}, bf16[64,64]{1,0:T(8,128)(2,1)S(1)}) custom-call(bf16[70,4,1024]{2,1,0:T(4,128)(2,1)} %bitcast.25, bf16[64,64]{1,0:T(8,128)(2,1)} %transform_ref.1), custom_call_target="tpu_custom_call" | custom-call | flops 573440 | bytes 1146880 | tf_op jit(solution)/shard_map/pallas_call | solution.py:207
  3.2 0.0 copy-start
  3.2 0.0 copy-start.1
  3.2 43.8 %all-to-all-start = ((bf16[16,35,4,128]{3,2,1,0:T(4,128)(2,1)}), bf16[16,35,4,128]{3,2,1,0:T(4,128)(2,1)S(1)}, u32[]{:S(2)}, u32[]{:S(2)}) async-start(bf16[16,35,4,128]{3,2,1,0:T(4,128)(2,1)} %get-tuple-element.14), calls=%async_computation | async-start | bytes 1146880 | tf_op jit(solution)/shard_map/all_to_all | solution.py:28
  47.1 0.0 copy-done
  47.1 0.0 copy-done.1
  47.1 0.3 shard_map.68
  47.3 29.9 %all-to-all-done = bf16[16,35,4,128]{3,2,1,0:T(4,128)(2,1)S(1)} async-done(((bf16[16,35,4,128]{3,2,1,0:T(4,128)(2,1)}), bf16[16,35,4,128]{3,2,1,0:T(4,128)(2,1)S(1)}, u32[]{:S(2)}, u32[]{:S(2)}) %all-to-all-start) | async-done | bytes 573472 | tf_op jit(solution)/shard_map/all_to_all | solution.py:28
  77.2 0.3 copy.8
  77.5 2.4 %shard_map.69 = f32[16,128]{1,0:T(8,128)S(1)} custom-call(bf16[35,64,128]{2,1,0:T(8,128)(2,1)S(1)} %bitcast.20, f32[35,16,128]{2,1,0:T(8,128)S(1)} %get-tuple-element.17.factor_ref, f32[8,128]{1,0:T(8,128)S(1)} %get-tuple-element.18.weight_ref, f32[8,128]{1,0:T(8,128)S(1)} %get-tuple-element.19.total_ref), custom_call_target="tpu_custom_call" | custom-call | flops 18350080 | bytes 573440 | tf_op jit(solution)/shard_map/pallas_call | solution.py:229
  79.9 2.5 %psum.14 = f32[16,128]{1,0:T(8,128)S(1)} all-reduce(f32[16,128]{1,0:T(8,128)S(1)} %shard_map.69), channel_id=1, replica_groups=mesh['parts'=2,'mem'=16,'space_0'=8,'space_1'=2] {'space_1'}, use_global_device_ids=true, to_apply=%region_1.0 | all-reduce | flops 2048 | bytes 16384 | tf_op jit(solution)/shard_map/psum | solution.py:234
  82.5 18.2 %psum.15.gram_ref = f32[16,128]{1,0:T(8,128)S(1)} all-reduce(f32[16,128]{1,0:T(8,128)S(1)} %psum.14), channel_id=1, replica_groups=mesh['parts'=2,'mem'=16,'space_0'=8,'space_1'=2] {'space_0'}, use_global_device_ids=true, to_apply=%region_2.0 | all-reduce | flops 2048 | bytes 16384 | tf_op jit(solution)/shard_map/psum | solution.py:234
  100.7 0.8 shard_map.70
  101.5 7.4 %all-to-all-start.2 = ((f32[16,4,4,128]{3,2,1,0:T(4,128)}), f32[16,4,4,128]{3,2,1,0:T(4,128)S(1)}, u32[]{:S(2)}, u32[]{:S(2)}) async-start(f32[16,4,4,128]{3,2,1,0:T(4,128)} %shard_map.70), calls=%async_computation.2 | async-start | bytes 262144 | tf_op jit(solution)/shard_map/all_to_all | solution.py:28
  108.9 0.3 convert_reduce_fusion
  109.2 0.4 fusion.1
  109.5 0.2 copy.11
  109.7 13.2 %all-to-all-done.2.gram_ref = f32[16,4,4,128]{3,2,1,0:T(4,128)S(1)} async-done(((f32[16,4,4,128]{3,2,1,0:T(4,128)}), f32[16,4,4,128]{3,2,1,0:T(4,128)S(1)}, u32[]{:S(2)}, u32[]{:S(2)}) %all-to-all-start.2) | async-done | bytes 131104 | tf_op jit(solution)/shard_map/all_to_all | solution.py:28
  122.9 33.1 %all_to_all.15.x_ref = bf16[16,35,4,128]{3,2,1,0:T(4,128)(2,1)S(1)} all-to-all(bf16[16,35,4,128]{3,2,1,0:T(4,128)(2,1)S(1)} %bitcast.23), channel_id=1, replica_groups=mesh['parts'=2,'mem'=16,'space_0'=8,'space_1'=2] {'mem'}, dimensions={0} | all-to-all | bytes 1146880 | tf_op jit(solution)/shard_map/all_to_all | solution.py:28
  156.0 2.3 %shard_map.71 = (bf16[70,4,1024]{2,1,0:T(4,128)(2,1)}, f32[64,64]{1,0:T(8,128)}, f32[64,64]{1,0:T(8,128)}) custom-call(bf16[16,35,4,128]{3,2,1,0:T(4,128)(2,1)S(1)} %all_to_all.15.x_ref, f32[16,4,4,128]{3,2,1,0:T(4,128)S(1)} %all-to-all-done.2.gram_ref, f32[64,64]{1,0:T(8,128)S(1)} %get-tuple-element.20.mixing_ref, f32[64,64]{1,0:T(8,128)S(1)} %get-tuple-element.21.turned_ref), custom_call_target="tpu_custom_call" | custom-call | flops 573440 | bytes 1146880 | tf_op jit(solution)/shard_map/pallas_call | solution.py:242
Async XLA Ops:
  3.2 43.9 %copy-start = (f32[16,1024]{1,0:T(8,128)S(1)}, f32[16,1024]{1,0:T(8,128)}, u32[]{:S(2)}) copy-start(f32[16,1024]{1,0:T(8,128)} %weight_ref.1) | copy-start | bytes 196612
  3.2 43.9 %copy-start.1 = (bf16[16,70]{1,0:T(8,128)(2,1)S(1)}, bf16[16,70]{1,0:T(8,128)(2,1)}, u32[]{:S(2)}) copy-start(bf16[16,70]{1,0:T(8,128)(2,1)} %operator_ref.1) | copy-start | bytes 6724
  3.2 74.0 %all-to-all-start = ((bf16[16,35,4,128]{3,2,1,0:T(4,128)(2,1)}), bf16[16,35,4,128]{3,2,1,0:T(4,128)(2,1)S(1)}, u32[]{:S(2)}, u32[]{:S(2)}) async-start(bf16[16,35,4,128]{3,2,1,0:T(4,128)(2,1)} %get-tuple-element.14), calls=%async_computation | async-start | bytes 1146880 | tf_op jit(solution)/shard_map/all_to_all | solution.py:28
  101.5 21.4 %all-to-all-start.2 = ((f32[16,4,4,128]{3,2,1,0:T(4,128)}), f32[16,4,4,128]{3,2,1,0:T(4,128)S(1)}, u32[]{:S(2)}, u32[]{:S(2)}) async-start(f32[16,4,4,128]{3,2,1,0:T(4,128)} %shard_map.70), calls=%async_computation.2 | async-start | bytes 262144 | tf_op jit(solution)/shard_map/all_to_all | solution.py:28

commit v9 on v8

--- a/solution.py
+++ b/solution.py
@@ -13,14 +13,13 @@
 LANES = 128
 GROUP = 4
 BLOCK = 16
-PACK_STEPS = 2
+PACK_STEPS = 5
 VMEM_LIMIT = 12 << 20
 HIGHEST = lax.Precision.HIGHEST
 
 
 SMEM = pl.BlockSpec(memory_space=pltpu.SMEM)
 VMEM = pl.BlockSpec(memory_space=pltpu.VMEM)
-ANY = pl.BlockSpec(memory_space=pl.ANY)
 HBM = pl.BlockSpec(memory_space=pltpu.HBM)
 
 
@@ -76,6 +75,15 @@
     keep_ref[...] = jnp.broadcast_to(keep, keep_ref.shape)
 
 
+def unpack_kernel(x_ref, o_ref):
+    depth, half = x_ref.shape[1], LANES // 2
+    for tile in range(o_ref.shape[2] // LANES):
+        at = slice(tile * LANES, (tile + 1) * LANES)
+        left, right = x_ref[2 * tile], x_ref[2 * tile + 1]
+        o_ref[:depth, :, at] = jnp.concatenate([left[..., :half], right[..., :half]], axis=-1)
+        o_ref[depth:, :, at] = jnp.concatenate([left[..., half:], right[..., half:]], axis=-1)
+
+
 def fold(gram, total):
     row = lax.broadcasted_iota(jnp.int32, (BLOCK, BLOCK), 0)
     column = lax.broadcasted_iota(jnp.int32, (BLOCK, BLOCK), 1)
@@ -172,23 +180,12 @@
         o_ref[:, i] = jnp.broadcast_to(piece[None], (o_ref.shape[0], *piece.shape))
 
 
-def final_kernel(
-    x_ref, gram_ref, mixing_ref, turned_ref, o_ref, prior_ref, posterior_ref, o, sem
-):
-    depth, half = x_ref.shape[1], LANES // 2
-    for tile in range(o.shape[2] // LANES):
-        at = slice(tile * LANES, (tile + 1) * LANES)
-        left, right = x_ref[2 * tile], x_ref[2 * tile + 1]
-        o[:depth, :, at] = jnp.concatenate([left[..., :half], right[..., :half]], axis=-1)
-        o[depth:, :, at] = jnp.concatenate([left[..., half:], right[..., half:]], axis=-1)
-    copy = pltpu.make_async_copy(o, o_ref, sem)
-    copy.start()
+def final_kernel(gram_ref, mixing_ref, turned_ref, prior_ref, posterior_ref):
     pieces = [jnp.sum(gram_ref[:, i], axis=0) for i in range(gram_ref.shape[1])]
     gram = unfold(jnp.concatenate(pieces, axis=0))
     prior_ref[...] = gram
     dot = functools.partial(jnp.dot, precision=HIGHEST, preferred_element_type=jnp.float32)
     posterior_ref[...] = dot(dot(turned_ref[...], gram), mixing_ref[...])
-    copy.wait()
 
 
 def per_device(mem, ensemble, transform, obs_operator, obs_weight):
@@ -236,14 +233,16 @@
         spread_kernel, vmem((mem, BLOCK // 4, 4, LANES), jnp.float32), [VMEM],
         MEMBERS**2, 2 * mem * MEMBERS**2,
     )(gram)
-    far_first = [i // 2 + i % 2 * (mem // 2) for i in range(mem)]
+    far_first = [i // 2 + (i + 1) % 2 * (mem // 2) for i in range(mem)]
     gram = exchange(gram, "mem", [far_first])
-    state = vmem((variables, local, cells), jnp.bfloat16)
-    analysis, prior_gram, posterior_gram = kernel(
-        final_kernel, (state, square, square), [VMEM] * 4, state_bytes,
-        2 * state_bytes, [pltpu.VMEM(state.shape, state.dtype), pltpu.SemaphoreType.DMA],
-        out_specs=(ANY, VMEM, VMEM),
-    )(mixed, gram, mixing, turned)
+    prior_gram, posterior_gram = kernel(
+        final_kernel, (square, square), [VMEM] * 3, 4 * MEMBERS**3, 16 * MEMBERS**2
+    )(gram, mixing, turned)
+
+    analysis = kernel(
+        unpack_kernel, vmem((variables, local, cells), jnp.bfloat16), [VMEM],
+        state_bytes, 2 * state_bytes,
+    )(mixed)
     return (analysis.transpose(1, 0, 2), prior_gram, posterior_gram)
 
 

time: 159 us -> 160 us (level)
  blocking collectives: 53.8 us -> 20.8 us
  starting transfers between devices: 51.2 us -> 70.1 us
  waiting for transfers between devices: 43.1 us -> 57.2 us
    all_to_all x1 -> x0, blocking collectives: 33.1 us -> none  [exchange(): lax.all_to_all(array, axis, split_axis=0, concat_axis=0, tiled=True, axis...]
    all_to_all x2 -> x3, starting transfers between devices: 51.2 us -> 70.1 us  [exchange(): lax.all_to_all(array, axis, split_axis=0, concat_axis=0, tiled=True, axis...]
    all_to_all x2 -> x3, waiting for transfers between devices: 43.1 us -> 57.2 us  [exchange(): lax.all_to_all(array, axis, split_axis=0, concat_axis=0, tiled=True, axis...]
  transfers between devices with their start and end apart: 2 -> 3, of which waited for: 2 -> 3; matrix products, arithmetic and copies ran while one was open for 1% -> 1% of each run, Pallas kernels for 0% -> 1%
where the time goes in v9:
time: 160 us
  starting transfers between devices  70.1 us (44%)
  waiting for transfers between devices  57.2 us (36%)
  blocking collectives  20.8 us (13%)
  Pallas kernels  8.87 us (6%)
    all_to_all x3, starting transfers between devices, exchange(): lax.all_to_all(array, axis, split_axis=0, concat_axis=0, tiled=True, axis...  70.1 us
    all_to_all x3, waiting for transfers between devices, exchange(): lax.all_to_all(array, axis, split_axis=0, concat_axis=0, tiled=True, axis...  57.2 us
    psum x2, blocking collectives, per_device(): gram = lax.psum(lax.psum(gram, 'space_1'), 'space_0')  20.8 us
  transfers between devices with their start and end apart: 3, of which 3 were waited for; matrix products, arithmetic and copies ran while one was open for 1% of the time, Pallas kernels for 1%

profile of v9, /device:TPU:80, one launch (start us, length us, event | category | flops | bytes accessed | tf_op | source)
XLA Modules:
  0.0 159.6 jit_solution(13393185439614446149)
XLA Ops:
  0.6 2.7 %shard_map.67 = (bf16[16,35,4,128]{3,2,1,0:T(4,128)(2,1)}, f32[64,128]{1,0:T(8,128)S(1)}, bf16[64,64]{1,0:T(8,128)(2,1)S(1)}) custom-call(bf16[70,4,1024]{2,1,0:T(4,128)(2,1)} %bitcast.24, bf16[64,64]{1,0:T(8,128)(2,1)} %transform_ref.1), custom_call_target="tpu_custom_call" | custom-call | flops 573440 | bytes 1146880 | tf_op jit(solution)/shard_map/pallas_call | solution.py:204
  3.3 0.0 copy-start
  3.4 0.0 copy-start.1
  3.4 43.8 %all-to-all-start = ((bf16[16,35,4,128]{3,2,1,0:T(4,128)(2,1)}), bf16[16,35,4,128]{3,2,1,0:T(4,128)(2,1)S(1)}, u32[]{:S(2)}, u32[]{:S(2)}) async-start(bf16[16,35,4,128]{3,2,1,0:T(4,128)(2,1)} %get-tuple-element.13), calls=%async_computation | async-start | bytes 1146880 | tf_op jit(solution)/shard_map/all_to_all | solution.py:27
  47.2 0.0 copy-done
  47.2 0.0 copy-done.1
  47.2 0.3 shard_map.69
  47.5 29.9 %all-to-all-done = bf16[16,35,4,128]{3,2,1,0:T(4,128)(2,1)S(1)} async-done(((bf16[16,35,4,128]{3,2,1,0:T(4,128)(2,1)}), bf16[16,35,4,128]{3,2,1,0:T(4,128)(2,1)S(1)}, u32[]{:S(2)}, u32[]{:S(2)}) %all-to-all-start) | async-done | bytes 573472 | tf_op jit(solution)/shard_map/all_to_all | solution.py:27
  77.4 0.3 copy.8
  77.7 2.4 %shard_map.70 = f32[16,128]{1,0:T(8,128)S(1)} custom-call(bf16[35,64,128]{2,1,0:T(8,128)(2,1)S(1)} %bitcast.20, f32[35,16,128]{2,1,0:T(8,128)S(1)} %get-tuple-element.16.factor_ref, f32[8,128]{1,0:T(8,128)S(1)} %get-tuple-element.17.weight_ref, f32[8,128]{1,0:T(8,128)S(1)} %get-tuple-element.18.total_ref), custom_call_target="tpu_custom_call" | custom-call | flops 18350080 | bytes 573440 | tf_op jit(solution)/shard_map/pallas_call | solution.py:226
  80.1 2.5 %psum.14 = f32[16,128]{1,0:T(8,128)S(1)} all-reduce(f32[16,128]{1,0:T(8,128)S(1)} %shard_map.70), channel_id=1, replica_groups=mesh['parts'=2,'mem'=16,'space_0'=8,'space_1'=2] {'space_1'}, use_global_device_ids=true, to_apply=%region_1.0 | all-reduce | flops 2048 | bytes 16384 | tf_op jit(solution)/shard_map/psum | solution.py:231
  82.6 18.2 %psum.15.gram_ref = f32[16,128]{1,0:T(8,128)S(1)} all-reduce(f32[16,128]{1,0:T(8,128)S(1)} %psum.14), channel_id=1, replica_groups=mesh['parts'=2,'mem'=16,'space_0'=8,'space_1'=2] {'space_0'}, use_global_device_ids=true, to_apply=%region_2.0 | all-reduce | flops 2048 | bytes 16384 | tf_op jit(solution)/shard_map/psum | solution.py:231
  100.9 0.8 shard_map.71
  101.6 14.7 %all-to-all-start.2 = ((f32[16,4,4,128]{3,2,1,0:T(4,128)}), f32[16,4,4,128]{3,2,1,0:T(4,128)S(1)}, u32[]{:S(2)}, u32[]{:S(2)}) async-start(f32[16,4,4,128]{3,2,1,0:T(4,128)} %shard_map.71), calls=%async_computation.2 | async-start | bytes 262144 | tf_op jit(solution)/shard_map/all_to_all | solution.py:27
  116.3 0.3 convert_reduce_fusion
  116.6 0.4 fusion.1
  116.9 1.0 copy.11
  117.9 2.8 %all-to-all-done.2.gram_ref = f32[16,4,4,128]{3,2,1,0:T(4,128)S(1)} async-done(((f32[16,4,4,128]{3,2,1,0:T(4,128)}), f32[16,4,4,128]{3,2,1,0:T(4,128)S(1)}, u32[]{:S(2)}, u32[]{:S(2)}) %all-to-all-start.2) | async-done | bytes 131104 | tf_op jit(solution)/shard_map/all_to_all | solution.py:27
  120.7 11.6 %all-to-all-start.1 = ((bf16[16,35,4,128]{3,2,1,0:T(4,128)(2,1)}), bf16[16,35,4,128]{3,2,1,0:T(4,128)(2,1)S(1)}, u32[]{:S(2)}, u32[]{:S(2)}) async-start(bf16[16,35,4,128]{3,2,1,0:T(4,128)(2,1)} %bitcast.19), calls=%async_computation.1 | async-start | bytes 1146880 | tf_op jit(solution)/shard_map/all_to_all | solution.py:27
  132.3 1.3 shard_map.72
  133.6 24.5 %all-to-all-done.1.x_ref = bf16[16,35,4,128]{3,2,1,0:T(4,128)(2,1)S(1)} async-done(((bf16[16,35,4,128]{3,2,1,0:T(4,128)(2,1)}), bf16[16,35,4,128]{3,2,1,0:T(4,128)(2,1)S(1)}, u32[]{:S(2)}, u32[]{:S(2)}) %all-to-all-start.1) | async-done | bytes 573472 | tf_op jit(solution)/shard_map/all_to_all | solution.py:27
  158.1 1.5 shard_map.68
Async XLA Ops:
  3.3 43.9 %copy-start = (f32[16,1024]{1,0:T(8,128)S(1)}, f32[16,1024]{1,0:T(8,128)}, u32[]{:S(2)}) copy-start(f32[16,1024]{1,0:T(8,128)} %weight_ref.1) | copy-start | bytes 196612
  3.4 43.9 %copy-start.1 = (bf16[16,70]{1,0:T(8,128)(2,1)S(1)}, bf16[16,70]{1,0:T(8,128)(2,1)}, u32[]{:S(2)}) copy-start(bf16[16,70]{1,0:T(8,128)(2,1)} %operator_ref.1) | copy-start | bytes 6724
  3.4 74.0 %all-to-all-start = ((bf16[16,35,4,128]{3,2,1,0:T(4,128)(2,1)}), bf16[16,35,4,128]{3,2,1,0:T(4,128)(2,1)S(1)}, u32[]{:S(2)}, u32[]{:S(2)}) async-start(bf16[16,35,4,128]{3,2,1,0:T(4,128)(2,1)} %get-tuple-element.13), calls=%async_computation | async-start | bytes 1146880 | tf_op jit(solution)/shard_map/all_to_all | solution.py:27
  101.6 19.1 %all-to-all-start.2 = ((f32[16,4,4,128]{3,2,1,0:T(4,128)}), f32[16,4,4,128]{3,2,1,0:T(4,128)S(1)}, u32[]{:S(2)}, u32[]{:S(2)}) async-start(f32[16,4,4,128]{3,2,1,0:T(4,128)} %shard_map.71), calls=%async_computation.2 | async-start | bytes 262144 | tf_op jit(solution)/shard_map/all_to_all | solution.py:27
  120.7 37.4 %all-to-all-start.1 = ((bf16[16,35,4,128]{3,2,1,0:T(4,128)(2,1)}), bf16[16,35,4,128]{3,2,1,0:T(4,128)(2,1)S(1)}, u32[]{:S(2)}, u32[]{:S(2)}) async-start(bf16[16,35,4,128]{3,2,1,0:T(4,128)(2,1)} %bitcast.19), calls=%async_computation.1 | async-start | bytes 1146880 | tf_op jit(solution)/shard_map/all_to_all | solution.py:27

commit v10 on v9

--- a/solution.py
+++ b/solution.py
@@ -233,8 +233,9 @@
         spread_kernel, vmem((mem, BLOCK // 4, 4, LANES), jnp.float32), [VMEM],
         MEMBERS**2, 2 * mem * MEMBERS**2,
     )(gram)
-    far_first = [i // 2 + (i + 1) % 2 * (mem // 2) for i in range(mem)]
-    gram = exchange(gram, "mem", [far_first])
+    order = [i // 2 + (i + 1) % 2 * (mem // 2) for i in range(mem)]
+    order = order[mem // 4 :] + order[: mem // 4]
+    gram = exchange(gram, "mem", [order])
     prior_gram, posterior_gram = kernel(
         final_kernel, (square, square), [VMEM] * 3, 4 * MEMBERS**3, 16 * MEMBERS**2
     )(gram, mixing, turned)

time: 160 us -> 159 us (level)
  starting transfers between devices: 70.1 us -> 66.4 us
  waiting for transfers between devices: 57.2 us -> 59.5 us
    all_to_all x3, starting transfers between devices: 70.1 us -> 66.4 us  [exchange(): lax.all_to_all(array, axis, split_axis=0, concat_axis=0, tiled=True, axis...]
    all_to_all x3, waiting for transfers between devices: 57.2 us -> 59.5 us  [exchange(): lax.all_to_all(array, axis, split_axis=0, concat_axis=0, tiled=True, axis...]
where the time goes in v10:
time: 159 us; the launch traced here: 158 us
  starting transfers between devices  66.4 us (42%)
  waiting for transfers between devices  59.5 us (37%)
  blocking collectives  20.8 us (13%)
  Pallas kernels  8.87 us (6%)
    all_to_all x3, starting transfers between devices, exchange(): lax.all_to_all(array, axis, split_axis=0, concat_axis=0, tiled=True, axis...  66.4 us
    all_to_all x3, waiting for transfers between devices, exchange(): lax.all_to_all(array, axis, split_axis=0, concat_axis=0, tiled=True, axis...  59.5 us
    psum x2, blocking collectives, per_device(): gram = lax.psum(lax.psum(gram, 'space_1'), 'space_0')  20.8 us
  transfers between devices with their start and end apart: 3, of which 3 were waited for; matrix products, arithmetic and copies ran while one was open for 1% of the time, Pallas kernels for 1%

profile of v10, /device:TPU:80, one launch (start us, length us, event | category | flops | bytes accessed | tf_op | source)
XLA Modules:
  0.0 158.2 jit_solution(12316512264611825987)
XLA Ops:
  0.6 2.7 %shard_map.67 = (bf16[16,35,4,128]{3,2,1,0:T(4,128)(2,1)}, f32[64,128]{1,0:T(8,128)S(1)}, bf16[64,64]{1,0:T(8,128)(2,1)S(1)}) custom-call(bf16[70,4,1024]{2,1,0:T(4,128)(2,1)} %bitcast.24, bf16[64,64]{1,0:T(8,128)(2,1)} %transform_ref.1), custom_call_target="tpu_custom_call" | custom-call | flops 573440 | bytes 1146880 | tf_op jit(solution)/shard_map/pallas_call | solution.py:204
  3.3 0.0 copy-start
  3.4 0.0 copy-start.1
  3.4 43.8 %all-to-all-start = ((bf16[16,35,4,128]{3,2,1,0:T(4,128)(2,1)}), bf16[16,35,4,128]{3,2,1,0:T(4,128)(2,1)S(1)}, u32[]{:S(2)}, u32[]{:S(2)}) async-start(bf16[16,35,4,128]{3,2,1,0:T(4,128)(2,1)} %get-tuple-element.13), calls=%async_computation | async-start | bytes 1146880 | tf_op jit(solution)/shard_map/all_to_all | solution.py:27
  47.2 0.0 copy-done
  47.2 0.0 copy-done.1
  47.2 0.3 shard_map.69
  47.5 29.9 %all-to-all-done = bf16[16,35,4,128]{3,2,1,0:T(4,128)(2,1)S(1)} async-done(((bf16[16,35,4,128]{3,2,1,0:T(4,128)(2,1)}), bf16[16,35,4,128]{3,2,1,0:T(4,128)(2,1)S(1)}, u32[]{:S(2)}, u32[]{:S(2)}) %all-to-all-start) | async-done | bytes 573472 | tf_op jit(solution)/shard_map/all_to_all | solution.py:27
  77.4 0.3 copy.8
  77.7 2.4 %shard_map.70 = f32[16,128]{1,0:T(8,128)S(1)} custom-call(bf16[35,64,128]{2,1,0:T(8,128)(2,1)S(1)} %bitcast.20, f32[35,16,128]{2,1,0:T(8,128)S(1)} %get-tuple-element.16.factor_ref, f32[8,128]{1,0:T(8,128)S(1)} %get-tuple-element.17.weight_ref, f32[8,128]{1,0:T(8,128)S(1)} %get-tuple-element.18.total_ref), custom_call_target="tpu_custom_call" | custom-call | flops 18350080 | bytes 573440 | tf_op jit(solution)/shard_map/pallas_call | solution.py:226
  80.1 2.5 %psum.14 = f32[16,128]{1,0:T(8,128)S(1)} all-reduce(f32[16,128]{1,0:T(8,128)S(1)} %shard_map.70), channel_id=1, replica_groups=mesh['parts'=2,'mem'=16,'space_0'=8,'space_1'=2] {'space_1'}, use_global_device_ids=true, to_apply=%region_1.0 | all-reduce | flops 2048 | bytes 16384 | tf_op jit(solution)/shard_map/psum | solution.py:231
  82.6 18.2 %psum.15.gram_ref = f32[16,128]{1,0:T(8,128)S(1)} all-reduce(f32[16,128]{1,0:T(8,128)S(1)} %psum.14), channel_id=1, replica_groups=mesh['parts'=2,'mem'=16,'space_0'=8,'space_1'=2] {'space_0'}, use_global_device_ids=true, to_apply=%region_2.0 | all-reduce | flops 2048 | bytes 16384 | tf_op jit(solution)/shard_map/psum | solution.py:231
  100.9 0.8 shard_map.71
  101.6 12.9 %all-to-all-start.2 = ((f32[16,4,4,128]{3,2,1,0:T(4,128)}), f32[16,4,4,128]{3,2,1,0:T(4,128)S(1)}, u32[]{:S(2)}, u32[]{:S(2)}) async-start(f32[16,4,4,128]{3,2,1,0:T(4,128)} %shard_map.71), calls=%async_computation.2 | async-start | bytes 262144 | tf_op jit(solution)/shard_map/all_to_all | solution.py:27
  114.5 0.3 convert_reduce_fusion
  114.8 0.4 fusion.1
  115.1 1.0 copy.11
  116.2 4.9 %all-to-all-done.2.gram_ref = f32[16,4,4,128]{3,2,1,0:T(4,128)S(1)} async-done(((f32[16,4,4,128]{3,2,1,0:T(4,128)}), f32[16,4,4,128]{3,2,1,0:T(4,128)S(1)}, u32[]{:S(2)}, u32[]{:S(2)}) %all-to-all-start.2) | async-done | bytes 131104 | tf_op jit(solution)/shard_map/all_to_all | solution.py:27
  121.0 9.7 %all-to-all-start.1 = ((bf16[16,35,4,128]{3,2,1,0:T(4,128)(2,1)}), bf16[16,35,4,128]{3,2,1,0:T(4,128)(2,1)S(1)}, u32[]{:S(2)}, u32[]{:S(2)}) async-start(bf16[16,35,4,128]{3,2,1,0:T(4,128)(2,1)} %bitcast.19), calls=%async_computation.1 | async-start | bytes 1146880 | tf_op jit(solution)/shard_map/all_to_all | solution.py:27
  130.7 1.3 shard_map.72
  132.0 24.7 %all-to-all-done.1.x_ref = bf16[16,35,4,128]{3,2,1,0:T(4,128)(2,1)S(1)} async-done(((bf16[16,35,4,128]{3,2,1,0:T(4,128)(2,1)}), bf16[16,35,4,128]{3,2,1,0:T(4,128)(2,1)S(1)}, u32[]{:S(2)}, u32[]{:S(2)}) %all-to-all-start.1) | async-done | bytes 573472 | tf_op jit(solution)/shard_map/all_to_all | solution.py:27
  156.7 1.5 shard_map.68
Async XLA Ops:
  3.3 43.9 %copy-start = (f32[16,1024]{1,0:T(8,128)S(1)}, f32[16,1024]{1,0:T(8,128)}, u32[]{:S(2)}) copy-start(f32[16,1024]{1,0:T(8,128)} %weight_ref.1) | copy-start | bytes 196612
  3.4 43.9 %copy-start.1 = (bf16[16,70]{1,0:T(8,128)(2,1)S(1)}, bf16[16,70]{1,0:T(8,128)(2,1)}, u32[]{:S(2)}) copy-start(bf16[16,70]{1,0:T(8,128)(2,1)} %operator_ref.1) | copy-start | bytes 6724
  3.4 74.0 %all-to-all-start = ((bf16[16,35,4,128]{3,2,1,0:T(4,128)(2,1)}), bf16[16,35,4,128]{3,2,1,0:T(4,128)(2,1)S(1)}, u32[]{:S(2)}, u32[]{:S(2)}) async-start(bf16[16,35,4,128]{3,2,1,0:T(4,128)(2,1)} %get-tuple-element.13), calls=%async_computation | async-start | bytes 1146880 | tf_op jit(solution)/shard_map/all_to_all | solution.py:27
  101.6 19.4 %all-to-all-start.2 = ((f32[16,4,4,128]{3,2,1,0:T(4,128)}), f32[16,4,4,128]{3,2,1,0:T(4,128)S(1)}, u32[]{:S(2)}, u32[]{:S(2)}) async-start(f32[16,4,4,128]{3,2,1,0:T(4,128)} %shard_map.71), calls=%async_computation.2 | async-start | bytes 262144 | tf_op jit(solution)/shard_map/all_to_all | solution.py:27
  121.0 35.7 %all-to-all-start.1 = ((bf16[16,35,4,128]{3,2,1,0:T(4,128)(2,1)}), bf16[16,35,4,128]{3,2,1,0:T(4,128)(2,1)S(1)}, u32[]{:S(2)}, u32[]{:S(2)}) async-start(bf16[16,35,4,128]{3,2,1,0:T(4,128)(2,1)} %bitcast.19), calls=%async_computation.1 | async-start | bytes 1146880 | tf_op jit(solution)/shard_map/all_to_all | solution.py:27

commit v11 on v9

--- a/solution.py
+++ b/solution.py
@@ -47,7 +47,13 @@
     )
 
 
-def pack_kernel(x_ref, transform_ref, o_ref, keep_ref, mixing_ref, x, sems, sem):
+def rotate(array, by, axis):
+    cut = array.shape[axis] - by
+    parts = (array[cut:], array[:cut]) if axis == 0 else (array[:, cut:], array[:, :cut])
+    return jnp.concatenate(parts, axis=axis)
+
+
+def pack_kernel(x_ref, transform_ref, o_ref, keep_ref, mixing_ref, x, read_transform, sems, sem):
     depth, half = o_ref.shape[1], LANES // 2
     cuts = [depth * i // PACK_STEPS for i in range(PACK_STEPS + 1)]
     steps = [slice(a, b) for a, b in zip(cuts[:-1], cuts[1:], strict=True)]
@@ -56,30 +62,32 @@
         [pltpu.make_async_copy(x_ref.at[s], x.at[s], sems.at[i, j]) for j, s in enumerate(both)]
         for i, both in enumerate(zip(steps, shifted, strict=True))
     ]
-    mixing_read = pltpu.make_async_copy(transform_ref, mixing_ref, sem)
+    mixing_read = pltpu.make_async_copy(transform_ref, read_transform, sem)
     for near_read, far_read in reads:
         near_read.start()
         far_read.start()
     mixing_read.start()
+    mixing_read.wait()
+    local, mem = o_ref.shape[2], o_ref.shape[0]
+    mixing = rotate(rotate(read_transform[...].astype(jnp.float32), local, 0), local, 1)
+    mixing_ref[...] = mixing.astype(mixing_ref.dtype)
+    keep = (1.0 - jnp.sum(mixing.T, axis=1, keepdims=True)) / MEMBERS
+    keep_ref[...] = jnp.broadcast_to(keep, keep_ref.shape)
     for (near_read, far_read), near, far in zip(reads, steps, shifted, strict=True):
         near_read.wait()
         far_read.wait()
         for tile in range(x.shape[2] // LANES):
             at = slice(tile * LANES, (tile + 1) * LANES)
             low, high = x[near, :, at], x[far, :, at]
-            o_ref[2 * tile, near] = jnp.concatenate([low[..., :half], high[..., :half]], axis=-1)
-            o_ref[2 * tile + 1, near] = jnp.concatenate([low[..., half:], high[..., half:]], axis=-1)
-    mixing_read.wait()
-    turned = mixing_ref[...].astype(jnp.float32).T
-    keep = (1.0 - jnp.sum(turned, axis=1, keepdims=True)) / MEMBERS
-    keep_ref[...] = jnp.broadcast_to(keep, keep_ref.shape)
+            o_ref[2 * tile + 1, near] = jnp.concatenate([low[..., :half], high[..., :half]], axis=-1)
+            o_ref[(2 * tile + 2) % mem, near] = jnp.concatenate([low[..., half:], high[..., half:]], axis=-1)
 
 
 def unpack_kernel(x_ref, o_ref):
     depth, half = x_ref.shape[1], LANES // 2
     for tile in range(o_ref.shape[2] // LANES):
         at = slice(tile * LANES, (tile + 1) * LANES)
-        left, right = x_ref[2 * tile], x_ref[2 * tile + 1]
+        left, right = x_ref[2 * tile + 1], x_ref[(2 * tile + 2) % x_ref.shape[0]]
         o_ref[:depth, :, at] = jnp.concatenate([left[..., :half], right[..., :half]], axis=-1)
         o_ref[depth:, :, at] = jnp.concatenate([left[..., half:], right[..., half:]], axis=-1)
 
@@ -180,12 +188,14 @@
         o_ref[:, i] = jnp.broadcast_to(piece[None], (o_ref.shape[0], *piece.shape))
 
 
-def final_kernel(gram_ref, mixing_ref, turned_ref, prior_ref, posterior_ref):
+def final_kernel(local, gram_ref, mixing_ref, turned_ref, prior_ref, posterior_ref):
     pieces = [jnp.sum(gram_ref[:, i], axis=0) for i in range(gram_ref.shape[1])]
     gram = unfold(jnp.concatenate(pieces, axis=0))
-    prior_ref[...] = gram
+    back = MEMBERS - local
+    prior_ref[...] = rotate(rotate(gram, back, 0), back, 1)
     dot = functools.partial(jnp.dot, precision=HIGHEST, preferred_element_type=jnp.float32)
-    posterior_ref[...] = dot(dot(turned_ref[...], gram), mixing_ref[...])
+    posterior = dot(dot(turned_ref[...], gram), mixing_ref[...])
+    posterior_ref[...] = rotate(rotate(posterior, back, 0), back, 1)
 
 
 def per_device(mem, ensemble, transform, obs_operator, obs_weight):
@@ -205,10 +215,12 @@
         pack_kernel, shapes, [HBM, HBM], state_bytes, 2 * state_bytes,
         [
             pltpu.VMEM((variables, local, cells), jnp.bfloat16),
+            pltpu.VMEM(transform.shape, transform.dtype),
             pltpu.SemaphoreType.DMA((PACK_STEPS, 2)), pltpu.SemaphoreType.DMA,
         ],
     )(in_hbm(ensemble.transpose(1, 0, 2)), in_hbm(transform))
-    members = exchange(blocks, "mem")
+    last_first = [(i - 1) % mem for i in range(mem)]
+    members = exchange(blocks, "mem", [last_first])
 
     shapes = ((depth, quantities, LANES), (quantities // halves, LANES), (8, LANES))
     factor, pairs, total, mixing, turned = kernel(
@@ -221,7 +233,7 @@
     totals = jnp.sum(members, axis=1, dtype=jnp.float32, keepdims=True)
     mixed = (combined + totals * keep_share[None]).astype(jnp.bfloat16)
     mixed = mixed.reshape(depth, mem, local, LANES).transpose(1, 0, 2, 3)
-    mixed = exchange(mixed, "mem")
+    mixed = exchange(mixed, "mem", [last_first])
 
     gram = kernel(
         gram_kernel, vmem((BLOCK, LANES), jnp.float32), [VMEM] * 4,
@@ -236,7 +248,7 @@
     far_first = [i // 2 + (i + 1) % 2 * (mem // 2) for i in range(mem)]
     gram = exchange(gram, "mem", [far_first])
     prior_gram, posterior_gram = kernel(
-        final_kernel, (square, square), [VMEM] * 3, 4 * MEMBERS**3, 16 * MEMBERS**2
+        functools.partial(final_kernel, local), (square, square), [VMEM] * 3, 4 * MEMBERS**3, 16 * MEMBERS**2
     )(gram, mixing, turned)
 
     analysis = kernel(

time: 160 us -> 158 us (0.988)
  waiting for transfers between devices: 57.2 us -> 52.9 us
  starting transfers between devices: 70.1 us -> 72.3 us
    all_to_all x3, waiting for transfers between devices: 57.2 us -> 52.9 us  [exchange(): lax.all_to_all(array, axis, split_axis=0, concat_axis=0, tiled=True, axis...]
    all_to_all x3, starting transfers between devices: 70.1 us -> 72.3 us  [exchange(): lax.all_to_all(array, axis, split_axis=0, concat_axis=0, tiled=True, axis...]
where the time goes in v11:
time: 158 us
  starting transfers between devices  72.3 us (46%)
  waiting for transfers between devices  52.9 us (33%)
  blocking collectives  20.8 us (13%)
  Pallas kernels  9.33 us (6%)
    all_to_all x3, starting transfers between devices, exchange(): lax.all_to_all(array, axis, split_axis=0, concat_axis=0, tiled=True, axis...  72.3 us
    all_to_all x3, waiting for transfers between devices, exchange(): lax.all_to_all(array, axis, split_axis=0, concat_axis=0, tiled=True, axis...  52.9 us
    psum x2, blocking collectives, per_device(): gram = lax.psum(lax.psum(gram, 'space_1'), 'space_0')  20.8 us
  transfers between devices with their start and end apart: 3, of which 3 were waited for; matrix products, arithmetic and copies ran while one was open for 1% of the time, Pallas kernels for 1%

profile of v11, /device:TPU:80, one launch (start us, length us, event | category | flops | bytes accessed | tf_op | source)
XLA Modules:
  0.0 157.9 jit_solution(894976455106945342)
XLA Ops:
  0.6 3.1 %shard_map.67 = (bf16[16,35,4,128]{3,2,1,0:T(4,128)(2,1)}, f32[64,128]{1,0:T(8,128)S(1)}, bf16[64,64]{1,0:T(8,128)(2,1)S(1)}) custom-call(bf16[70,4,1024]{2,1,0:T(4,128)(2,1)} %bitcast.24, bf16[64,64]{1,0:T(8,128)(2,1)} %transform_ref.1), custom_call_target="tpu_custom_call" | custom-call | flops 573440 | bytes 1146880 | tf_op jit(solution)/shard_map/pallas_call | solution.py:214
  3.7 0.0 copy-start
  3.7 0.0 copy-start.1
  3.7 45.6 %all-to-all-start = ((bf16[16,35,4,128]{3,2,1,0:T(4,128)(2,1)}), bf16[16,35,4,128]{3,2,1,0:T(4,128)(2,1)S(1)}, u32[]{:S(2)}, u32[]{:S(2)}) async-start(bf16[16,35,4,128]{3,2,1,0:T(4,128)(2,1)} %get-tuple-element.13), calls=%async_computation | async-start | bytes 1146880 | tf_op jit(solution)/shard_map/all_to_all | solution.py:27
  49.4 0.0 copy-done
  49.4 0.0 copy-done.1
  49.4 0.3 shard_map.69
  49.6 28.0 %all-to-all-done = bf16[16,35,4,128]{3,2,1,0:T(4,128)(2,1)S(1)} async-done(((bf16[16,35,4,128]{3,2,1,0:T(4,128)(2,1)}), bf16[16,35,4,128]{3,2,1,0:T(4,128)(2,1)S(1)}, u32[]{:S(2)}, u32[]{:S(2)}) %all-to-all-start) | async-done | bytes 573472 | tf_op jit(solution)/shard_map/all_to_all | solution.py:27
  77.6 0.3 copy.8
  77.9 2.4 %shard_map.70 = f32[16,128]{1,0:T(8,128)S(1)} custom-call(bf16[35,64,128]{2,1,0:T(8,128)(2,1)S(1)} %bitcast.20, f32[35,16,128]{2,1,0:T(8,128)S(1)} %get-tuple-element.16.factor_ref, f32[8,128]{1,0:T(8,128)S(1)} %get-tuple-element.17.weight_ref, f32[8,128]{1,0:T(8,128)S(1)} %get-tuple-element.18.total_ref), custom_call_target="tpu_custom_call" | custom-call | flops 18350080 | bytes 573440 | tf_op jit(solution)/shard_map/pallas_call | solution.py:238
  80.3 2.5 %psum.14 = f32[16,128]{1,0:T(8,128)S(1)} all-reduce(f32[16,128]{1,0:T(8,128)S(1)} %shard_map.70), channel_id=1, replica_groups=mesh['parts'=2,'mem'=16,'space_0'=8,'space_1'=2] {'space_1'}, use_global_device_ids=true, to_apply=%region_1.0 | all-reduce | flops 2048 | bytes 16384 | tf_op jit(solution)/shard_map/psum | solution.py:243
  82.8 18.2 %psum.15.gram_ref = f32[16,128]{1,0:T(8,128)S(1)} all-reduce(f32[16,128]{1,0:T(8,128)S(1)} %psum.14), channel_id=1, replica_groups=mesh['parts'=2,'mem'=16,'space_0'=8,'space_1'=2] {'space_0'}, use_global_device_ids=true, to_apply=%region_2.0 | all-reduce | flops 2048 | bytes 16384 | tf_op jit(solution)/shard_map/psum | solution.py:243
  101.1 0.8 shard_map.71
  101.9 14.8 %all-to-all-start.2 = ((f32[16,4,4,128]{3,2,1,0:T(4,128)}), f32[16,4,4,128]{3,2,1,0:T(4,128)S(1)}, u32[]{:S(2)}, u32[]{:S(2)}) async-start(f32[16,4,4,128]{3,2,1,0:T(4,128)} %shard_map.71), calls=%async_computation.2 | async-start | bytes 262144 | tf_op jit(solution)/shard_map/all_to_all | solution.py:27
  116.7 0.3 convert_reduce_fusion
  116.9 0.4 fusion.1
  117.3 1.0 copy.11
  118.3 2.8 %all-to-all-done.2.gram_ref = f32[16,4,4,128]{3,2,1,0:T(4,128)S(1)} async-done(((f32[16,4,4,128]{3,2,1,0:T(4,128)}), f32[16,4,4,128]{3,2,1,0:T(4,128)S(1)}, u32[]{:S(2)}, u32[]{:S(2)}) %all-to-all-start.2) | async-done | bytes 131104 | tf_op jit(solution)/shard_map/all_to_all | solution.py:27
  121.1 11.8 %all-to-all-start.1 = ((bf16[16,35,4,128]{3,2,1,0:T(4,128)(2,1)}), bf16[16,35,4,128]{3,2,1,0:T(4,128)(2,1)S(1)}, u32[]{:S(2)}, u32[]{:S(2)}) async-start(bf16[16,35,4,128]{3,2,1,0:T(4,128)(2,1)} %bitcast.19), calls=%async_computation.1 | async-start | bytes 1146880 | tf_op jit(solution)/shard_map/all_to_all | solution.py:27
  132.9 1.3 shard_map.72
  134.3 22.1 %all-to-all-done.1.x_ref = bf16[16,35,4,128]{3,2,1,0:T(4,128)(2,1)S(1)} async-done(((bf16[16,35,4,128]{3,2,1,0:T(4,128)(2,1)}), bf16[16,35,4,128]{3,2,1,0:T(4,128)(2,1)S(1)}, u32[]{:S(2)}, u32[]{:S(2)}) %all-to-all-start.1) | async-done | bytes 573472 | tf_op jit(solution)/shard_map/all_to_all | solution.py:27
  156.4 1.5 shard_map.68
Async XLA Ops:
  3.7 45.6 %copy-start = (f32[16,1024]{1,0:T(8,128)S(1)}, f32[16,1024]{1,0:T(8,128)}, u32[]{:S(2)}) copy-start(f32[16,1024]{1,0:T(8,128)} %weight_ref.1) | copy-start | bytes 196612
  3.7 45.6 %copy-start.1 = (bf16[16,70]{1,0:T(8,128)(2,1)S(1)}, bf16[16,70]{1,0:T(8,128)(2,1)}, u32[]{:S(2)}) copy-start(bf16[16,70]{1,0:T(8,128)(2,1)} %operator_ref.1) | copy-start | bytes 6724
  3.7 73.9 %all-to-all-start = ((bf16[16,35,4,128]{3,2,1,0:T(4,128)(2,1)}), bf16[16,35,4,128]{3,2,1,0:T(4,128)(2,1)S(1)}, u32[]{:S(2)}, u32[]{:S(2)}) async-start(bf16[16,35,4,128]{3,2,1,0:T(4,128)(2,1)} %get-tuple-element.13), calls=%async_computation | async-start | bytes 1146880 | tf_op jit(solution)/shard_map/all_to_all | solution.py:27
  101.9 19.2 %all-to-all-start.2 = ((f32[16,4,4,128]{3,2,1,0:T(4,128)}), f32[16,4,4,128]{3,2,1,0:T(4,128)S(1)}, u32[]{:S(2)}, u32[]{:S(2)}) async-start(f32[16,4,4,128]{3,2,1,0:T(4,128)} %shard_map.71), calls=%async_computation.2 | async-start | bytes 262144 | tf_op jit(solution)/shard_map/all_to_all | solution.py:27
  121.1 35.3 %all-to-all-start.1 = ((bf16[16,35,4,128]{3,2,1,0:T(4,128)(2,1)}), bf16[16,35,4,128]{3,2,1,0:T(4,128)(2,1)S(1)}, u32[]{:S(2)}, u32[]{:S(2)}) async-start(bf16[16,35,4,128]{3,2,1,0:T(4,128)(2,1)} %bitcast.19), calls=%async_computation.1 | async-start | bytes 1146880 | tf_op jit(solution)/shard_map/all_to_all | solution.py:27

commit v12 on v11

--- a/solution.py
+++ b/solution.py
@@ -13,7 +13,7 @@
 LANES = 128
 GROUP = 4
 BLOCK = 16
-PACK_STEPS = 5
+PACK_STEPS = 2
 VMEM_LIMIT = 12 << 20
 HIGHEST = lax.Precision.HIGHEST
 
@@ -63,10 +63,10 @@
         for i, both in enumerate(zip(steps, shifted, strict=True))
     ]
     mixing_read = pltpu.make_async_copy(transform_ref, read_transform, sem)
+    mixing_read.start()
     for near_read, far_read in reads:
         near_read.start()
         far_read.start()
-    mixing_read.start()
     mixing_read.wait()
     local, mem = o_ref.shape[2], o_ref.shape[0]
     mixing = rotate(rotate(read_transform[...].astype(jnp.float32), local, 0), local, 1)
@@ -245,8 +245,8 @@
         spread_kernel, vmem((mem, BLOCK // 4, 4, LANES), jnp.float32), [VMEM],
         MEMBERS**2, 2 * mem * MEMBERS**2,
     )(gram)
-    far_first = [i // 2 + (i + 1) % 2 * (mem // 2) for i in range(mem)]
-    gram = exchange(gram, "mem", [far_first])
+    order = [i // 2 + (i + 1) % 2 * (mem // 2) for i in range(mem)]
+    gram = exchange(gram, "mem", [order[2:] + order[:2]])
     prior_gram, posterior_gram = kernel(
         functools.partial(final_kernel, local), (square, square), [VMEM] * 3, 4 * MEMBERS**3, 16 * MEMBERS**2
     )(gram, mixing, turned)

time: 158 us -> 159 us (level)
  no operation moved by 1% of the time
where the time goes in v12:
time: 159 us; the launch traced here: 158 us
  starting transfers between devices  71.4 us (45%)
  waiting for transfers between devices  54.3 us (34%)
  blocking collectives  20.8 us (13%)
  Pallas kernels  8.99 us (6%)
    all_to_all x3, starting transfers between devices, exchange(): lax.all_to_all(array, axis, split_axis=0, concat_axis=0, tiled=True, axis...  71.4 us
    all_to_all x3, waiting for transfers between devices, exchange(): lax.all_to_all(array, axis, split_axis=0, concat_axis=0, tiled=True, axis...  54.3 us
    psum x2, blocking collectives, per_device(): gram = lax.psum(lax.psum(gram, 'space_1'), 'space_0')  20.8 us
  transfers between devices with their start and end apart: 3, of which 3 were waited for; matrix products, arithmetic and copies ran while one was open for 1% of the time, Pallas kernels for 1%

profile of v12, /device:TPU:80, one launch (start us, length us, event | category | flops | bytes accessed | tf_op | source)
XLA Modules:
  0.0 158.1 jit_solution(17957571782310243895)
XLA Ops:
  0.6 2.7 %shard_map.67 = (bf16[16,35,4,128]{3,2,1,0:T(4,128)(2,1)}, f32[64,128]{1,0:T(8,128)S(1)}, bf16[64,64]{1,0:T(8,128)(2,1)S(1)}) custom-call(bf16[70,4,1024]{2,1,0:T(4,128)(2,1)} %bitcast.24, bf16[64,64]{1,0:T(8,128)(2,1)} %transform_ref.1), custom_call_target="tpu_custom_call" | custom-call | flops 573440 | bytes 1146880 | tf_op jit(solution)/shard_map/pallas_call | solution.py:214
  3.4 0.0 copy-start
  3.4 0.0 copy-start.1
  3.4 45.6 %all-to-all-start = ((bf16[16,35,4,128]{3,2,1,0:T(4,128)(2,1)}), bf16[16,35,4,128]{3,2,1,0:T(4,128)(2,1)S(1)}, u32[]{:S(2)}, u32[]{:S(2)}) async-start(bf16[16,35,4,128]{3,2,1,0:T(4,128)(2,1)} %get-tuple-element.13), calls=%async_computation | async-start | bytes 1146880 | tf_op jit(solution)/shard_map/all_to_all | solution.py:27
  49.0 0.0 copy-done
  49.0 0.0 copy-done.1
  49.0 0.3 shard_map.69
  49.3 28.0 %all-to-all-done = bf16[16,35,4,128]{3,2,1,0:T(4,128)(2,1)S(1)} async-done(((bf16[16,35,4,128]{3,2,1,0:T(4,128)(2,1)}), bf16[16,35,4,128]{3,2,1,0:T(4,128)(2,1)S(1)}, u32[]{:S(2)}, u32[]{:S(2)}) %all-to-all-start) | async-done | bytes 573472 | tf_op jit(solution)/shard_map/all_to_all | solution.py:27
  77.3 0.3 copy.8
  77.6 2.4 %shard_map.70 = f32[16,128]{1,0:T(8,128)S(1)} custom-call(bf16[35,64,128]{2,1,0:T(8,128)(2,1)S(1)} %bitcast.20, f32[35,16,128]{2,1,0:T(8,128)S(1)} %get-tuple-element.16.factor_ref, f32[8,128]{1,0:T(8,128)S(1)} %get-tuple-element.17.weight_ref, f32[8,128]{1,0:T(8,128)S(1)} %get-tuple-element.18.total_ref), custom_call_target="tpu_custom_call" | custom-call | flops 18350080 | bytes 573440 | tf_op jit(solution)/shard_map/pallas_call | solution.py:238
  80.0 2.5 %psum.14 = f32[16,128]{1,0:T(8,128)S(1)} all-reduce(f32[16,128]{1,0:T(8,128)S(1)} %shard_map.70), channel_id=1, replica_groups=mesh['parts'=2,'mem'=16,'space_0'=8,'space_1'=2] {'space_1'}, use_global_device_ids=true, to_apply=%region_1.0 | all-reduce | flops 2048 | bytes 16384 | tf_op jit(solution)/shard_map/psum | solution.py:243
  82.5 18.2 %psum.15.gram_ref = f32[16,128]{1,0:T(8,128)S(1)} all-reduce(f32[16,128]{1,0:T(8,128)S(1)} %psum.14), channel_id=1, replica_groups=mesh['parts'=2,'mem'=16,'space_0'=8,'space_1'=2] {'space_0'}, use_global_device_ids=true, to_apply=%region_2.0 | all-reduce | flops 2048 | bytes 16384 | tf_op jit(solution)/shard_map/psum | solution.py:243
  100.8 0.8 shard_map.71
  101.5 14.0 %all-to-all-start.2 = ((f32[16,4,4,128]{3,2,1,0:T(4,128)}), f32[16,4,4,128]{3,2,1,0:T(4,128)S(1)}, u32[]{:S(2)}, u32[]{:S(2)}) async-start(f32[16,4,4,128]{3,2,1,0:T(4,128)} %shard_map.71), calls=%async_computation.2 | async-start | bytes 262144 | tf_op jit(solution)/shard_map/all_to_all | solution.py:27
  115.5 0.3 convert_reduce_fusion
  115.8 0.4 fusion.1
  116.1 1.0 copy.11
  117.1 3.7 %all-to-all-done.2.gram_ref = f32[16,4,4,128]{3,2,1,0:T(4,128)S(1)} async-done(((f32[16,4,4,128]{3,2,1,0:T(4,128)}), f32[16,4,4,128]{3,2,1,0:T(4,128)S(1)}, u32[]{:S(2)}, u32[]{:S(2)}) %all-to-all-start.2) | async-done | bytes 131104 | tf_op jit(solution)/shard_map/all_to_all | solution.py:27
  120.9 11.8 %all-to-all-start.1 = ((bf16[16,35,4,128]{3,2,1,0:T(4,128)(2,1)}), bf16[16,35,4,128]{3,2,1,0:T(4,128)(2,1)S(1)}, u32[]{:S(2)}, u32[]{:S(2)}) async-start(bf16[16,35,4,128]{3,2,1,0:T(4,128)(2,1)} %bitcast.19), calls=%async_computation.1 | async-start | bytes 1146880 | tf_op jit(solution)/shard_map/all_to_all | solution.py:27
  132.7 1.3 shard_map.72
  134.0 22.6 %all-to-all-done.1.x_ref = bf16[16,35,4,128]{3,2,1,0:T(4,128)(2,1)S(1)} async-done(((bf16[16,35,4,128]{3,2,1,0:T(4,128)(2,1)}), bf16[16,35,4,128]{3,2,1,0:T(4,128)(2,1)S(1)}, u32[]{:S(2)}, u32[]{:S(2)}) %all-to-all-start.1) | async-done | bytes 573472 | tf_op jit(solution)/shard_map/all_to_all | solution.py:27
  156.6 1.5 shard_map.68
Async XLA Ops:
  3.4 45.6 %copy-start = (f32[16,1024]{1,0:T(8,128)S(1)}, f32[16,1024]{1,0:T(8,128)}, u32[]{:S(2)}) copy-start(f32[16,1024]{1,0:T(8,128)} %weight_ref.1) | copy-start | bytes 196612
  3.4 45.6 %copy-start.1 = (bf16[16,70]{1,0:T(8,128)(2,1)S(1)}, bf16[16,70]{1,0:T(8,128)(2,1)}, u32[]{:S(2)}) copy-start(bf16[16,70]{1,0:T(8,128)(2,1)} %operator_ref.1) | copy-start | bytes 6724
  3.4 73.9 %all-to-all-start = ((bf16[16,35,4,128]{3,2,1,0:T(4,128)(2,1)}), bf16[16,35,4,128]{3,2,1,0:T(4,128)(2,1)S(1)}, u32[]{:S(2)}, u32[]{:S(2)}) async-start(bf16[16,35,4,128]{3,2,1,0:T(4,128)(2,1)} %get-tuple-element.13), calls=%async_computation | async-start | bytes 1146880 | tf_op jit(solution)/shard_map/all_to_all | solution.py:27
  101.5 19.3 %all-to-all-start.2 = ((f32[16,4,4,128]{3,2,1,0:T(4,128)}), f32[16,4,4,128]{3,2,1,0:T(4,128)S(1)}, u32[]{:S(2)}, u32[]{:S(2)}) async-start(f32[16,4,4,128]{3,2,1,0:T(4,128)} %shard_map.71), calls=%async_computation.2 | async-start | bytes 262144 | tf_op jit(solution)/shard_map/all_to_all | solution.py:27
  120.9 35.8 %all-to-all-start.1 = ((bf16[16,35,4,128]{3,2,1,0:T(4,128)(2,1)}), bf16[16,35,4,128]{3,2,1,0:T(4,128)(2,1)S(1)}, u32[]{:S(2)}, u32[]{:S(2)}) async-start(bf16[16,35,4,128]{3,2,1,0:T(4,128)(2,1)} %bitcast.19), calls=%async_computation.1 | async-start | bytes 1146880 | tf_op jit(solution)/shard_map/all_to_all | solution.py:27
